TPU v7x, 32 devices: a whole 2x2x4 slice. The times are simulated.
32 devices in a mesh: horiz: 4 (over y, x), depth: 8 (over z, core).
Axes of the slice: x: 2, y: 2, z: 4, core: 2. Of those that a mesh axis runs over, the one named last changes fastest.
Arguments:
- fields: float32 [3, 256, 128, 256], P(None, 'depth', 'horiz'), may hold values from -6 to 6
- diffusivity: float32 [256, 128, 256], P('depth', 'horiz'), may hold values from 0.05 to 0.24
- offsets: int32 [128], P('horiz'), may hold values from 0 to 3
- coupling: float32 [4, 256], P(None, 'depth'), may hold values from 200 to 1600, as said below
- inverse: float32 [4, 256, 32], P(None, 'depth'), as said below
Outputs:
- advanced: float32 [3, 256, 128, 256], P(None, 'depth', 'horiz')
Inputs may be any that keep to these rules, and one draw needn't show every extreme that they name: coupling[o, k] = coupling[0, k + o] wherever both exist. inverse[o, r * 32 + i, j] is entry (i, j) of the inverse of a block matrix: on the levels k of block r it has diagonal 1 + coupling[o, k] + coupling[o, k + 1] (the first term 0 for k = 0, the second 0 for k = 255) and -coupling[o, k] between levels k - 1 and k; in every block, row and column 31 are those of the identity.
All inputs are finite; a program needn't handle non-finite values.
Results may differ from a plain program's by a relative error of at most 0.0003.
Values sent between devices are 32-bit elements; how exact they have to be, the bound alone decides.
No kernel may reach another device: no remote copies, remote signals or barrier semaphores. Data moves between devices by JAX's collectives and lax.ppermute only.
A program may use at most 64 MiB of HBM per device.

v0:
```python
import jax
import jax.numpy as jnp
from jax import lax
from jax.sharding import PartitionSpec as P

exact_mode = lax.Precision.HIGHEST
wave_gain = 0.5


def padded_2(block, sides, width):
    for axis, dim in sides:
        count = lax.axis_size(axis)
        forward = [(i, i + 1) for i in range(count - 1)]
        forward.append((count - 1, 0))
        backward = [(target, source) for source, target in forward]
        low = lax.ppermute(
            lax.slice_in_dim(block, block.shape[dim] - width, None, axis=dim), axis, forward
        )
        high = lax.ppermute(lax.slice_in_dim(block, 0, width, axis=dim), axis, backward)
        block = jnp.concatenate([low, block, high], axis=dim)
    return block


def passed_along(block, axis, distance):
    devices = range(lax.axis_size(axis))
    route = [(i - distance, i) for i in devices if i - distance in devices]
    return lax.ppermute(block, axis, route)


def tendency(centre, east_side, west_side, diffusivity):
    north_side = jnp.roll(centre, -1, axis=3)
    south_side = jnp.roll(centre, 1, axis=3)
    laplace = east_side + west_side + north_side + south_side - 4.0 * centre
    slope_along = 0.5 * (east_side - west_side)
    slope_across = 0.5 * (north_side - south_side)
    pushed = centre + diffusivity[None] * laplace
    first_part = pushed[0] - wave_gain * slope_along[2]
    second_part = pushed[1] - wave_gain * slope_across[2]
    third_part = pushed[2] - wave_gain * (slope_along[0] + slope_across[1])
    return jnp.stack([first_part, second_part, third_part])


def eliminate(level_slab, inverse_rows, coupling_rows, selector, block_index):
    chosen = jnp.einsum("jo,oab->jab", selector, inverse_rows, precision=exact_mode)
    line_coupling = jnp.dot(selector, coupling_rows, precision=exact_mode)
    solved = jnp.einsum("jab,fbjy->fajy", chosen, level_slab, precision=exact_mode)
    below_face = line_coupling[:, 0]
    upper_gate = line_coupling[:, -1]
    lower_gate = jnp.where(block_index > 0, below_face, jnp.zeros_like(below_face))
    spike_low = chosen[:, :, 0] * lower_gate[:, None]
    spike_high = chosen[:, :, -2] * upper_gate[:, None]
    return (solved, spike_low, spike_high, below_face, upper_gate)


def interface_rows(solved, spike_low, spike_high, upper_gate, got_rows, got_lines):
    lower_band = -upper_gate * spike_low[:, -2]
    main_band = 1.0 + upper_gate + got_lines[0] - upper_gate * spike_high[:, -2] - got_lines[1]
    upper_band = -got_lines[2]
    target = solved[:, -1] + upper_gate[None, :, None] * solved[:, -2] + got_rows
    return (lower_band, main_band, upper_band, target)


def thomas(lower_band, main_band, upper_band, target):

    def forward_step(state_now, row_data):
        prev_ratio, prev_value = state_now
        low_row, main_row, up_row, target_row = row_data
        pivot_value = main_row - low_row * prev_ratio
        ratio_now = up_row / pivot_value
        value_now = (target_row - low_row[None, :, None] * prev_value) / pivot_value[None, :, None]
        return ((ratio_now, value_now), (ratio_now, value_now))

    anchor = jnp.zeros_like(target[0])
    start_ratio = jnp.zeros_like(main_band[0])
    _, (ratios, values) = lax.scan(
        forward_step, (start_ratio, anchor), (lower_band, main_band, upper_band, target)
    )

    def backward_step(next_value, row_data):
        ratio_now, value_now = row_data
        result_now = value_now - ratio_now[None, :, None] * next_value
        return (result_now, result_now)

    _, results = lax.scan(backward_step, anchor, (ratios, values), reverse=True)
    return results


def assemble(solved, spike_low, spike_high, previous, self_value):
    lifted = (
        solved
        + spike_low.T[None, :, :, None] * previous[:, None]
        + spike_high.T[None, :, :, None] * self_value[:, None]
    )
    return jnp.concatenate([lifted[:, :-1], self_value[:, None]], axis=1)


def body(fields, diffusivity, offsets, coupling, inverse):
    padded = padded_2(fields, (("horiz", 2),), 1)
    forcing = tendency(padded[:, :, 1:-1], padded[:, :, 2:], padded[:, :, :-2], diffusivity)
    selector = (offsets[:, None] == jnp.arange(inverse.shape[0], dtype=jnp.int32)[None, :]).astype(
        jnp.float32
    )
    depth_rank = lax.axis_index("depth")
    solved, spike_low, spike_high, below_face, upper_gate = eliminate(
        forcing, inverse, coupling, selector, depth_rank
    )
    send_lines = jnp.stack(
        [below_face, below_face * spike_low[:, 0], below_face * spike_high[:, 0]]
    )
    send_rows = below_face[None, :, None] * solved[:, 0]
    got_rows, got_lines = passed_along((send_rows, send_lines), "depth", -1)
    lower_band, main_band, upper_band, target = interface_rows(
        solved, spike_low, spike_high, upper_gate, got_rows, got_lines
    )
    every_lower, every_main, every_upper, every_target = (
        lax.all_gather(lower_band[None], "depth", axis=0, tiled=True),
        lax.all_gather(main_band[None], "depth", axis=0, tiled=True),
        lax.all_gather(upper_band[None], "depth", axis=0, tiled=True),
        lax.all_gather(target[None], "depth", axis=0, tiled=True),
    )
    interfaces = thomas(every_lower, every_main, every_upper, every_target)
    self_value = lax.dynamic_index_in_dim(interfaces, depth_rank, 0, keepdims=False)
    previous = lax.dynamic_index_in_dim(
        interfaces, jnp.maximum(depth_rank - 1, 0), 0, keepdims=False
    )
    previous = jnp.where(depth_rank > 0, previous, jnp.zeros_like(previous))
    return assemble(solved, spike_low, spike_high, previous, self_value)


def solution(mesh):
    return jax.shard_map(
        body,
        mesh=mesh,
        in_specs=(
            P(None, "depth", "horiz", None),
            P("depth", "horiz", None),
            P("horiz"),
            P(None, "depth"),
            P(None, "depth", None),
        ),
        out_specs=P(None, "depth", "horiz", None),
        check_vma=False,
    )
```

profile of v0, /device:TPU:0, one launch (start us, length us, event | category | flops | bytes accessed | tf_op | source)
XLA Modules:
  0.0 154.1 jit_solution(5793986876285499726)
XLA Ops:
  0.0 3.7 %copy.110 = f32[3,32,32,256]{3,1,0,2:T(8,128)S(1)} copy(f32[3,32,32,256]{3,2,1,0:T(8,128)} %param.9) | data formatting | bytes 6291456 | tf_op args[0]
  4.5 3.9 %collective-permute-start = (f32[3,32,1,256]{3,1,0,2:T(8,128)}, f32[3,32,1,256]{3,1,0,2:T(8,128)S(1)}, u32[]{:S(2)}, u32[]{:S(2)}) collective-permute-start(f32[3,32,1,256]{3,1,0,2:T(8,128)} %get-tuple-element.260), channel_id=1, source_target_pairs={{8,0},{16,8},{24,16},{0,24},{9,1},{17,9},{25,17},{1,25},{10,2},{18... | collective-permute-start | bytes 294920 | tf_op jit(solution)/shard_map/ppermute | solution.py:19
  11.0 1.3 collective-permute-start.2
  12.3 3.9 %fusion.45 = (f32[3,32,32,255]{3,1,0,2:T(8,128)}, f32[3,32,32,255]{3,1,0,2:T(8,128)}) fusion(f32[3,32,32,256]{3,1,0,2:T(8,128)S(1)} %copy.110), kind=kLoop, calls=%fused_computation.82 | loop fusion | bytes 12533760 | tf_op jit(solution)/shard_map/jit(_roll_static)/slice | solution.py:31
  16.3 2.2 %fusion.46 = (f32[3,32,32,1]{3,1,0,2:T(8,128)}, f32[3,32,32,1]{3,1,0,2:T(8,128)}) fusion(f32[3,32,32,256]{3,1,0,2:T(8,128)S(1)} %copy.110), kind=kLoop, calls=%fused_computation.83 | loop fusion | bytes 49152 | tf_op jit(solution)/shard_map/jit(_roll_static)/slice | solution.py:31
  20.4 1.2 fusion.33
  21.6 2.8 %copy.100 = f32[32,32,256]{2,0,1:T(8,128)} copy(f32[32,32,256]{2,1,0:T(8,128)} %param.10) | data formatting | bytes 2097152 | tf_op args[1]
  24.4 2.3 %copy.123 = f32[32,32,32,1]{2,1,3,0:T(8,128)} copy(f32[32,32,32,1]{0,2,1,3:T(8,128)} %bitcast.121) | data formatting | bytes 262144 | tf_op jit(solution)/shard_map/jo,oab->jab/dot_general | solution.py:44
  26.7 18.5 %all-reduce = f32[256]{0:T(256)S(1)} all-reduce(f32[256]{0:T(256)} %fusion.33), channel_id=2, replica_groups=mesh['horiz'=4,'depth'=8] {'depth'}, use_global_device_ids=true, to_apply=%add | all-reduce | flops 256 | bytes 2048
  46.1 5.4 %multiply_add_fusion = (f32[3,32,32,256]{3,1,0,2:T(8,128)S(1)}, f32[3,32,32,256]{3,1,0,2:T(8,128)S(1)}, f32[3,32,32,256]{3,1,0,2:T(8,128)S(1)}) fusion(f32[3,32,32,256]{3,1,0,2:T(8,128)S(1)} %copy.110, f32[3,32,1,256]{3,1,0,2:T(8,128)S(1)} %collective-permute-done, f32[3,32,1,256]{3,1,0,2:T(8,128)} %collective-permute-done.1, ...), kind=kLoop, calls=%fused_computation.34 | loop fusion | flops 11796480 | bytes 20119552 | tf_op jit(solution)/shard_map/add | solution.py:36
  51.5 0.8 fusion.21
  52.5 2.9 %fusion.15 = f32[3,32,32,256]{3,1,0,2:T(8,128)S(1)} fusion(f32[32,32,32,1]{2,1,3,0:T(8,128)S(1)} %copy-done.2, f32[1,32,32,256]{3,1,0,2:T(8,128)S(1)} %get-tuple-element.253, f32[1,32,32,256]{3,1,0,2:T(8,128)S(1)} %get-tuple-element.254, f32[1,32,32,256]{3,1,0,2:T(8,128)S(1)} %get-tuple-element.252), kind=kOutput, calls=%fused_computation.35 | convolution fusion | flops 303562752 | bytes 6422528 | tf_op jit(solution)/shard_map/jab,fbjy->fajy/dot_general | solution.py:46
  55.7 1.3 collective-permute-start.3
  57.0 0.7 fusion.39
  57.7 9.5 %all-gather.2 = f32[8,1,32]{2,1,0:T(1,128)S(1)} all-gather(f32[1,1,32]{2,1,0:T(1,128)S(1)} %get-tuple-element.277), channel_id=1, replica_groups=mesh['horiz'=4,'depth'=8] {'depth'}, dimensions={0}, use_global_device_ids=true | all-gather | bytes 1152 | tf_op jit(solution)/shard_map/all_gather | solution.py:118
  67.2 9.3 %all-gather.3 = f32[8,1,32]{2,1,0:T(1,128)S(1)} all-gather(f32[1,1,32]{2,1,0:T(1,128)S(1)} %get-tuple-element.276), channel_id=1, replica_groups=mesh['horiz'=4,'depth'=8] {'depth'}, dimensions={0}, use_global_device_ids=true | all-gather | bytes 1152 | tf_op jit(solution)/shard_map/all_gather | solution.py:117
  76.6 17.2 %all-gather.1 = f32[24,32,256]{2,1,0:T(8,128)} all-gather(f32[3,32,256]{2,1,0:T(8,128)S(1)} %fusion.23), channel_id=3, replica_groups=mesh['horiz'=4,'depth'=8] {'depth'}, dimensions={0}, use_global_device_ids=true | all-gather | bytes 884736 | tf_op jit(solution)/shard_map/all_gather | solution.py:119
  93.8 1.0 broadcast.54.clone
  94.8 34.1 %while.34 = (s32[]{:T(128)}, f32[32]{0:T(128)S(1)}, f32[3,32,256]{2,1,0:T(8,128)S(1)}, f32[8,32]{1,0:T(8,128)}, f32[8,3,32,256]{3,2,1,0:T(8,128)}, /*index=5*/f3...) while((s32[]{:T(128)}, f32[32]{0:T(128)S(1)}, ...), condition=%wide.region_1.2_spmd.clone, body=%wide.region_0.1_spmd.clone.sunk | while | flops 98435 | bytes 395396 | solution.py:75
  96.2 1.6 %bitcast_dynamic-update-slice_fusion.4 = (f32[8,3,32,256]{3,2,1,0:T(8,128)}, f32[3,32,256]{2,1,0:T(8,128)S(1)}) fusion(f32[8,3,32,256]{3,2,1,0:T(8,128)} %get-tuple-element.391, s32[]{:T(128)} %get-tuple-element.387, f32[32]{0:T(128)S(1)} %get-tuple-element.366, f32[3,32,256]{2,1,0:T(8,128)S(1)} %get-tuple-element.389, pred[]{:T(512)S(6)} %compare.6, ...), kind=kLoop, calls=%fused_computation.clone.1 | loop fusion | flops 98304 | bytes 393985 | tf_op jit(solution)/shard_map/while/body/jit(dynamic_update_index_in_dim)/dynamic_update_slice | solution.py:75
  97.8 1.3 dynamic_update_slice.26
  100.5 1.6 %bitcast_dynamic-update-slice_fusion.4 = (f32[8,3,32,256]{3,2,1,0:T(8,128)}, f32[3,32,256]{2,1,0:T(8,128)S(1)}) fusion(f32[8,3,32,256]{3,2,1,0:T(8,128)} %get-tuple-element.391, s32[]{:T(128)} %get-tuple-element.387, f32[32]{0:T(128)S(1)} %get-tuple-element.366, f32[3,32,256]{2,1,0:T(8,128)S(1)} %get-tuple-element.389, pred[]{:T(512)S(6)} %compare.6, ...), kind=kLoop, calls=%fused_computation.clone.1 | loop fusion | flops 98304 | bytes 393985 | tf_op jit(solution)/shard_map/while/body/jit(dynamic_update_index_in_dim)/dynamic_update_slice | solution.py:75
  102.1 1.3 dynamic_update_slice.26
  104.7 1.6 %bitcast_dynamic-update-slice_fusion.4 = (f32[8,3,32,256]{3,2,1,0:T(8,128)}, f32[3,32,256]{2,1,0:T(8,128)S(1)}) fusion(f32[8,3,32,256]{3,2,1,0:T(8,128)} %get-tuple-element.391, s32[]{:T(128)} %get-tuple-element.387, f32[32]{0:T(128)S(1)} %get-tuple-element.366, f32[3,32,256]{2,1,0:T(8,128)S(1)} %get-tuple-element.389, pred[]{:T(512)S(6)} %compare.6, ...), kind=kLoop, calls=%fused_computation.clone.1 | loop fusion | flops 98304 | bytes 393985 | tf_op jit(solution)/shard_map/while/body/jit(dynamic_update_index_in_dim)/dynamic_update_slice | solution.py:75
  106.4 1.3 dynamic_update_slice.26
  109.0 1.6 %bitcast_dynamic-update-slice_fusion.4 = (f32[8,3,32,256]{3,2,1,0:T(8,128)}, f32[3,32,256]{2,1,0:T(8,128)S(1)}) fusion(f32[8,3,32,256]{3,2,1,0:T(8,128)} %get-tuple-element.391, s32[]{:T(128)} %get-tuple-element.387, f32[32]{0:T(128)S(1)} %get-tuple-element.366, f32[3,32,256]{2,1,0:T(8,128)S(1)} %get-tuple-element.389, pred[]{:T(512)S(6)} %compare.6, ...), kind=kLoop, calls=%fused_computation.clone.1 | loop fusion | flops 98304 | bytes 393985 | tf_op jit(solution)/shard_map/while/body/jit(dynamic_update_index_in_dim)/dynamic_update_slice | solution.py:75
  110.6 1.3 dynamic_update_slice.26
  113.2 1.6 %bitcast_dynamic-update-slice_fusion.4 = (f32[8,3,32,256]{3,2,1,0:T(8,128)}, f32[3,32,256]{2,1,0:T(8,128)S(1)}) fusion(f32[8,3,32,256]{3,2,1,0:T(8,128)} %get-tuple-element.391, s32[]{:T(128)} %get-tuple-element.387, f32[32]{0:T(128)S(1)} %get-tuple-element.366, f32[3,32,256]{2,1,0:T(8,128)S(1)} %get-tuple-element.389, pred[]{:T(512)S(6)} %compare.6, ...), kind=kLoop, calls=%fused_computation.clone.1 | loop fusion | flops 98304 | bytes 393985 | tf_op jit(solution)/shard_map/while/body/jit(dynamic_update_index_in_dim)/dynamic_update_slice | solution.py:75
  114.9 1.3 dynamic_update_slice.26
  117.5 1.6 %bitcast_dynamic-update-slice_fusion.4 = (f32[8,3,32,256]{3,2,1,0:T(8,128)}, f32[3,32,256]{2,1,0:T(8,128)S(1)}) fusion(f32[8,3,32,256]{3,2,1,0:T(8,128)} %get-tuple-element.391, s32[]{:T(128)} %get-tuple-element.387, f32[32]{0:T(128)S(1)} %get-tuple-element.366, f32[3,32,256]{2,1,0:T(8,128)S(1)} %get-tuple-element.389, pred[]{:T(512)S(6)} %compare.6, ...), kind=kLoop, calls=%fused_computation.clone.1 | loop fusion | flops 98304 | bytes 393985 | tf_op jit(solution)/shard_map/while/body/jit(dynamic_update_index_in_dim)/dynamic_update_slice | solution.py:75
  119.1 1.3 dynamic_update_slice.26
  121.8 1.6 %bitcast_dynamic-update-slice_fusion.4 = (f32[8,3,32,256]{3,2,1,0:T(8,128)}, f32[3,32,256]{2,1,0:T(8,128)S(1)}) fusion(f32[8,3,32,256]{3,2,1,0:T(8,128)} %get-tuple-element.391, s32[]{:T(128)} %get-tuple-element.387, f32[32]{0:T(128)S(1)} %get-tuple-element.366, f32[3,32,256]{2,1,0:T(8,128)S(1)} %get-tuple-element.389, pred[]{:T(512)S(6)} %compare.6, ...), kind=kLoop, calls=%fused_computation.clone.1 | loop fusion | flops 98304 | bytes 393985 | tf_op jit(solution)/shard_map/while/body/jit(dynamic_update_index_in_dim)/dynamic_update_slice | solution.py:75
  123.4 1.3 dynamic_update_slice.26
  126.0 1.6 %bitcast_dynamic-update-slice_fusion.4 = (f32[8,3,32,256]{3,2,1,0:T(8,128)}, f32[3,32,256]{2,1,0:T(8,128)S(1)}) fusion(f32[8,3,32,256]{3,2,1,0:T(8,128)} %get-tuple-element.391, s32[]{:T(128)} %get-tuple-element.387, f32[32]{0:T(128)S(1)} %get-tuple-element.366, f32[3,32,256]{2,1,0:T(8,128)S(1)} %get-tuple-element.389, pred[]{:T(512)S(6)} %compare.6, ...), kind=kLoop, calls=%fused_computation.clone.1 | loop fusion | flops 98304 | bytes 393985 | tf_op jit(solution)/shard_map/while/body/jit(dynamic_update_index_in_dim)/dynamic_update_slice | solution.py:75
  127.6 1.3 dynamic_update_slice.26
  128.9 1.0 broadcast.54
  129.9 18.4 %while.35 = (s32[]{:T(128)}, f32[3,32,256]{2,1,0:T(8,128)S(1)}, f32[8,3,32,256]{3,2,1,0:T(8,128)}, f32[8,3,32,256]{3,2,1,0:T(8,128)}, f32[8,32]{1,0:T(8,128)}, /*index=5*/s32[]{:T(128)}, s32[]{:T(128)}, s32[]{:T(128)}) while((s32[]{:T(128)}, f32[3,32,256]{2,1,0:T(8,128)S(1)}, f32[8,3,32,256]{3,2,1,0:T(8,128)}, ...), condition=%wide.region_3.4_spmd.clone, body=%wide.region_2.3_spmd.clone.sunk | while | flops 73732 | bytes 393715 | solution.py:84
  130.6 1.6 %bitcast_dynamic-update-slice_fusion.5 = (f32[8,3,32,256]{3,2,1,0:T(8,128)}, f32[3,32,256]{2,1,0:T(8,128)S(1)}) fusion(f32[8,3,32,256]{3,2,1,0:T(8,128)} %get-tuple-element.419, s32[]{:T(128)S(6)} %sub.90, f32[3,32,256]{2,1,0:T(8,128)S(1)} %get-tuple-element.418, pred[]{:T(512)S(6)} %compare.7, f32[32]{0:T(128)S(1)} %fusion.57, ...), kind=kLoop, calls=%fused_computation.14.clone.1 | loop fusion | flops 73728 | bytes 393349 | tf_op jit(solution)/shard_map/while/body/jit(dynamic_update_index_in_dim)/dynamic_update_slice | solution.py:75
  132.8 1.6 %bitcast_dynamic-update-slice_fusion.5 = (f32[8,3,32,256]{3,2,1,0:T(8,128)}, f32[3,32,256]{2,1,0:T(8,128)S(1)}) fusion(f32[8,3,32,256]{3,2,1,0:T(8,128)} %get-tuple-element.419, s32[]{:T(128)S(6)} %sub.90, f32[3,32,256]{2,1,0:T(8,128)S(1)} %get-tuple-element.418, pred[]{:T(512)S(6)} %compare.7, f32[32]{0:T(128)S(1)} %fusion.57, ...), kind=kLoop, calls=%fused_computation.14.clone.1 | loop fusion | flops 73728 | bytes 393349 | tf_op jit(solution)/shard_map/while/body/jit(dynamic_update_index_in_dim)/dynamic_update_slice | solution.py:75
  135.1 1.6 %bitcast_dynamic-update-slice_fusion.5 = (f32[8,3,32,256]{3,2,1,0:T(8,128)}, f32[3,32,256]{2,1,0:T(8,128)S(1)}) fusion(f32[8,3,32,256]{3,2,1,0:T(8,128)} %get-tuple-element.419, s32[]{:T(128)S(6)} %sub.90, f32[3,32,256]{2,1,0:T(8,128)S(1)} %get-tuple-element.418, pred[]{:T(512)S(6)} %compare.7, f32[32]{0:T(128)S(1)} %fusion.57, ...), kind=kLoop, calls=%fused_computation.14.clone.1 | loop fusion | flops 73728 | bytes 393349 | tf_op jit(solution)/shard_map/while/body/jit(dynamic_update_index_in_dim)/dynamic_update_slice | solution.py:75
  137.4 1.6 %bitcast_dynamic-update-slice_fusion.5 = (f32[8,3,32,256]{3,2,1,0:T(8,128)}, f32[3,32,256]{2,1,0:T(8,128)S(1)}) fusion(f32[8,3,32,256]{3,2,1,0:T(8,128)} %get-tuple-element.419, s32[]{:T(128)S(6)} %sub.90, f32[3,32,256]{2,1,0:T(8,128)S(1)} %get-tuple-element.418, pred[]{:T(512)S(6)} %compare.7, f32[32]{0:T(128)S(1)} %fusion.57, ...), kind=kLoop, calls=%fused_computation.14.clone.1 | loop fusion | flops 73728 | bytes 393349 | tf_op jit(solution)/shard_map/while/body/jit(dynamic_update_index_in_dim)/dynamic_update_slice | solution.py:75
  139.7 1.6 %bitcast_dynamic-update-slice_fusion.5 = (f32[8,3,32,256]{3,2,1,0:T(8,128)}, f32[3,32,256]{2,1,0:T(8,128)S(1)}) fusion(f32[8,3,32,256]{3,2,1,0:T(8,128)} %get-tuple-element.419, s32[]{:T(128)S(6)} %sub.90, f32[3,32,256]{2,1,0:T(8,128)S(1)} %get-tuple-element.418, pred[]{:T(512)S(6)} %compare.7, f32[32]{0:T(128)S(1)} %fusion.57, ...), kind=kLoop, calls=%fused_computation.14.clone.1 | loop fusion | flops 73728 | bytes 393349 | tf_op jit(solution)/shard_map/while/body/jit(dynamic_update_index_in_dim)/dynamic_update_slice | solution.py:75
  142.0 1.6 %bitcast_dynamic-update-slice_fusion.5 = (f32[8,3,32,256]{3,2,1,0:T(8,128)}, f32[3,32,256]{2,1,0:T(8,128)S(1)}) fusion(f32[8,3,32,256]{3,2,1,0:T(8,128)} %get-tuple-element.419, s32[]{:T(128)S(6)} %sub.90, f32[3,32,256]{2,1,0:T(8,128)S(1)} %get-tuple-element.418, pred[]{:T(512)S(6)} %compare.7, f32[32]{0:T(128)S(1)} %fusion.57, ...), kind=kLoop, calls=%fused_computation.14.clone.1 | loop fusion | flops 73728 | bytes 393349 | tf_op jit(solution)/shard_map/while/body/jit(dynamic_update_index_in_dim)/dynamic_update_slice | solution.py:75
  144.3 1.6 %bitcast_dynamic-update-slice_fusion.5 = (f32[8,3,32,256]{3,2,1,0:T(8,128)}, f32[3,32,256]{2,1,0:T(8,128)S(1)}) fusion(f32[8,3,32,256]{3,2,1,0:T(8,128)} %get-tuple-element.419, s32[]{:T(128)S(6)} %sub.90, f32[3,32,256]{2,1,0:T(8,128)S(1)} %get-tuple-element.418, pred[]{:T(512)S(6)} %compare.7, f32[32]{0:T(128)S(1)} %fusion.57, ...), kind=kLoop, calls=%fused_computation.14.clone.1 | loop fusion | flops 73728 | bytes 393349 | tf_op jit(solution)/shard_map/while/body/jit(dynamic_update_index_in_dim)/dynamic_update_slice | solution.py:75
  146.6 1.6 %bitcast_dynamic-update-slice_fusion.5 = (f32[8,3,32,256]{3,2,1,0:T(8,128)}, f32[3,32,256]{2,1,0:T(8,128)S(1)}) fusion(f32[8,3,32,256]{3,2,1,0:T(8,128)} %get-tuple-element.419, s32[]{:T(128)S(6)} %sub.90, f32[3,32,256]{2,1,0:T(8,128)S(1)} %get-tuple-element.418, pred[]{:T(512)S(6)} %compare.7, f32[32]{0:T(128)S(1)} %fusion.57, ...), kind=kLoop, calls=%fused_computation.14.clone.1 | loop fusion | flops 73728 | bytes 393349 | tf_op jit(solution)/shard_map/while/body/jit(dynamic_update_index_in_dim)/dynamic_update_slice | solution.py:75
  148.3 1.0 select_bitcast_fusion
  149.5 0.7 fusion.8
  150.7 3.5 %copy.122 = f32[3,32,32,256]{3,2,1,0:T(8,128)} copy(f32[3,32,32,256]{3,1,0,2:T(8,128)S(1)} %pad_maximum_fusion.4) | data formatting | bytes 6291456 | tf_op jit(solution)/shard_map/concatenate | solution.py:94
  (80 shorter events, 22.9 us)
Async XLA Ops:
  0.0 8.4 %copy-start = (f32[4,32,32]{2,1,0:T(8,128)S(1)}, f32[4,32,32]{2,1,0:T(8,128)}, u32[]{:S(2)}) copy-start(f32[4,32,32]{2,1,0:T(8,128)} %param.13) | copy-start | bytes 49156
  0.0 8.4 %copy-start.8 = (s32[32]{0:T(128)S(1)}, s32[32]{0:T(128)}, u32[]{:S(2)}) copy-start(s32[32]{0:T(128)} %param.11) | copy-start | bytes 388
  0.0 9.0 %copy-start.10 = (f32[4,32]{1,0:T(4,128)S(1)}, f32[4,32]{1,0:T(4,128)}, u32[]{:S(2)}) copy-start(f32[4,32]{1,0:T(4,128)} %param.12) | copy-start | bytes 1540
  4.5 41.6 %collective-permute-start = (f32[3,32,1,256]{3,1,0,2:T(8,128)}, f32[3,32,1,256]{3,1,0,2:T(8,128)S(1)}, u32[]{:S(2)}, u32[]{:S(2)}) collective-permute-start(f32[3,32,1,256]{3,1,0,2:T(8,128)} %get-tuple-element.260), channel_id=1, source_target_pairs={{8,0},{16,8},{24,16},{0,24},{9,1},{17,9},{25,17},{1,25},{10,2},{18... | collective-permute-start | bytes 294920 | tf_op jit(solution)/shard_map/ppermute | solution.py:19
  8.4 37.7 %collective-permute-start.1 = (f32[3,32,1,256]{3,1,0,2:T(8,128)}, f32[3,32,1,256]{3,1,0,2:T(8,128)}, u32[]{:S(2)}, u32[]{:S(2)}) collective-permute-start(f32[3,32,1,256]{3,1,0,2:T(8,128)} %get-tuple-element.259), channel_id=1, source_target_pairs={{0,8},{8,16},{16,24},{24,0},{1,9},{9,17},{17,25},{25,1},{2,10},{10... | collective-permute-start | bytes 294920 | tf_op jit(solution)/shard_map/ppermute | solution.py:16
  9.0 0.8 copy-start.1
  9.8 10.6 %copy-start.9 = (f32[32,32]{0,1:T(8,128)}, f32[32,32]{0,1:T(8,128)S(1)}, u32[]{:S(2)}) copy-start(f32[32,32]{0,1:T(8,128)S(1)} %fusion.26) | copy-start | bytes 12292
  10.5 8.0 %copy-start.5 = (f32[32]{0:T(128)}, f32[32]{0:T(128)S(1)}, u32[]{:S(2)}) copy-start(f32[32]{0:T(128)S(1)} %get-tuple-element.272) | copy-start | bytes 388
  10.5 5.8 %copy-start.4 = (f32[32,32]{0,1:T(8,128)}, f32[32,32]{0,1:T(8,128)S(1)}, u32[]{:S(2)}) copy-start(f32[32,32]{0,1:T(8,128)S(1)} %broadcast_multiply_fusion) | copy-start | bytes 12292
  11.0 45.9 %collective-permute-start.2 = (f32[3,32]{1,0:T(4,128)}, f32[3,32]{1,0:T(4,128)}, u32[]{:S(2)}, u32[]{:S(2)}) collective-permute-start(f32[3,32]{1,0:T(4,128)} %pad_maximum_fusion.5), channel_id=1, source_target_pairs={{1,0},{2,1},{3,2},{4,3},{5,4},{6,5},{7,6},{9,8},{10,9},{11,10},{12... | collective-permute-start | bytes 1160 | tf_op jit(solution)/shard_map/ppermute | solution.py:27
  16.3 2.2 %copy-start.11 = (u32[32]{0:T(128)S(1)}, u32[32]{0:T(128)}, u32[]{:S(2)}) copy-start(u32[32]{0:T(128)} %constant.82) | copy-start | bytes 388
  51.5 1.0 copy-start.2
  52.5 3.1 %copy-start.7 = (f32[32]{0:T(128)S(1)}, f32[32]{0:T(128)}, u32[]{:S(2)}) copy-start(f32[32]{0:T(128)} %get-tuple-element.270) | copy-start | bytes 388
  52.5 24.0 %copy-start.6 = (f32[32]{0:T(128)S(1)}, f32[32]{0:T(128)}, u32[]{:S(2)}) copy-start(f32[32]{0:T(128)} %copy-done.5) | copy-start | bytes 388
  52.5 42.3 %copy-start.3 = (f32[32]{0:T(128)S(1)}, f32[32]{0:T(128)}, u32[]{:S(2)}) copy-start(f32[32]{0:T(128)} %custom-call) | copy-start | bytes 388
  55.7 20.8 %collective-permute-start.3 = (f32[3,32,256]{2,1,0:T(8,128)S(1)}, f32[3,32,256]{2,1,0:T(8,128)S(1)}, u32[]{:S(2)}, u32[]{:S(2)}) collective-permute-start(f32[3,32,256]{2,1,0:T(8,128)S(1)} %bitcast_multiply_fusion), channel_id=1, source_target_pairs={{1,0},{2,1},{3,2},{4,3},{5,4},{6,5},{7,6},{9,8},{10,9},{11,10},{12... | collective-permute-start | bytes 294920 | tf_op jit(solution)/shard_map/ppermute | solution.py:27
where the time goes:
time: 156 us; the launch traced here: 154 us
  blocking collectives  54.6 us (35%)
  local copies, waits for them, and re-layouts  45.6 us (29%)
  other arithmetic  42.9 us (28%)
  starting transfers between devices  6.49 us (4%)
  matrix products  3.67 us (2%)
    dynamic_update_slice x16, other arithmetic, thomas(): lax.scan(forward_step, (start_ratio, anchor), (lower_band, main_band, upp...  25.9 us
    unnamed x1, blocking collectives  18.5 us
    all_gather x1, blocking collectives, body(): lax.all_gather(target[None], 'depth', axis=0, tiled=True)  17.2 us
    dynamic_update_slice x8, local copies, waits for them, and re-layouts, thomas(): lax.scan(forward_step, (start_ratio, anchor), (lower_band, main_band, upp...  10.2 us
    all_gather x1, blocking collectives, body(): lax.all_gather(upper_band[None], 'depth', axis=0, tiled=True)  9.5 us
    all_gather x1, blocking collectives, body(): lax.all_gather(main_band[None], 'depth', axis=0, tiled=True)  9.27 us
    unnamed x30, local copies, waits for them, and re-layouts  8.71 us
    slice x2, local copies, waits for them, and re-layouts, tendency(): north_side = jnp.roll(centre, -1, axis=3)  6.17 us
  transfers between devices with their start and end apart: 4, of which 0 were waited for; matrix products, arithmetic and copies ran while one was open for 17% of the time, Pallas kernels for 0%

commit v1 on v0

v1 whole, which is shorter than its diff:
```python
import functools

import jax
import jax.numpy as jnp
from jax import lax
from jax.experimental import pallas as pl
from jax.experimental.pallas import tpu as pltpu
from jax.sharding import PartitionSpec as P

wave_gain = 0.5
SUB = 8
LANE = 128
VMEM = pltpu.VMEM
F32 = jnp.float32
BF16 = jnp.bfloat16


def vmem_spec():
    return pl.BlockSpec(memory_space=VMEM)


def choose(offs, rows):
    value = jnp.broadcast_to(rows[0], offs.shape)
    for o in range(1, len(rows)):
        value = jnp.where(offs == o, jnp.broadcast_to(rows[o], offs.shape), value)
    return value


def split_bf16(x):
    high = x.astype(BF16)
    low = (x - high.astype(F32)).astype(BF16)
    return high, low


def table_kernel(offs_ref, coupling_ref, inverse_ref, big_ref, offsb_ref, spikes_ref, coefs_ref, wide_ref):
    count, levels, _ = inverse_ref.shape
    lines = offsb_ref.shape[0]
    groups = lines // SUB
    rank = lax.axis_index("depth")

    for g in range(groups):
        sub = lax.broadcasted_iota(jnp.int32, (SUB, LANE), 0)
        value = jnp.zeros((SUB, LANE), jnp.int32)
        for j in range(SUB):
            value = jnp.where(sub == j, offs_ref[g * SUB + j], value)
        offsb_ref[g * SUB : (g + 1) * SUB, :] = value

    for o in range(count):
        gate = jnp.broadcast_to(coupling_ref[o : o + 1, levels - 1 : levels], (1, LANE))
        face = jnp.broadcast_to(coupling_ref[o : o + 1, 0:1], (1, LANE))
        face = jnp.where(rank > 0, face, jnp.zeros_like(face))
        low = jnp.broadcast_to(inverse_ref[o, :, 0:1], (levels, LANE)) * face
        high = jnp.broadcast_to(inverse_ref[o, :, levels - 2 : levels - 1], (levels, LANE)) * gate
        spikes_ref[0, o] = low
        spikes_ref[1, o] = high
        b = face - face * low[0:1]
        e = -face * high[0:1]
        l = -gate * low[levels - 2 : levels - 1]
        a = 1.0 + gate - gate * high[levels - 2 : levels - 1]
        for c, row in enumerate((b, e, l, a, gate, face)):
            coefs_ref[c * count + o : c * count + o + 1, :] = row

    width = levels * SUB
    spread = (
        lax.broadcasted_iota(jnp.int32, (levels, width), 1) // SUB
        == lax.broadcasted_iota(jnp.int32, (levels, width), 0)
    ).astype(F32)
    for o in range(count):
        wide_ref[o] = lax.dot_general(
            inverse_ref[o],
            spread,
            (((1,), (0,)), ((), ())),
            precision=lax.Precision.HIGHEST,
            preferred_element_type=F32,
        )
    lane = lax.broadcasted_iota(jnp.int32, (SUB, width), 1)
    sub = lax.broadcasted_iota(jnp.int32, (SUB, width), 0)
    diagonal = lane % SUB == sub
    zero = jnp.zeros((SUB, width), F32)
    offs_wide = [
        jnp.concatenate([offsb_ref[g * SUB : (g + 1) * SUB, :]] * (width // LANE), axis=1) for g in range(groups)
    ]

    def one_pair(k, _):
        rows = [[wide_ref[o, pl.ds(2 * k + i, 1), :] for o in range(count)] for i in range(2)]
        for g in range(groups):
            both = jnp.concatenate(
                [jnp.where(diagonal, choose(offs_wide[g], rows[i]), zero) for i in range(2)], axis=0
            )
            high, low = split_bf16(both)
            at = pl.multiple_of(k * 2 * SUB, 2 * SUB)
            big_ref[g, 0, pl.ds(at, 2 * SUB), :] = high
            big_ref[g, 1, pl.ds(at, 2 * SUB), :] = low
        return 0

    lax.fori_loop(0, levels // 2, one_pair, 0)


def forcing_kernel(
    fields_ref, diff_ref, west_ref, east_ref, big_ref, offsb_ref, coefs_ref, solved_ref, send_ref, keep_ref, work_ref
):
    parts, levels, lines, ny = fields_ref.shape
    groups = lines // SUB
    half = ny // 2
    count = coefs_ref.shape[0] // 6
    core = lax.axis_index("depth") % 2
    sub = lax.broadcasted_iota(jnp.int32, (SUB, ny), 0)

    for g in range(groups):
        first = g * SUB

        def one_level(k, _):
            centre, across, along, both = [], [], [], []
            for i in range(parts):
                c = fields_ref[i, k, first : first + SUB, :]
                north = pltpu.roll(c, ny - 1, 1)
                south = pltpu.roll(c, 1, 1)
                if g > 0:
                    row_w = fields_ref[i, k, first - 1 : first, :]
                else:
                    row_w = west_ref[i, pl.ds(k, 1), :]
                if g < groups - 1:
                    row_e = fields_ref[i, k, first + SUB : first + SUB + 1, :]
                else:
                    row_e = east_ref[i, pl.ds(k, 1), :]
                east = jnp.where(sub == SUB - 1, jnp.broadcast_to(row_e, c.shape), pltpu.roll(c, SUB - 1, 0))
                west = jnp.where(sub == 0, jnp.broadcast_to(row_w, c.shape), pltpu.roll(c, 1, 0))
                centre.append(c)
                both.append((east + west) + (north + south) - 4.0 * c)
                along.append(east - west)
                across.append(north - south)
            d = diff_ref[k, first : first + SUB, :]
            scale = 0.5 * wave_gain
            out = (
                centre[0] + d * both[0] - scale * along[2],
                centre[1] + d * both[1] - scale * across[2],
                centre[2] + d * both[2] - scale * (along[0] + across[1]),
            )
            at = pl.multiple_of(k * SUB, SUB)
            for i in range(parts):
                work_ref[i, pl.ds(at, SUB), :] = out[i]
            return 0

        lax.fori_loop(0, levels, one_level, 0, unroll=4)
        offs = offsb_ref[first : first + SUB, :]
        gate = choose(offs, [coefs_ref[4 * count + o : 4 * count + o + 1, :] for o in range(count)])
        face = choose(offs, [coefs_ref[5 * count + o : 5 * count + o + 1, :] for o in range(count)])
        for i in range(parts):
            x_high, x_low = split_bf16(work_ref[i])
            m_high = big_ref[g, 0]
            m_low = big_ref[g, 1]
            result = (
                jnp.dot(m_high, x_high, preferred_element_type=F32)
                + jnp.dot(m_low, x_high, preferred_element_type=F32)
                + jnp.dot(m_high, x_low, preferred_element_type=F32)
            )
            solved_ref[i, :, first : first + SUB, :] = result.reshape(levels, SUB, ny)
            last = result[(levels - 1) * SUB :, :]
            before = result[(levels - 2) * SUB : (levels - 1) * SUB, :]
            top = result[:SUB, :]
            for h in range(2):
                cut = slice(h * half, (h + 1) * half)
                a_side = last[:, cut] + gate * before[:, cut]
                b_side = face * top[:, cut]
                for k, value in enumerate((a_side, b_side)):
                    at = (k * parts + i) * lines + first

                    @pl.when(core == h)
                    def _():
                        keep_ref[at : at + SUB, :] = value

                    @pl.when(core != h)
                    def _():
                        send_ref[at : at + SUB, :] = value

    base = 2 * parts * lines
    send_ref[base : base + 4 * count, :] = coefs_ref[: 4 * count, :]
    keep_ref[base : base + 4 * count, :] = coefs_ref[: 4 * count, :]


def unpack(ref, rows, count):
    a_side = ref[:rows, :]
    b_side = ref[rows : 2 * rows, :]
    base = 2 * rows
    b, e, l, a = [ref[base + c * count : base + (c + 1) * count, :] for c in range(4)]
    return a_side, b_side, b, e, l, a


def per_line(offs, table, parts):
    rows = [table[o : o + 1, :] for o in range(table.shape[0])]
    value = choose(offs, rows)
    return jnp.concatenate([value] * parts, axis=0)


def merged(bit, mine_ref, got_ref, offs, parts, count):
    lines = offs.shape[0]
    rows = parts * lines
    lower_is_mine = (lax.axis_index("depth") >> bit) % 2 == 0
    mine = unpack(mine_ref, rows, count)
    got = unpack(got_ref, rows, count)
    a_1, b_1, cb_1, ce_1, cl_1, ca_1 = [jnp.where(lower_is_mine, x, y) for x, y in zip(mine, got)]
    a_2, b_2, cb_2, ce_2, cl_2, ca_2 = [jnp.where(lower_is_mine, y, x) for x, y in zip(mine, got)]
    inverse = 1.0 / (ca_1 + cb_2)
    total = a_1 + b_2
    down = ce_1 * inverse
    up = cl_2 * inverse
    a_new = a_2 - per_line(offs, up, parts) * total
    b_new = b_1 - per_line(offs, down, parts) * total
    cb = cb_1 - down * cl_1
    ce = -down * ce_2
    cl = -up * cl_1
    ca = ca_2 - up * ce_2
    middle = per_line(offs, inverse, parts) * total
    return (a_new, b_new, cb, ce, cl, ca), (middle, cl_1 * inverse, ce_2 * inverse)


def store_saved(saved_ref, saved, count):
    middle, low, high = saved
    rows = middle.shape[0]
    saved_ref[:rows, :] = middle
    saved_ref[rows : rows + count, :] = low
    saved_ref[rows + count : rows + 2 * count, :] = high


def store_element(ref, element, count):
    rows = element[0].shape[0]
    ref[:rows, :] = element[0]
    ref[rows : 2 * rows, :] = element[1]
    for c in range(4):
        ref[2 * rows + c * count : 2 * rows + (c + 1) * count, :] = element[2 + c]


def merge_kernel(bit, parts, count, mine_ref, got_ref, offsb_ref, element_ref, saved_ref):
    element, saved = merged(bit, mine_ref, got_ref, offsb_ref[...], parts, count)
    store_element(element_ref, element, count)
    store_saved(saved_ref, saved, count)


def merge_last_kernel(bit, parts, count, mine_ref, got_ref, offsb_ref, element_ref, saved_ref, send_ref):
    offs = offsb_ref[...]
    element, saved = merged(bit, mine_ref, got_ref, offs, parts, count)
    store_element(element_ref, element, count)
    store_saved(saved_ref, saved, count)
    a_side, b_side, cb, ce, cl, ca = element
    rows = a_side.shape[0]
    lower = (lax.axis_index("depth") >> (bit + 1)) == 0
    ratio = ce / ca
    send_ref[:rows, :] = jnp.where(lower, a_side, b_side - per_line(offs, ratio, parts) * a_side)
    send_ref[rows : rows + count, :] = jnp.where(lower, ca, cb - ratio * cl)


def solve_kernel(bits, parts, count, *refs):
    sent_ref, got_ref, element_ref, offsb_ref = refs[:4]
    saved_refs = refs[4 : 4 + bits]
    send_ref, keep_ref = refs[4 + bits :]
    offs = offsb_ref[...]
    rows = parts * offs.shape[0]
    rank = lax.axis_index("depth")
    pivot = sent_ref[rows : rows + count, :] + got_ref[rows : rows + count, :]
    shared = (sent_ref[:rows, :] + got_ref[:rows, :]) * per_line(offs, 1.0 / pivot, parts)
    a_side, _, _, _, cl, ca = unpack(element_ref, rows, count)
    inverse = 1.0 / ca
    top = per_line(offs, inverse, parts) * a_side - per_line(offs, cl * inverse, parts) * shared
    lower = (rank >> bits) == 0
    below = jnp.where(lower, jnp.zeros_like(shared), shared)
    above = jnp.where(lower, shared, top)
    for bit in reversed(range(bits)):
        saved_ref = saved_refs[bit]
        low = saved_ref[rows : rows + count, :]
        high = saved_ref[rows + count : rows + 2 * count, :]
        middle = saved_ref[:rows, :] - per_line(offs, low, parts) * below - per_line(offs, high, parts) * above
        lower = (rank >> bit) % 2 == 0
        if bit > 0:
            below, above = jnp.where(lower, below, middle), jnp.where(lower, middle, above)
        else:
            keep_ref[:rows, :] = jnp.where(lower, below, middle)
            keep_ref[rows:, :] = jnp.where(lower, middle, above)
            send_ref[:rows, :] = jnp.where(lower, middle, below)
            send_ref[rows:, :] = jnp.where(lower, above, middle)


def finish_kernel(solved_ref, own_ref, other_ref, offsb_ref, spikes_ref, out_ref):
    parts, levels, lines, ny = solved_ref.shape
    groups = lines // SUB
    half = ny // 2
    count = spikes_ref.shape[1]
    rows = parts * lines
    core = lax.axis_index("depth") % 2
    for g in range(groups):
        first = g * SUB
        offs = offsb_ref[first : first + SUB, :]
        ends = []
        for k in range(2):
            for i in range(parts):
                at = k * rows + i * lines + first
                own = own_ref[at : at + SUB, :]
                other = other_ref[at : at + SUB, :]
                ends.append((jnp.where(core == 0, own, other), jnp.where(core == 0, other, own)))

        def one_level(k, _):
            low = choose(offs, [spikes_ref[0, o, pl.ds(k, 1), :] for o in range(count)])
            high = choose(offs, [spikes_ref[1, o, pl.ds(k, 1), :] for o in range(count)])
            for i in range(parts):
                for h in range(2):
                    cut = slice(h * half, (h + 1) * half)
                    value = solved_ref[i, k, first : first + SUB, cut]
                    out_ref[i, k, first : first + SUB, cut] = (
                        value + low * ends[i][h] + high * ends[parts + i][h]
                    )
            return 0

        lax.fori_loop(0, levels - 1, one_level, 0, unroll=2)
        for i in range(parts):
            for h in range(2):
                cut = slice(h * half, (h + 1) * half)
                out_ref[i, levels - 1, first : first + SUB, cut] = ends[parts + i][h]


def call(kernel, outs, args, scratch=(), specs=None):
    return pl.pallas_call(
        kernel,
        out_shape=[jax.ShapeDtypeStruct(s, d) for s, d in outs],
        in_specs=specs or [vmem_spec()] * len(args),
        out_specs=[vmem_spec()] * len(outs),
        scratch_shapes=list(scratch),
    )(*args)


def body(fields, diffusivity, offsets, coupling, inverse):
    parts, levels, lines, ny = fields.shape
    count = inverse.shape[0]
    half = ny // 2
    groups = lines // SUB
    width = levels * SUB
    around = lax.axis_size("horiz")
    ranks = lax.axis_size("depth")
    bits = ranks.bit_length() - 1
    assert ranks == 1 << bits and bits >= 2 and half == LANE

    def swap(x, bit):
        return lax.ppermute(x, "depth", [(i, i ^ (1 << bit)) for i in range(ranks)])

    forward = [(i, (i + 1) % around) for i in range(around)]
    backward = [(i, (i - 1) % around) for i in range(around)]
    west = lax.ppermute(fields[:, :, lines - 1, :], "horiz", forward)
    east = lax.ppermute(fields[:, :, 0, :], "horiz", backward)

    big, offsb, spikes, coefs = call(
        table_kernel,
        [
            ((groups, 2, width, width), BF16),
            ((lines, LANE), jnp.int32),
            ((2, count, levels, LANE), F32),
            ((6 * count, LANE), F32),
        ],
        (offsets, coupling, inverse),
        scratch=[pltpu.VMEM((count, levels, width), F32)],
        specs=[pl.BlockSpec(memory_space=pltpu.SMEM), vmem_spec(), vmem_spec()],
    )
    rows = parts * lines
    element_shape = ((2 * rows + 4 * count, half), F32)
    saved_shape = ((rows + 2 * count, half), F32)
    solved, send, keep = call(
        forcing_kernel,
        [((parts, levels, lines, ny), F32), element_shape, element_shape],
        (fields, diffusivity, west, east, big, offsb, coefs),
        scratch=[pltpu.VMEM((parts, width, ny), F32)],
    )
    got = swap(send, 0)
    mine = keep
    saved = []
    for bit in range(bits - 1):
        if bit < bits - 2:
            mine, kept = call(
                functools.partial(merge_kernel, bit, parts, count),
                [element_shape, saved_shape],
                (mine, got, offsb),
            )
            got = swap(mine, bit + 1)
        else:
            mine, kept, send = call(
                functools.partial(merge_last_kernel, bit, parts, count),
                [element_shape, saved_shape, ((rows + count, half), F32)],
                (mine, got, offsb),
            )
            got = swap(send, bit + 1)
        saved.append(kept)
    pair = ((2 * rows, half), F32)
    theirs, own = call(
        functools.partial(solve_kernel, bits - 1, parts, count),
        [pair, pair],
        (send, got, mine, offsb, *saved),
    )
    other = swap(theirs, 0)
    (out,) = call(
        finish_kernel,
        [((parts, levels, lines, ny), F32)],
        (solved, own, other, offsb, spikes),
    )
    return out


def solution(mesh):
    return jax.shard_map(
        body,
        mesh=mesh,
        in_specs=(
            P(None, "depth", "horiz", None),
            P("depth", "horiz", None),
            P("horiz"),
            P(None, "depth"),
            P(None, "depth", None),
        ),
        out_specs=P(None, "depth", "horiz", None),
        check_vma=False,
    )
```

time: 156 us -> 49.8 us (0.32); the launches traced: 154 us -> 49.5 us
  blocking collectives: 54.6 us -> 0 us
  other arithmetic: 42.9 us -> 0 us
  local copies, waits for them, and re-layouts: 45.6 us -> 4.69 us
  Pallas kernels: 0 us -> 24.7 us
  waiting for transfers between devices: 0.01 us -> 11.9 us
  matrix products: 3.67 us -> 0 us
  starting transfers between devices: 6.49 us -> 8.22 us
    all_gather x3 -> x0, blocking collectives: 36 us -> none  [the longest x1 17.2 us: body(): lax.all_gather(target[None], 'depth', axis=0, tiled=True)]
    dynamic_update_slice x16 -> x0, other arithmetic: 25.9 us -> none  [thomas(): lax.scan(forward_step, (start_ratio, anchor), (lower_band, main_band, upp...]
    pallas_call x0 -> x6, Pallas kernels: none -> 24.7 us  [call(): pl.pallas_call(kernel, out_shape=[jax.ShapeDtypeStruct(s, d) for s, d in...]
    unnamed x1 -> x0, blocking collectives: 18.5 us -> none
    ppermute x4 -> x6, waiting for transfers between devices: 0.01 us -> 11.9 us  [the longest x4 9.34 us: swap(): return lax.ppermute(x, 'depth', [(i, i ^ 1 << bit) for i in range(ranks)])]
    dynamic_update_slice x8 -> x0, local copies, waits for them, and re-layouts: 10.2 us -> none  [thomas(): lax.scan(forward_step, (start_ratio, anchor), (lower_band, main_band, upp...]
    add x3 -> x0, other arithmetic: 6.14 us -> none  [the longest x1 5.35 us: tendency(): pushed = centre + diffusivity[None] * laplace]
    slice x5 -> x1, local copies, waits for them, and re-layouts: 7.1 us -> 1.51 us  [body(): east = lax.ppermute(fields[:, :, 0, :], 'horiz', backward)]
  transfers between devices with their start and end apart: 4 -> 6, of which waited for: 0 -> 6; matrix products, arithmetic and copies ran while one was open for 17% -> 0% of each run, Pallas kernels for 0% -> 5%
where the time goes in v1:
time: 49.8 us; the launch traced here: 49.5 us
  Pallas kernels  24.7 us (50%)
  waiting for transfers between devices  11.9 us (24%)
  starting transfers between devices  8.22 us (17%)
  local copies, waits for them, and re-layouts  4.69 us (9%)
    pallas_call x6, Pallas kernels, call(): pl.pallas_call(kernel, out_shape=[jax.ShapeDtypeStruct(s, d) for s, d in...  24.7 us
    ppermute x4, waiting for transfers between devices, swap(): return lax.ppermute(x, 'depth', [(i, i ^ 1 << bit) for i in range(ranks)])  9.34 us
    ppermute x4, starting transfers between devices, swap(): return lax.ppermute(x, 'depth', [(i, i ^ 1 << bit) for i in range(ranks)])  4.17 us
    unnamed x14, local copies, waits for them, and re-layouts  3.18 us
    ppermute x1, starting transfers between devices, body(): west = lax.ppermute(fields[:, :, lines - 1, :], 'horiz', forward)  3.02 us
    ppermute x1, waiting for transfers between devices, body(): east = lax.ppermute(fields[:, :, 0, :], 'horiz', backward)  1.77 us
    slice x1, local copies, waits for them, and re-layouts, body(): east = lax.ppermute(fields[:, :, 0, :], 'horiz', backward)  1.51 us
    ppermute x1, starting transfers between devices, body(): east = lax.ppermute(fields[:, :, 0, :], 'horiz', backward)  1.03 us
  transfers between devices with their start and end apart: 6, of which 6 were waited for; matrix products, arithmetic and copies ran while one was open for 0% of the time, Pallas kernels for 5%

profile of v1, /device:TPU:0, one launch (start us, length us, event | category | flops | bytes accessed | tf_op | source)
XLA Modules:
  0.0 49.5 jit_solution(2502053192858932460)
XLA Ops:
  0.0 1.5 %fusion = (f32[3,32,1,256]{3,2,1,0:T(1,128)S(1)}, f32[3,32,1,256]{3,2,1,0:T(1,128)S(1)}) fusion(f32[3,32,32,256]{3,2,1,0:T(8,128)} %fields_ref.1), kind=kLoop, calls=%fused_computation.2 | loop fusion | bytes 393216 | tf_op jit(solution)/shard_map/slice | solution.py:346
  1.5 3.0 %collective-permute-start = (f32[3,32,256]{2,1,0:T(8,128)S(1)}, f32[3,32,256]{2,1,0:T(8,128)S(1)}, u32[]{:S(2)}, u32[]{:S(2)}) collective-permute-start(f32[3,32,256]{2,1,0:T(8,128)S(1)} %bitcast.6), channel_id=1, source_target_pairs={{0,8},{8,16},{16,24},{24,0},{1,9},{9,17},{17,25},{25,1},{2,10},{10... | collective-permute-start | bytes 294920 | tf_op jit(solution)/shard_map/ppermute | solution.py:345
  4.6 1.0 %collective-permute-start.1 = (f32[3,32,256]{2,1,0:T(8,128)S(1)}, f32[3,32,256]{2,1,0:T(8,128)S(1)}, u32[]{:S(2)}, u32[]{:S(2)}) collective-permute-start(f32[3,32,256]{2,1,0:T(8,128)S(1)} %bitcast.7), channel_id=1, source_target_pairs={{0,24},{8,0},{16,8},{24,16},{1,25},{9,1},{17,9},{25,17},{2,26},{10... | collective-permute-start | bytes 294920 | tf_op jit(solution)/shard_map/ppermute | solution.py:346
  5.6 2.5 %shard_map.55 = (bf16[4,2,256,256]{3,2,1,0:T(8,128)(2,1)}, s32[32,128]{1,0:T(8,128)}, f32[2,4,32,128]{3,2,1,0:T(8,128)}, f32[24,128]{1,0:T(8,128)}) custom-call(s32[32]{0:T(128)} %offs_ref.1, f32[4,32]{1,0:T(4,128)} %coupling_ref.1, f32[4,32,32]{2,1,0:T(8,128)} %inverse_ref.1), custom_call_target="tpu_custom_call" | custom-call | tf_op jit(solution)/shard_map/pallas_call | solution.py:320
  8.1 0.8 %collective-permute-done.west_ref = f32[3,32,256]{2,1,0:T(8,128)S(1)} collective-permute-done((f32[3,32,256]{2,1,0:T(8,128)S(1)}, f32[3,32,256]{2,1,0:T(8,128)S(1)}, u32[]{:S(2)}, u32[]{:S(2)}) %collective-permute-start) | collective-permute-done | bytes 98336 | tf_op jit(solution)/shard_map/ppermute | solution.py:345
  8.9 0.0 copy-start.2
  8.9 1.8 %collective-permute-done.1.east_ref = f32[3,32,256]{2,1,0:T(8,128)S(1)} collective-permute-done((f32[3,32,256]{2,1,0:T(8,128)S(1)}, f32[3,32,256]{2,1,0:T(8,128)S(1)}, u32[]{:S(2)}, u32[]{:S(2)}) %collective-permute-start.1) | collective-permute-done | bytes 98336 | tf_op jit(solution)/shard_map/ppermute | solution.py:346
  10.7 0.0 copy-start.3
  10.7 0.0 copy-done.2
  10.7 0.6 %copy-done.3 = f32[3,32,256]{2,1,0:T(8,128)} copy-done((f32[3,32,256]{2,1,0:T(8,128)}, f32[3,32,256]{2,1,0:T(8,128)S(1)}, u32[]{:S(2)}) %copy-start.3) | copy-done | bytes 98328
  11.3 12.6 %shard_map.56 = (f32[3,32,32,256]{3,2,1,0:T(8,128)}, f32[208,128]{1,0:T(8,128)}, f32[208,128]{1,0:T(8,128)}) custom-call(f32[3,32,32,256]{3,2,1,0:T(8,128)} %fields_ref.1, f32[32,32,256]{2,1,0:T(8,128)} %diff_ref.1, f32[3,32,256]{2,1,0:T(8,128)} %copy-done.2, f32[3,32,256]{2,1,0:T(8,128)} %copy-done.3, bf16[4,2,256,256]{3,2,1,0:T(8,128)(2,1)} %get-tuple-element.19.big_ref, ...), custom_call_target="tpu_custom_call" | custom-call | tf_op jit(solution)/shard_map/pallas_call | solution.py:320
  23.9 0.0 collective-permute-start.2
  23.9 1.5 %collective-permute-done.2.got_ref = f32[208,128]{1,0:T(8,128)S(1)} collective-permute-done((f32[208,128]{1,0:T(8,128)}, f32[208,128]{1,0:T(8,128)S(1)}, u32[]{:S(2)}, u32[]{:S(2)}) %collective-permute-start.2) | collective-permute-done | bytes 106528 | tf_op jit(solution)/shard_map/ppermute | solution.py:341
  25.4 0.0 copy-start
  25.4 0.6 %copy-done = f32[208,128]{1,0:T(8,128)} copy-done((f32[208,128]{1,0:T(8,128)}, f32[208,128]{1,0:T(8,128)S(1)}, u32[]{:S(2)}) %copy-start) | copy-done | bytes 106520
  26.1 1.7 %shard_map.57 = (f32[208,128]{1,0:T(8,128)}, f32[104,128]{1,0:T(8,128)}) custom-call(f32[208,128]{1,0:T(8,128)} %get-tuple-element.23.mine_ref, f32[208,128]{1,0:T(8,128)} %copy-done, s32[32,128]{1,0:T(8,128)} %get-tuple-element.20.offsb_ref.refs_3_), custom_call_target="tpu_custom_call" | custom-call | tf_op jit(solution)/shard_map/pallas_call | solution.py:320
  27.7 1.6 %collective-permute-start.3 = (f32[208,128]{1,0:T(8,128)}, f32[208,128]{1,0:T(8,128)S(1)}, u32[]{:S(2)}, u32[]{:S(2)}) collective-permute-start(f32[208,128]{1,0:T(8,128)} %get-tuple-element.25.mine_ref), channel_id=1, source_target_pairs={{0,2},{1,3},{2,0},{3,1},{4,6},{5,7},{6,4},{7,5},{8,10},{9,11},{10,... | collective-permute-start | bytes 319496 | tf_op jit(solution)/shard_map/ppermute | solution.py:341
  29.3 3.7 %collective-permute-done.3.got_ref = f32[208,128]{1,0:T(8,128)S(1)} collective-permute-done((f32[208,128]{1,0:T(8,128)}, f32[208,128]{1,0:T(8,128)S(1)}, u32[]{:S(2)}, u32[]{:S(2)}) %collective-permute-start.3) | collective-permute-done | bytes 106528 | tf_op jit(solution)/shard_map/ppermute | solution.py:341
  33.0 0.0 copy-start.1
  33.0 0.6 %copy-done.1 = f32[208,128]{1,0:T(8,128)} copy-done((f32[208,128]{1,0:T(8,128)}, f32[208,128]{1,0:T(8,128)S(1)}, u32[]{:S(2)}) %copy-start.1) | copy-done | bytes 106520
  33.6 1.7 %shard_map.58 = (f32[208,128]{1,0:T(8,128)}, f32[104,128]{1,0:T(8,128)}, f32[100,128]{1,0:T(8,128)}) custom-call(f32[208,128]{1,0:T(8,128)} %get-tuple-element.25.mine_ref, f32[208,128]{1,0:T(8,128)} %copy-done.1, s32[32,128]{1,0:T(8,128)} %get-tuple-element.20.offsb_ref.refs_3_), custom_call_target="tpu_custom_call" | custom-call | tf_op jit(solution)/shard_map/pallas_call | solution.py:320
  35.3 2.6 %collective-permute-start.4 = (f32[100,128]{1,0:T(8,128)}, f32[100,128]{1,0:T(8,128)S(1)}, u32[]{:S(2)}, u32[]{:S(2)}) collective-permute-start(f32[100,128]{1,0:T(8,128)} %get-tuple-element.26.refs_0_), channel_id=1, source_target_pairs={{0,4},{1,5},{2,6},{3,7},{4,0},{5,1},{6,2},{7,3},{8,12},{9,13},{10,... | collective-permute-start | bytes 153608 | tf_op jit(solution)/shard_map/ppermute | solution.py:341
  37.9 2.7 %collective-permute-done.4.refs_1_ = f32[100,128]{1,0:T(8,128)S(1)} collective-permute-done((f32[100,128]{1,0:T(8,128)}, f32[100,128]{1,0:T(8,128)S(1)}, u32[]{:S(2)}, u32[]{:S(2)}) %collective-permute-start.4) | collective-permute-done | bytes 51232 | tf_op jit(solution)/shard_map/ppermute | solution.py:341
  40.5 0.0 copy-start.5
  40.5 0.6 %copy-done.5 = f32[100,128]{1,0:T(8,128)} copy-done((f32[100,128]{1,0:T(8,128)}, f32[100,128]{1,0:T(8,128)S(1)}, u32[]{:S(2)}) %copy-start.5) | copy-done | bytes 51224
  41.1 1.7 %shard_map.59 = (f32[192,128]{1,0:T(8,128)}, f32[192,128]{1,0:T(8,128)}) custom-call(f32[100,128]{1,0:T(8,128)} %get-tuple-element.26.refs_0_, f32[100,128]{1,0:T(8,128)} %copy-done.5, f32[208,128]{1,0:T(8,128)} %get-tuple-element.27.refs_2_, s32[32,128]{1,0:T(8,128)} %get-tuple-element.20.offsb_ref.refs_3_, f32[104,128]{1,0:T(8,128)} %get-tuple-element.28.refs_4_, ...), custom_call_target="tpu_custom_call" | custom-call | tf_op jit(solution)/shard_map/pallas_call | solution.py:320
  42.9 0.0 collective-permute-start.5
  42.9 1.5 %collective-permute-done.5.other_ref = f32[192,128]{1,0:T(8,128)S(1)} collective-permute-done((f32[192,128]{1,0:T(8,128)}, f32[192,128]{1,0:T(8,128)S(1)}, u32[]{:S(2)}, u32[]{:S(2)}) %collective-permute-start.5) | collective-permute-done | bytes 98336 | tf_op jit(solution)/shard_map/ppermute | solution.py:341
  44.4 0.0 copy-start.4
  44.4 0.6 %copy-done.4 = f32[192,128]{1,0:T(8,128)} copy-done((f32[192,128]{1,0:T(8,128)}, f32[192,128]{1,0:T(8,128)S(1)}, u32[]{:S(2)}) %copy-start.4) | copy-done | bytes 98328
  45.0 4.5 %shard_map.60 = f32[3,32,32,256]{3,2,1,0:T(8,128)} custom-call(f32[3,32,32,256]{3,2,1,0:T(8,128)} %get-tuple-element.22.solved_ref, f32[192,128]{1,0:T(8,128)} %get-tuple-element.30.own_ref, f32[192,128]{1,0:T(8,128)} %copy-done.4, s32[32,128]{1,0:T(8,128)} %get-tuple-element.20.offsb_ref.refs_3_, f32[2,4,32,128]{3,2,1,0:T(8,128)} %get-tuple-element.32.spikes_ref), custom_call_target="tpu_custom_call" | custom-call | tf_op jit(solution)/shard_map/pallas_call | solution.py:320
  (2 shorter events, 0.0 us)
Async XLA Ops:
  1.5 7.4 %collective-permute-start = (f32[3,32,256]{2,1,0:T(8,128)S(1)}, f32[3,32,256]{2,1,0:T(8,128)S(1)}, u32[]{:S(2)}, u32[]{:S(2)}) collective-permute-start(f32[3,32,256]{2,1,0:T(8,128)S(1)} %bitcast.6), channel_id=1, source_target_pairs={{0,8},{8,16},{16,24},{24,0},{1,9},{9,17},{17,25},{25,1},{2,10},{10... | collective-permute-start | bytes 294920 | tf_op jit(solution)/shard_map/ppermute | solution.py:345
  4.6 6.1 %collective-permute-start.1 = (f32[3,32,256]{2,1,0:T(8,128)S(1)}, f32[3,32,256]{2,1,0:T(8,128)S(1)}, u32[]{:S(2)}, u32[]{:S(2)}) collective-permute-start(f32[3,32,256]{2,1,0:T(8,128)S(1)} %bitcast.7), channel_id=1, source_target_pairs={{0,24},{8,0},{16,8},{24,16},{1,25},{9,1},{17,9},{25,17},{2,26},{10... | collective-permute-start | bytes 294920 | tf_op jit(solution)/shard_map/ppermute | solution.py:346
  8.9 1.8 %copy-start.2 = (f32[3,32,256]{2,1,0:T(8,128)}, f32[3,32,256]{2,1,0:T(8,128)S(1)}, u32[]{:S(2)}) copy-start(f32[3,32,256]{2,1,0:T(8,128)S(1)} %collective-permute-done.west_ref) | copy-start | bytes 294916
  10.7 0.6 %copy-start.3 = (f32[3,32,256]{2,1,0:T(8,128)}, f32[3,32,256]{2,1,0:T(8,128)S(1)}, u32[]{:S(2)}) copy-start(f32[3,32,256]{2,1,0:T(8,128)S(1)} %collective-permute-done.1.east_ref) | copy-start | bytes 294916
  23.9 1.5 %collective-permute-start.2 = (f32[208,128]{1,0:T(8,128)}, f32[208,128]{1,0:T(8,128)S(1)}, u32[]{:S(2)}, u32[]{:S(2)}) collective-permute-start(f32[208,128]{1,0:T(8,128)} %get-tuple-element.24), channel_id=1, source_target_pairs={{0,1},{1,0},{2,3},{3,2},{4,5},{5,4},{6,7},{7,6},{8,9},{9,8},{10,11... | collective-permute-start | bytes 319496 | tf_op jit(solution)/shard_map/ppermute | solution.py:341
  25.4 0.6 %copy-start = (f32[208,128]{1,0:T(8,128)}, f32[208,128]{1,0:T(8,128)S(1)}, u32[]{:S(2)}) copy-start(f32[208,128]{1,0:T(8,128)S(1)} %collective-permute-done.2.got_ref) | copy-start | bytes 319492
  27.7 5.2 %collective-permute-start.3 = (f32[208,128]{1,0:T(8,128)}, f32[208,128]{1,0:T(8,128)S(1)}, u32[]{:S(2)}, u32[]{:S(2)}) collective-permute-start(f32[208,128]{1,0:T(8,128)} %get-tuple-element.25.mine_ref), channel_id=1, source_target_pairs={{0,2},{1,3},{2,0},{3,1},{4,6},{5,7},{6,4},{7,5},{8,10},{9,11},{10,... | collective-permute-start | bytes 319496 | tf_op jit(solution)/shard_map/ppermute | solution.py:341
  33.0 0.6 %copy-start.1 = (f32[208,128]{1,0:T(8,128)}, f32[208,128]{1,0:T(8,128)S(1)}, u32[]{:S(2)}) copy-start(f32[208,128]{1,0:T(8,128)S(1)} %collective-permute-done.3.got_ref) | copy-start | bytes 319492
  35.3 5.2 %collective-permute-start.4 = (f32[100,128]{1,0:T(8,128)}, f32[100,128]{1,0:T(8,128)S(1)}, u32[]{:S(2)}, u32[]{:S(2)}) collective-permute-start(f32[100,128]{1,0:T(8,128)} %get-tuple-element.26.refs_0_), channel_id=1, source_target_pairs={{0,4},{1,5},{2,6},{3,7},{4,0},{5,1},{6,2},{7,3},{8,12},{9,13},{10,... | collective-permute-start | bytes 153608 | tf_op jit(solution)/shard_map/ppermute | solution.py:341
  40.5 0.6 %copy-start.5 = (f32[100,128]{1,0:T(8,128)}, f32[100,128]{1,0:T(8,128)S(1)}, u32[]{:S(2)}) copy-start(f32[100,128]{1,0:T(8,128)S(1)} %collective-permute-done.4.refs_1_) | copy-start | bytes 153604
  42.9 1.5 %collective-permute-start.5 = (f32[192,128]{1,0:T(8,128)}, f32[192,128]{1,0:T(8,128)S(1)}, u32[]{:S(2)}, u32[]{:S(2)}) collective-permute-start(f32[192,128]{1,0:T(8,128)} %get-tuple-element.31), channel_id=1, source_target_pairs={{0,1},{1,0},{2,3},{3,2},{4,5},{5,4},{6,7},{7,6},{8,9},{9,8},{10,11... | collective-permute-start | bytes 294920 | tf_op jit(solution)/shard_map/ppermute | solution.py:341
  44.4 0.6 %copy-start.4 = (f32[192,128]{1,0:T(8,128)}, f32[192,128]{1,0:T(8,128)S(1)}, u32[]{:S(2)}) copy-start(f32[192,128]{1,0:T(8,128)S(1)} %collective-permute-done.5.other_ref) | copy-start | bytes 294916

commit v2 on v1

v2 whole, which is shorter than its diff:
```python
import functools

import jax
import jax.numpy as jnp
from jax import lax
from jax.experimental import pallas as pl
from jax.experimental.pallas import tpu as pltpu
from jax.sharding import PartitionSpec as P

wave_gain = 0.5
SUB = 8
LANE = 128
VMEM = pltpu.VMEM
F32 = jnp.float32
BF16 = jnp.bfloat16


def vmem_spec():
    return pl.BlockSpec(memory_space=VMEM)


def choose(offs, rows):
    value = jnp.broadcast_to(rows[0], offs.shape)
    for o in range(1, len(rows)):
        value = jnp.where(offs == o, jnp.broadcast_to(rows[o], offs.shape), value)
    return value


def split_bf16(x):
    high = x.astype(BF16)
    low = (x - high.astype(F32)).astype(BF16)
    return high, low


def outermost_kernel(fields_ref, first_ref, last_ref, stage_ref, sems):
    parts, levels, lines, ny = fields_ref.shape
    copies = []
    for e, start in enumerate((0, lines - SUB)):
        copy = pltpu.make_async_copy(fields_ref.at[:, :, pl.ds(start, SUB), :], stage_ref.at[e], sems.at[e])
        copy.start()
        copies.append(copy)
    sub = lax.broadcasted_iota(jnp.int32, (SUB, ny), 0)
    for e, (line, ref) in enumerate(((0, first_ref), (SUB - 1, last_ref))):
        copies[e].wait()
        for i in range(parts):
            for c in range(levels // SUB):
                value = jnp.zeros((SUB, ny), F32)
                for t in range(SUB):
                    row = stage_ref[e, i, c * SUB + t, line : line + 1, :]
                    value = jnp.where(sub == t, jnp.broadcast_to(row, value.shape), value)
                ref[i, c * SUB : (c + 1) * SUB, :] = value


def fill_tables(offs_ref, coupling_ref, inverse_ref, offsb_ref, spikes_ref, rows_ref, coefs_ref):
    count, levels, _ = inverse_ref.shape
    lines = offsb_ref.shape[0]
    rank = lax.axis_index("depth")

    sub = lax.broadcasted_iota(jnp.int32, (SUB, LANE), 0)
    for g in range(lines // SUB):
        value = jnp.zeros((SUB, LANE), jnp.int32)
        for j in range(SUB):
            value = jnp.where(sub == j, offs_ref[g * SUB + j], value)
        offsb_ref[g * SUB : (g + 1) * SUB, :] = value

    eye = lax.broadcasted_iota(jnp.int32, (levels, levels), 0) == lax.broadcasted_iota(
        jnp.int32, (levels, levels), 1
    )
    for o in range(count):
        gate = jnp.broadcast_to(coupling_ref[o : o + 1, levels - 1 : levels], (1, LANE))
        face = jnp.broadcast_to(coupling_ref[o : o + 1, 0:1], (1, LANE))
        face = jnp.where(rank > 0, face, jnp.zeros_like(face))
        low = jnp.broadcast_to(inverse_ref[o, :, 0:1], (levels, LANE)) * face
        high = jnp.broadcast_to(inverse_ref[o, :, levels - 2 : levels - 1], (levels, LANE)) * gate
        spikes_ref[0, o] = low
        spikes_ref[1, o] = high
        for k, level in enumerate((0, levels - 2)):
            row = jnp.broadcast_to(inverse_ref[o, level : level + 1, :], (levels, levels))
            column = jnp.sum(jnp.where(eye, row, jnp.zeros_like(row)), axis=1, keepdims=True)
            rows_ref[k, o] = jnp.broadcast_to(column, (levels, LANE))
        b = face - face * low[0:1]
        e = -face * high[0:1]
        l = -gate * low[levels - 2 : levels - 1]
        a = 1.0 + gate - gate * high[levels - 2 : levels - 1]
        for c, row in enumerate((b, e, l, a, gate, face)):
            coefs_ref[c * count + o : c * count + o + 1, :] = row


def force_group(
    g, slot, stages, fields_ref, diff_ref, west_ref, east_ref, offsb_ref, rows_ref, coefs_ref, forcing_ref, sides_ref
):
    parts, levels, lines, ny = fields_ref.shape
    groups = lines // SUB
    half = ny // 2
    count = rows_ref.shape[1]
    first = g * SUB
    sub = lax.broadcasted_iota(jnp.int32, (SUB, ny), 0)
    offs = offsb_ref[first : first + SUB, :]
    gate = choose(offs, [coefs_ref[4 * count + o : 4 * count + o + 1, :] for o in range(count)])
    face = choose(offs, [coefs_ref[5 * count + o : 5 * count + o + 1, :] for o in range(count)])

    def one_level(k, sums):
        centre, across, along, both = [], [], [], []
        for i in range(parts):
            c = fields_ref[i, k, first : first + SUB, :]
            north = pltpu.roll(c, ny - 1, 1)
            south = pltpu.roll(c, 1, 1)
            if g > 0:
                row_w = fields_ref[i, k, first - 1 : first, :]
            else:
                row_w = west_ref[i, pl.ds(k, 1), :]
            if g < groups - 1:
                row_e = fields_ref[i, k, first + SUB : first + SUB + 1, :]
            else:
                row_e = east_ref[i, pl.ds(k, 1), :]
            east = jnp.where(sub == SUB - 1, jnp.broadcast_to(row_e, c.shape), pltpu.roll(c, SUB - 1, 0))
            west = jnp.where(sub == 0, jnp.broadcast_to(row_w, c.shape), pltpu.roll(c, 1, 0))
            centre.append(c)
            both.append((east + west) + (north + south) - 4.0 * c)
            along.append(east - west)
            across.append(north - south)
        d = diff_ref[k, first : first + SUB, :]
        scale = 0.5 * wave_gain
        out = (
            centre[0] + d * both[0] - scale * along[2],
            centre[1] + d * both[1] - scale * across[2],
            centre[2] + d * both[2] - scale * (along[0] + across[1]),
        )
        at = pl.multiple_of(k * SUB, SUB)
        top = choose(offs, [rows_ref[0, o, pl.ds(k, 1), :] for o in range(count)])
        bottom = choose(offs, [rows_ref[1, o, pl.ds(k, 1), :] for o in range(count)])
        new = []
        for i in range(parts):
            forcing_ref[slot, i, pl.ds(at, SUB), :] = out[i]
            for h in range(2):
                piece = out[i][:, h * half : (h + 1) * half]
                at_0, at_1 = sums[2 * (i * 2 + h)], sums[2 * (i * 2 + h) + 1]
                new += [at_0 + top * piece, at_1 + bottom * piece]
        return tuple(new)

    sums = tuple(jnp.zeros((SUB, half), F32) for _ in range(4 * parts))
    step = levels // len(stages)
    for c, wait in enumerate(stages):
        wait()
        sums = lax.fori_loop(c * step, (c + 1) * step, one_level, sums, unroll=step)
    for i in range(parts):
        for h in range(2):
            cut = slice(h * half, (h + 1) * half)
            last = forcing_ref[slot, i, (levels - 1) * SUB :, cut]
            sides_ref[0, i, slot, :, cut] = last + gate * sums[2 * (i * 2 + h) + 1]
            sides_ref[1, i, slot, :, cut] = face * sums[2 * (i * 2 + h)]


def nothing():
    pass


def inner_kernel(
    fields_hbm,
    diff_hbm,
    offs_ref,
    coupling_ref,
    inverse_ref,
    fields_ref,
    diff_ref,
    offsb_ref,
    spikes_ref,
    rows_ref,
    coefs_ref,
    forcing_ref,
    sides_ref,
    sems,
):
    parts, levels, lines, _ = fields_ref.shape
    groups = lines // SUB
    chunks = sems.shape[0] // (parts + 1)
    step = levels // chunks
    waits = []
    for c in range(chunks):
        at = pl.ds(c * step, step)
        copies = [
            pltpu.make_async_copy(fields_hbm.at[i, at], fields_ref.at[i, at], sems.at[c * (parts + 1) + i])
            for i in range(parts)
        ]
        copies.append(pltpu.make_async_copy(diff_hbm.at[at], diff_ref.at[at], sems.at[c * (parts + 1) + parts]))
        for copy in copies:
            copy.start()
        waits.append(lambda copies=copies: [copy.wait() for copy in copies])
    fill_tables(offs_ref, coupling_ref, inverse_ref, offsb_ref, spikes_ref, rows_ref, coefs_ref)
    for slot, g in enumerate(range(1, groups - 1)):
        force_group(
            g,
            slot,
            waits if slot == 0 else [nothing] * chunks,
            fields_ref,
            diff_ref,
            None,
            None,
            offsb_ref,
            rows_ref,
            coefs_ref,
            forcing_ref,
            sides_ref,
        )


def edge_kernel(
    fields_ref,
    diff_ref,
    west_ref,
    east_ref,
    offsb_ref,
    rows_ref,
    coefs_ref,
    inner_ref,
    forcing_ref,
    send_ref,
    keep_ref,
    sides_ref,
):
    parts, levels, lines, ny = fields_ref.shape
    groups = lines // SUB
    half = ny // 2
    count = rows_ref.shape[1]
    core = lax.axis_index("depth") % 2
    for slot, g in enumerate((0, groups - 1)):
        force_group(
            g,
            slot,
            [nothing] * (levels // SUB),
            fields_ref,
            diff_ref,
            west_ref,
            east_ref,
            offsb_ref,
            rows_ref,
            coefs_ref,
            forcing_ref,
            sides_ref,
        )
    for g in range(groups):
        ref, slot = place(g, groups, inner_ref, sides_ref)
        for i in range(parts):
            for k in range(2):
                at = (k * parts + i) * lines + g * SUB
                left, right = ref[k, i, slot, :, :half], ref[k, i, slot, :, half:]
                keep_ref[at : at + SUB, :] = jnp.where(core == 0, left, right)
                send_ref[at : at + SUB, :] = jnp.where(core == 0, right, left)

    base = 2 * parts * lines
    send_ref[base : base + 4 * count, :] = coefs_ref[: 4 * count, :]
    keep_ref[base : base + 4 * count, :] = coefs_ref[: 4 * count, :]


def place(g, groups, inner_ref, outer_ref):
    if g == 0:
        return outer_ref, 0
    if g == groups - 1:
        return outer_ref, 1
    return inner_ref, g - 1


def block_kernel(after_ref, inner_ref, outer_ref, offsb_ref, inverse_ref, solved_ref, token_ref, wide_ref, big_ref):
    count, levels, _ = inverse_ref.shape
    groups, parts, width, ny = solved_ref.shape
    token_ref[...] = after_ref[:SUB, :]

    spread = (
        lax.broadcasted_iota(jnp.int32, (levels, width), 1) // SUB
        == lax.broadcasted_iota(jnp.int32, (levels, width), 0)
    ).astype(F32)
    for o in range(count):
        wide_ref[o] = lax.dot_general(
            inverse_ref[o],
            spread,
            (((1,), (0,)), ((), ())),
            precision=lax.Precision.HIGHEST,
            preferred_element_type=F32,
        )
    lane = lax.broadcasted_iota(jnp.int32, (SUB, width), 1)
    sub = lax.broadcasted_iota(jnp.int32, (SUB, width), 0)
    diagonal = lane % SUB == sub
    zero = jnp.zeros((SUB, width), F32)
    offs_wide = [
        jnp.concatenate([offsb_ref[g * SUB : (g + 1) * SUB, :]] * (width // LANE), axis=1) for g in range(groups)
    ]

    def one_pair(k, _):
        rows = [[wide_ref[o, pl.ds(2 * k + i, 1), :] for o in range(count)] for i in range(2)]
        for g in range(groups):
            both = jnp.concatenate(
                [jnp.where(diagonal, choose(offs_wide[g], rows[i]), zero) for i in range(2)], axis=0
            )
            high, low = split_bf16(both)
            at = pl.multiple_of(k * 2 * SUB, 2 * SUB)
            big_ref[g, 0, pl.ds(at, 2 * SUB), :] = high
            big_ref[g, 1, pl.ds(at, 2 * SUB), :] = low
        return 0

    lax.fori_loop(0, levels // 2, one_pair, 0)
    for g in range(groups):
        ref, slot = place(g, groups, inner_ref, outer_ref)
        m_high = big_ref[g, 0]
        m_low = big_ref[g, 1]
        for i in range(parts):
            x_high, x_low = split_bf16(ref[slot, i])
            solved_ref[g, i] = (
                jnp.dot(m_high, x_high, preferred_element_type=F32)
                + jnp.dot(m_low, x_high, preferred_element_type=F32)
                + jnp.dot(m_high, x_low, preferred_element_type=F32)
            )


def unpack(ref, rows, count):
    a_side = ref[:rows, :]
    b_side = ref[rows : 2 * rows, :]
    base = 2 * rows
    b, e, l, a = [ref[base + c * count : base + (c + 1) * count, :] for c in range(4)]
    return a_side, b_side, b, e, l, a


def per_line(offs, table, parts):
    rows = [table[o : o + 1, :] for o in range(table.shape[0])]
    value = choose(offs, rows)
    return jnp.concatenate([value] * parts, axis=0)


def merged(bit, mine_ref, got_ref, offs, parts, count):
    lines = offs.shape[0]
    rows = parts * lines
    lower_is_mine = (lax.axis_index("depth") >> bit) % 2 == 0
    mine = unpack(mine_ref, rows, count)
    got = unpack(got_ref, rows, count)
    a_1, b_1, cb_1, ce_1, cl_1, ca_1 = [jnp.where(lower_is_mine, x, y) for x, y in zip(mine, got)]
    a_2, b_2, cb_2, ce_2, cl_2, ca_2 = [jnp.where(lower_is_mine, y, x) for x, y in zip(mine, got)]
    inverse = 1.0 / (ca_1 + cb_2)
    total = a_1 + b_2
    down = ce_1 * inverse
    up = cl_2 * inverse
    a_new = a_2 - per_line(offs, up, parts) * total
    b_new = b_1 - per_line(offs, down, parts) * total
    cb = cb_1 - down * cl_1
    ce = -down * ce_2
    cl = -up * cl_1
    ca = ca_2 - up * ce_2
    middle = per_line(offs, inverse, parts) * total
    return (a_new, b_new, cb, ce, cl, ca), (middle, cl_1 * inverse, ce_2 * inverse)


def store_saved(saved_ref, saved, count):
    middle, low, high = saved
    rows = middle.shape[0]
    saved_ref[:rows, :] = middle
    saved_ref[rows : rows + count, :] = low
    saved_ref[rows + count : rows + 2 * count, :] = high


def store_element(ref, element, count):
    rows = element[0].shape[0]
    ref[:rows, :] = element[0]
    ref[rows : 2 * rows, :] = element[1]
    for c in range(4):
        ref[2 * rows + c * count : 2 * rows + (c + 1) * count, :] = element[2 + c]


def merge_kernel(bit, parts, count, mine_ref, got_ref, offsb_ref, element_ref, saved_ref):
    element, saved = merged(bit, mine_ref, got_ref, offsb_ref[...], parts, count)
    store_element(element_ref, element, count)
    store_saved(saved_ref, saved, count)


def merge_last_kernel(bit, parts, count, mine_ref, got_ref, offsb_ref, token_ref, element_ref, saved_ref, send_ref):
    offs = offsb_ref[...]
    element, saved = merged(bit, mine_ref, got_ref, offs, parts, count)
    store_element(element_ref, element, count)
    store_saved(saved_ref, saved, count)
    a_side, b_side, cb, ce, cl, ca = element
    rows = a_side.shape[0]
    lower = (lax.axis_index("depth") >> (bit + 1)) == 0
    ratio = ce / ca
    send_ref[:rows, :] = jnp.where(lower, a_side, b_side - per_line(offs, ratio, parts) * a_side)
    send_ref[rows : rows + count, :] = jnp.where(lower, ca, cb - ratio * cl)


def solve_kernel(bits, parts, count, *refs):
    sent_ref, got_ref, element_ref, offsb_ref = refs[:4]
    saved_refs = refs[4 : 4 + bits]
    send_ref, keep_ref = refs[4 + bits :]
    offs = offsb_ref[...]
    rows = parts * offs.shape[0]
    rank = lax.axis_index("depth")
    pivot = sent_ref[rows : rows + count, :] + got_ref[rows : rows + count, :]
    shared = (sent_ref[:rows, :] + got_ref[:rows, :]) * per_line(offs, 1.0 / pivot, parts)
    a_side, _, _, _, cl, ca = unpack(element_ref, rows, count)
    inverse = 1.0 / ca
    top = per_line(offs, inverse, parts) * a_side - per_line(offs, cl * inverse, parts) * shared
    lower = (rank >> bits) == 0
    below = jnp.where(lower, jnp.zeros_like(shared), shared)
    above = jnp.where(lower, shared, top)
    for bit in reversed(range(bits)):
        saved_ref = saved_refs[bit]
        low = saved_ref[rows : rows + count, :]
        high = saved_ref[rows + count : rows + 2 * count, :]
        middle = saved_ref[:rows, :] - per_line(offs, low, parts) * below - per_line(offs, high, parts) * above
        lower = (rank >> bit) % 2 == 0
        if bit > 0:
            below, above = jnp.where(lower, below, middle), jnp.where(lower, middle, above)
        else:
            keep_ref[:rows, :] = jnp.where(lower, below, middle)
            keep_ref[rows:, :] = jnp.where(lower, middle, above)
            send_ref[:rows, :] = jnp.where(lower, middle, below)
            send_ref[rows:, :] = jnp.where(lower, above, middle)


def finish_kernel(step, solved_ref, own_ref, other_ref, offsb_ref, spikes_ref, out_ref, stage_ref, sems):
    parts, levels, lines, ny = out_ref.shape
    groups = lines // SUB
    half = ny // 2
    count = spikes_ref.shape[1]
    rows = parts * lines
    core = lax.axis_index("depth") % 2

    def ends(g):
        values = []
        for k in range(2):
            for i in range(parts):
                at = k * rows + i * lines + g * SUB
                own = own_ref[at : at + SUB, :]
                other = other_ref[at : at + SUB, :]
                values.append((jnp.where(core == 0, own, other), jnp.where(core == 0, other, own)))
        return values

    copies = []
    for c in range(levels // step):
        for g in range(groups):
            lane = slice(g * SUB, (g + 1) * SUB)
            offs = offsb_ref[lane, :]
            side = ends(g)

            def one_level(k, _):
                at = pl.multiple_of(k * SUB, SUB)
                low = choose(offs, [spikes_ref[0, o, pl.ds(k, 1), :] for o in range(count)])
                high = choose(offs, [spikes_ref[1, o, pl.ds(k, 1), :] for o in range(count)])
                for i in range(parts):
                    for h in range(2):
                        cut = slice(h * half, (h + 1) * half)
                        stage_ref[i, k, lane, cut] = (
                            solved_ref[g, i, pl.ds(at, SUB), cut] + low * side[i][h] + high * side[parts + i][h]
                        )
                return 0

            stop = (c + 1) * step
            last = stop == levels
            lax.fori_loop(c * step, stop - 1 if last else stop, one_level, 0, unroll=True)
            if last:
                for i in range(parts):
                    for h in range(2):
                        cut = slice(h * half, (h + 1) * half)
                        stage_ref[i, levels - 1, lane, cut] = side[parts + i][h]
        for i in range(parts):
            at = pl.ds(c * step, step)
            copy = pltpu.make_async_copy(stage_ref.at[i, at], out_ref.at[i, at], sems.at[c * parts + i])
            copy.start()
            copies.append(copy)
    for copy in copies:
        copy.wait()


def call(kernel, outs, args, scratch=(), specs=None, keep=True):
    put = [pltpu.with_memory_space_constraint(x, VMEM) for x in args] if specs is None else args
    return pl.pallas_call(
        kernel,
        out_shape=[VMEM(s, d) if keep else jax.ShapeDtypeStruct(s, d) for s, d in outs],
        in_specs=specs or [vmem_spec()] * len(args),
        out_specs=[vmem_spec() if keep else pl.BlockSpec(memory_space=pl.ANY)] * len(outs),
        scratch_shapes=list(scratch),
        compiler_params=pltpu.CompilerParams(vmem_limit_bytes=16 * 2**20),
    )(*put)


def body(fields, diffusivity, offsets, coupling, inverse):
    parts, levels, lines, ny = fields.shape
    count = inverse.shape[0]
    half = ny // 2
    groups = lines // SUB
    width = levels * SUB
    around = lax.axis_size("horiz")
    ranks = lax.axis_size("depth")
    bits = ranks.bit_length() - 1
    assert ranks == 1 << bits and bits >= 2 and half == LANE and groups >= 3

    def swap(x, bit):
        return lax.ppermute(x, "depth", [(i, i ^ (1 << bit)) for i in range(ranks)])

    anywhere = pl.BlockSpec(memory_space=pltpu.HBM)
    fields = pltpu.with_memory_space_constraint(fields, pltpu.HBM)
    diffusivity = pltpu.with_memory_space_constraint(diffusivity, pltpu.HBM)
    edge = ((parts, levels, ny), F32)
    first, last = call(
        outermost_kernel,
        [edge, edge],
        (fields,),
        scratch=[pltpu.VMEM((2, parts, levels, SUB, ny), F32), pltpu.SemaphoreType.DMA((2,))],
        specs=[anywhere],
    )
    west = lax.ppermute(last, "horiz", [(i, (i + 1) % around) for i in range(around)])
    east = lax.ppermute(first, "horiz", [(i, (i - 1) % around) for i in range(around)])

    rows = parts * lines
    chunks = levels // SUB
    table = ((2, count, levels, LANE), F32)
    fields_v, diff_v, offsb, spikes, k_rows, coefs, inner, sides = call(
        inner_kernel,
        [
            (fields.shape, F32),
            (diffusivity.shape, F32),
            ((lines, LANE), jnp.int32),
            table,
            table,
            ((6 * count, LANE), F32),
            ((groups - 2, parts, width, ny), F32),
            ((2, parts, groups - 2, SUB, ny), F32),
        ],
        (fields, diffusivity, offsets, coupling, inverse),
        scratch=[pltpu.SemaphoreType.DMA(((parts + 1) * chunks,))],
        specs=[anywhere, anywhere, pl.BlockSpec(memory_space=pltpu.SMEM), vmem_spec(), vmem_spec()],
    )
    element_shape = ((2 * rows + 4 * count, half), F32)
    saved_shape = ((rows + 2 * count, half), F32)
    outer, send, mine = call(
        edge_kernel,
        [((2, parts, width, ny), F32), element_shape, element_shape],
        (fields_v, diff_v, west, east, offsb, k_rows, coefs, sides),
        scratch=[pltpu.VMEM((2, parts, 2, SUB, ny), F32)],
    )
    got = swap(send, 0)
    saved = []
    for bit in range(bits - 1):
        if bit < bits - 2:
            mine, kept = call(
                functools.partial(merge_kernel, bit, parts, count),
                [element_shape, saved_shape],
                (mine, got, offsb),
            )
            got = swap(mine, bit + 1)
        if bit == 0:
            solved, token = call(
                block_kernel,
                [((groups, parts, width, ny), F32), ((SUB, LANE), F32)],
                (mine, inner, outer, offsb, inverse),
                scratch=[
                    pltpu.VMEM((count, levels, width), F32),
                    pltpu.VMEM((groups, 2, width, width), BF16),
                ],
            )
        if bit == bits - 2:
            mine, kept, send = call(
                functools.partial(merge_last_kernel, bit, parts, count),
                [element_shape, saved_shape, ((rows + count, half), F32)],
                (mine, got, offsb, token),
            )
            got = swap(send, bit + 1)
        saved.append(kept)
    pair = ((2 * rows, half), F32)
    theirs, own = call(
        functools.partial(solve_kernel, bits - 1, parts, count),
        [pair, pair],
        (send, got, mine, offsb, *saved),
    )
    other = swap(theirs, 0)
    (out,) = call(
        functools.partial(finish_kernel, SUB),
        [((parts, levels, lines, ny), F32)],
        (solved, own, other, offsb, spikes),
        scratch=[pltpu.VMEM((parts, levels, lines, ny), F32), pltpu.SemaphoreType.DMA((parts * chunks,))],
        keep=False,
    )
    return out


def solution(mesh):
    return jax.shard_map(
        body,
        mesh=mesh,
        in_specs=(
            P(None, "depth", "horiz", None),
            P("depth", "horiz", None),
            P("horiz"),
            P(None, "depth"),
            P(None, "depth", None),
        ),
        out_specs=P(None, "depth", "horiz", None),
        check_vma=False,
    )
```

time: 49.8 us -> 27.1 us (0.54)
  Pallas kernels: 24.7 us -> 10.6 us
  local copies, waits for them, and re-layouts: 4.69 us -> 0.01 us
  waiting for transfers between devices: 11.9 us -> 7.75 us
    pallas_call x6 -> x8, Pallas kernels: 24.7 us -> 10.6 us  [call(): pl.pallas_call(kernel, out_shape=[VMEM(s, d) if keep else jax.ShapeDtypeS...]
    unnamed x14 -> x6, local copies, waits for them, and re-layouts: 3.18 us -> 0.01 us
    ppermute x4, waiting for transfers between devices: 9.34 us -> 6.4 us  [swap(): return lax.ppermute(x, 'depth', [(i, i ^ 1 << bit) for i in range(ranks)])]
    slice x1 -> x0, local copies, waits for them, and re-layouts: 1.51 us -> none  [body(): east = lax.ppermute(fields[:, :, 0, :], 'horiz', backward)]
    ppermute x2, waiting for transfers between devices: 2.57 us -> 1.35 us  [the longest x1 1.34 us: body(): lax.ppermute(first, 'horiz', [(i, (i - 1) % around) for i in range(around)])]
  transfers between devices with their start and end apart: 6 -> 6, of which waited for: 6 -> 5; matrix products, arithmetic and copies ran while one was open for 0% -> 0% of each run, Pallas kernels for 5% -> 22%
where the time goes in v2:
time: 27.1 us; the launch traced here: 26.9 us
  Pallas kernels  10.6 us (39%)
  starting transfers between devices  8.48 us (31%)
  waiting for transfers between devices  7.75 us (29%)
    pallas_call x8, Pallas kernels, call(): pl.pallas_call(kernel, out_shape=[VMEM(s, d) if keep else jax.ShapeDtypeS...  10.6 us
    ppermute x4, waiting for transfers between devices, swap(): return lax.ppermute(x, 'depth', [(i, i ^ 1 << bit) for i in range(ranks)])  6.4 us
    ppermute x4, starting transfers between devices, swap(): return lax.ppermute(x, 'depth', [(i, i ^ 1 << bit) for i in range(ranks)])  4.44 us
    ppermute x1, starting transfers between devices, body(): lax.ppermute(last, 'horiz', [(i, (i + 1) % around) for i in range(around)])  3.02 us
    ppermute x1, waiting for transfers between devices, body(): lax.ppermute(first, 'horiz', [(i, (i - 1) % around) for i in range(around)])  1.34 us
    ppermute x1, starting transfers between devices, body(): lax.ppermute(first, 'horiz', [(i, (i - 1) % around) for i in range(around)])  1.02 us
  transfers between devices with their start and end apart: 6, of which 5 were waited for; matrix products, arithmetic and copies ran while one was open for 0% of the time, Pallas kernels for 22%

profile of v2, /device:TPU:0, one launch (start us, length us, event | category | flops | bytes accessed | tf_op | source)
XLA Modules:
  0.0 26.9 jit_solution(2599050030138352844)
XLA Ops:
  0.0 0.0 copy-start
  0.0 0.0 copy-start.1
  0.0 0.0 copy-start.2
  0.0 1.5 %shard_map.56 = (f32[3,32,256]{2,1,0:T(8,128)S(1)}, f32[3,32,256]{2,1,0:T(8,128)S(1)}) custom-call(f32[3,32,32,256]{3,2,1,0:T(8,128)} %fields_ref.1), custom_call_target="tpu_custom_call" | custom-call | tf_op jit(solution)/shard_map/pallas_call | solution.py:471
  1.5 3.0 %collective-permute-start = (f32[3,32,256]{2,1,0:T(8,128)S(1)}, f32[3,32,256]{2,1,0:T(8,128)S(1)}, u32[]{:S(2)}, u32[]{:S(2)}) collective-permute-start(f32[3,32,256]{2,1,0:T(8,128)S(1)} %get-tuple-element.29), channel_id=1, source_target_pairs={{0,8},{8,16},{16,24},{24,0},{1,9},{9,17},{17,25},{25,1},{2,10},{10... | collective-permute-start | bytes 294920 | tf_op jit(solution)/shard_map/ppermute | solution.py:506
  4.5 1.0 %collective-permute-start.1 = (f32[3,32,256]{2,1,0:T(8,128)S(1)}, f32[3,32,256]{2,1,0:T(8,128)S(1)}, u32[]{:S(2)}, u32[]{:S(2)}) collective-permute-start(f32[3,32,256]{2,1,0:T(8,128)S(1)} %get-tuple-element.30), channel_id=1, source_target_pairs={{0,24},{8,0},{16,8},{24,16},{1,25},{9,1},{17,9},{25,17},{2,26},{10... | collective-permute-start | bytes 294920 | tf_op jit(solution)/shard_map/ppermute | solution.py:507
  5.5 0.0 copy-done
  5.5 0.0 copy-done.1
  5.5 0.0 copy-done.2
  5.5 3.7 %shard_map.55 = (f32[3,32,32,256]{3,2,1,0:T(8,128)S(1)}, f32[32,32,256]{2,1,0:T(8,128)S(1)}, s32[32,128]{1,0:T(8,128)S(1)}, f32[2,4,32,128]{3,2,1,0:T(8,128)S(1)...) custom-call(f32[3,32,32,256]{3,2,1,0:T(8,128)} %fields_ref.1, ...), custom_call_target="tpu_custom_call" | custom-call | tf_op jit(solution)/shard_map/pallas_call | solution.py:471
  9.3 0.0 collective-permute-done.west_ref
  9.3 1.3 %collective-permute-done.1.east_ref = f32[3,32,256]{2,1,0:T(8,128)S(1)} collective-permute-done((f32[3,32,256]{2,1,0:T(8,128)S(1)}, f32[3,32,256]{2,1,0:T(8,128)S(1)}, u32[]{:S(2)}, u32[]{:S(2)}) %collective-permute-start.1) | collective-permute-done | bytes 98336 | tf_op jit(solution)/shard_map/ppermute | solution.py:507
  10.6 1.3 %shard_map.57 = (f32[2,3,256,256]{3,2,1,0:T(8,128)S(1)}, f32[208,128]{1,0:T(8,128)S(1)}, f32[208,128]{1,0:T(8,128)S(1)}) custom-call(f32[3,32,32,256]{3,2,1,0:T(8,128)S(1)} %get-tuple-element.27.fields_ref, f32[32,32,256]{2,1,0:T(8,128)S(1)} %get-tuple-element.28.diff_ref, f32[3,32,256]{2,1,0:T(8,128)S(1)} %collective-permute-done.west_ref, ...), custom_call_target="tpu_custom_call" | custom-call | tf_op jit(solution)/shard_map/pallas_call | solution.py:471
  11.9 0.1 collective-permute-start.2
  12.0 1.3 %collective-permute-done.2.got_ref = f32[208,128]{1,0:T(8,128)S(1)} collective-permute-done((f32[208,128]{1,0:T(8,128)S(1)}, f32[208,128]{1,0:T(8,128)S(1)}, u32[]{:S(2)}, u32[]{:S(2)}) %collective-permute-start.2) | collective-permute-done | bytes 106528 | tf_op jit(solution)/shard_map/ppermute | solution.py:493
  13.3 1.6 %collective-permute-start.3 = (f32[208,128]{1,0:T(8,128)S(1)}, f32[208,128]{1,0:T(8,128)S(1)}, u32[]{:S(2)}, u32[]{:S(2)}) collective-permute-start(f32[208,128]{1,0:T(8,128)S(1)} %get-tuple-element.37.after_ref.mine_ref), channel_id=1, source_target_pairs={{0,2},{1,3},{2,0},{3,1},{4,6},{5,7},{6,4},{7,5},{8,10},{9,11},{10,... | collective-permute-start | bytes 319496 | tf_op jit(solution)/shard_map/ppermute | solution.py:493
  15.0 2.1 %shard_map.59 = (f32[4,3,256,256]{3,2,1,0:T(8,128)S(1)}, f32[8,128]{1,0:T(8,128)S(1)}) custom-call(f32[208,128]{1,0:T(8,128)S(1)} %get-tuple-element.37.after_ref.mine_ref, f32[2,3,256,256]{3,2,1,0:T(8,128)S(1)} %get-tuple-element.38.inner_ref, f32[2,3,256,256]{3,2,1,0:T(8,128)S(1)} %get-tuple-element.39.outer_ref, ...), custom_call_target="tpu_custom_call" | custom-call | tf_op jit(solution)/shard_map/pallas_call | solution.py:471
  17.0 1.4 %collective-permute-done.3.got_ref = f32[208,128]{1,0:T(8,128)S(1)} collective-permute-done((f32[208,128]{1,0:T(8,128)S(1)}, f32[208,128]{1,0:T(8,128)S(1)}, u32[]{:S(2)}, u32[]{:S(2)}) %collective-permute-start.3) | collective-permute-done | bytes 106528 | tf_op jit(solution)/shard_map/ppermute | solution.py:493
  18.4 0.1 shard_map.60
  18.5 2.7 %collective-permute-start.4 = (f32[100,128]{1,0:T(8,128)S(1)}, f32[100,128]{1,0:T(8,128)S(1)}, u32[]{:S(2)}, u32[]{:S(2)}) collective-permute-start(f32[100,128]{1,0:T(8,128)S(1)} %get-tuple-element.42.refs_0_), channel_id=1, source_target_pairs={{0,4},{1,5},{2,6},{3,7},{4,0},{5,1},{6,2},{7,3},{8,12},{9,13},{10,... | collective-permute-start | bytes 153608 | tf_op jit(solution)/shard_map/ppermute | solution.py:493
  21.1 2.4 %collective-permute-done.4.refs_1_ = f32[100,128]{1,0:T(8,128)S(1)} collective-permute-done((f32[100,128]{1,0:T(8,128)S(1)}, f32[100,128]{1,0:T(8,128)S(1)}, u32[]{:S(2)}, u32[]{:S(2)}) %collective-permute-start.4) | collective-permute-done | bytes 51232 | tf_op jit(solution)/shard_map/ppermute | solution.py:493
  23.6 0.1 shard_map.61
  23.6 0.1 collective-permute-start.5
  23.7 1.3 %collective-permute-done.5.other_ref = f32[192,128]{1,0:T(8,128)S(1)} collective-permute-done((f32[192,128]{1,0:T(8,128)S(1)}, f32[192,128]{1,0:T(8,128)S(1)}, u32[]{:S(2)}, u32[]{:S(2)}) %collective-permute-start.5) | collective-permute-done | bytes 98336 | tf_op jit(solution)/shard_map/ppermute | solution.py:493
  25.0 1.9 %shard_map.62 = f32[3,32,32,256]{3,2,1,0:T(8,128)} custom-call(f32[4,3,256,256]{3,2,1,0:T(8,128)S(1)} %get-tuple-element.40.solved_ref, f32[192,128]{1,0:T(8,128)S(1)} %get-tuple-element.46.own_ref, f32[192,128]{1,0:T(8,128)S(1)} %collective-permute-done.5.other_ref, s32[32,128]{1,0:T(8,128)S(1)} %get-tuple-element.31.offsb_ref.refs_3_, ...), custom_call_target="tpu_custom_call" | custom-call | tf_op jit(solution)/shard_map/pallas_call | solution.py:471
  (1 shorter events, 0.0 us)
Async XLA Ops:
  0.0 5.5 %copy-start = (f32[4,32,32]{2,1,0:T(8,128)S(1)}, f32[4,32,32]{2,1,0:T(8,128)}, u32[]{:S(2)}) copy-start(f32[4,32,32]{2,1,0:T(8,128)} %inverse_ref.3) | copy-start | bytes 49156
  0.0 5.5 %copy-start.1 = (f32[4,32]{1,0:T(4,128)S(1)}, f32[4,32]{1,0:T(4,128)}, u32[]{:S(2)}) copy-start(f32[4,32]{1,0:T(4,128)} %coupling_ref.1) | copy-start | bytes 1540
  0.0 5.5 %copy-start.2 = (s32[32]{0:T(128)S(1)}, s32[32]{0:T(128)}, u32[]{:S(2)}) copy-start(s32[32]{0:T(128)} %offs_ref.1) | copy-start | bytes 388
  1.5 7.8 %collective-permute-start = (f32[3,32,256]{2,1,0:T(8,128)S(1)}, f32[3,32,256]{2,1,0:T(8,128)S(1)}, u32[]{:S(2)}, u32[]{:S(2)}) collective-permute-start(f32[3,32,256]{2,1,0:T(8,128)S(1)} %get-tuple-element.29), channel_id=1, source_target_pairs={{0,8},{8,16},{16,24},{24,0},{1,9},{9,17},{17,25},{25,1},{2,10},{10... | collective-permute-start | bytes 294920 | tf_op jit(solution)/shard_map/ppermute | solution.py:506
  4.5 6.1 %collective-permute-start.1 = (f32[3,32,256]{2,1,0:T(8,128)S(1)}, f32[3,32,256]{2,1,0:T(8,128)S(1)}, u32[]{:S(2)}, u32[]{:S(2)}) collective-permute-start(f32[3,32,256]{2,1,0:T(8,128)S(1)} %get-tuple-element.30), channel_id=1, source_target_pairs={{0,24},{8,0},{16,8},{24,16},{1,25},{9,1},{17,9},{25,17},{2,26},{10... | collective-permute-start | bytes 294920 | tf_op jit(solution)/shard_map/ppermute | solution.py:507
  11.9 1.4 %collective-permute-start.2 = (f32[208,128]{1,0:T(8,128)S(1)}, f32[208,128]{1,0:T(8,128)S(1)}, u32[]{:S(2)}, u32[]{:S(2)}) collective-permute-start(f32[208,128]{1,0:T(8,128)S(1)} %get-tuple-element.36), channel_id=1, source_target_pairs={{0,1},{1,0},{2,3},{3,2},{4,5},{5,4},{6,7},{7,6},{8,9},{9,8},{10,11... | collective-permute-start | bytes 319496 | tf_op jit(solution)/shard_map/ppermute | solution.py:493
  13.3 5.1 %collective-permute-start.3 = (f32[208,128]{1,0:T(8,128)S(1)}, f32[208,128]{1,0:T(8,128)S(1)}, u32[]{:S(2)}, u32[]{:S(2)}) collective-permute-start(f32[208,128]{1,0:T(8,128)S(1)} %get-tuple-element.37.after_ref.mine_ref), channel_id=1, source_target_pairs={{0,2},{1,3},{2,0},{3,1},{4,6},{5,7},{6,4},{7,5},{8,10},{9,11},{10,... | collective-permute-start | bytes 319496 | tf_op jit(solution)/shard_map/ppermute | solution.py:493
  18.5 5.1 %collective-permute-start.4 = (f32[100,128]{1,0:T(8,128)S(1)}, f32[100,128]{1,0:T(8,128)S(1)}, u32[]{:S(2)}, u32[]{:S(2)}) collective-permute-start(f32[100,128]{1,0:T(8,128)S(1)} %get-tuple-element.42.refs_0_), channel_id=1, source_target_pairs={{0,4},{1,5},{2,6},{3,7},{4,0},{5,1},{6,2},{7,3},{8,12},{9,13},{10,... | collective-permute-start | bytes 153608 | tf_op jit(solution)/shard_map/ppermute | solution.py:493
  23.6 1.4 %collective-permute-start.5 = (f32[192,128]{1,0:T(8,128)S(1)}, f32[192,128]{1,0:T(8,128)S(1)}, u32[]{:S(2)}, u32[]{:S(2)}) collective-permute-start(f32[192,128]{1,0:T(8,128)S(1)} %get-tuple-element.47), channel_id=1, source_target_pairs={{0,1},{1,0},{2,3},{3,2},{4,5},{5,4},{6,7},{7,6},{8,9},{9,8},{10,11... | collective-permute-start | bytes 294920 | tf_op jit(solution)/shard_map/ppermute | solution.py:493

commit v3 on v2

--- a/solution.py
+++ b/solution.py
@@ -32,23 +32,58 @@
     return high, low
 
 
-def outermost_kernel(fields_ref, first_ref, last_ref, stage_ref, sems):
+def outermost_kernel(
+    fields_ref,
+    diff_ref,
+    offs_hbm,
+    coupling_hbm,
+    inverse_hbm,
+    side_ref,
+    far_ref,
+    diff_rows_ref,
+    offs_ref,
+    coupling_ref,
+    inverse_ref,
+    stage_ref,
+    diff_stage_ref,
+    sems,
+):
     parts, levels, lines, ny = fields_ref.shape
+    even = lax.axis_index("horiz") % 2 == 0
     copies = []
-    for e, start in enumerate((0, lines - SUB)):
-        copy = pltpu.make_async_copy(fields_ref.at[:, :, pl.ds(start, SUB), :], stage_ref.at[e], sems.at[e])
+    for e, line in enumerate((0, lines - 1)):
+        copy = pltpu.make_async_copy(fields_ref.at[:, :, pl.ds(line, 1), :], stage_ref.at[e], sems.at[e])
         copy.start()
         copies.append(copy)
+        copy = pltpu.make_async_copy(diff_ref.at[:, pl.ds(line, 1), :], diff_stage_ref.at[e], sems.at[5 + e])
+        copy.start()
+        copies.append(copy)
+    small = ((offs_hbm, offs_ref), (coupling_hbm, coupling_ref), (inverse_hbm, inverse_ref))
+    for n, (source, target) in enumerate(small):
+        copy = pltpu.make_async_copy(source, target, sems.at[2 + n])
+        copy.start()
+        copies.append(copy)
+    for copy in copies:
+        copy.wait()
+    for i in range(parts):
+        for c in range(levels // SUB):
+            at = slice(c * SUB, (c + 1) * SUB)
+            first, last = [gather_rows(lambda k: stage_ref[e, i, k, 0:1, :], c, ny) for e in range(2)]
+            side_ref[i, at, :] = jnp.where(even, last, first)
+            far_ref[i, at, :] = jnp.where(even, first, last)
+    for e in range(2):
+        for c in range(levels // SUB):
+            diff_rows_ref[e, c * SUB : (c + 1) * SUB, :] = gather_rows(
+                lambda k: diff_stage_ref[e, k, 0:1, :], c, ny
+            )
+
+
+def gather_rows(row_at, c, ny):
     sub = lax.broadcasted_iota(jnp.int32, (SUB, ny), 0)
-    for e, (line, ref) in enumerate(((0, first_ref), (SUB - 1, last_ref))):
-        copies[e].wait()
-        for i in range(parts):
-            for c in range(levels // SUB):
-                value = jnp.zeros((SUB, ny), F32)
-                for t in range(SUB):
-                    row = stage_ref[e, i, c * SUB + t, line : line + 1, :]
-                    value = jnp.where(sub == t, jnp.broadcast_to(row, value.shape), value)
-                ref[i, c * SUB : (c + 1) * SUB, :] = value
+    value = jnp.zeros((SUB, ny), F32)
+    for t in range(SUB):
+        value = jnp.where(sub == t, jnp.broadcast_to(row_at(c * SUB + t), value.shape), value)
+    return value
 
 
 def fill_tables(offs_ref, coupling_ref, inverse_ref, offsb_ref, spikes_ref, rows_ref, coefs_ref):
@@ -56,12 +91,11 @@
     lines = offsb_ref.shape[0]
     rank = lax.axis_index("depth")
 
-    sub = lax.broadcasted_iota(jnp.int32, (SUB, LANE), 0)
-    for g in range(lines // SUB):
-        value = jnp.zeros((SUB, LANE), jnp.int32)
-        for j in range(SUB):
-            value = jnp.where(sub == j, offs_ref[g * SUB + j], value)
-        offsb_ref[g * SUB : (g + 1) * SUB, :] = value
+    square = (lines, lines)
+    own = lax.broadcasted_iota(jnp.int32, square, 0) == lax.broadcasted_iota(jnp.int32, square, 1)
+    row = jnp.broadcast_to(offs_ref[...].astype(F32), square)
+    column = jnp.sum(jnp.where(own, row, jnp.zeros_like(row)), axis=1, keepdims=True)
+    offsb_ref[...] = jnp.broadcast_to(column, (lines, LANE)).astype(jnp.int32)
 
     eye = lax.broadcasted_iota(jnp.int32, (levels, levels), 0) == lax.broadcasted_iota(
         jnp.int32, (levels, levels), 1
@@ -86,9 +120,7 @@
             coefs_ref[c * count + o : c * count + o + 1, :] = row
 
 
-def force_group(
-    g, slot, stages, fields_ref, diff_ref, west_ref, east_ref, offsb_ref, rows_ref, coefs_ref, forcing_ref, sides_ref
-):
+def force_group(g, fields_ref, diff_ref, offsb_ref, rows_ref, coefs_ref, forcing_ref, sides_ref):
     parts, levels, lines, ny = fields_ref.shape
     groups = lines // SUB
     half = ny // 2
@@ -108,11 +140,11 @@
             if g > 0:
                 row_w = fields_ref[i, k, first - 1 : first, :]
             else:
-                row_w = west_ref[i, pl.ds(k, 1), :]
+                row_w = jnp.zeros((1, ny), F32)
             if g < groups - 1:
                 row_e = fields_ref[i, k, first + SUB : first + SUB + 1, :]
             else:
-                row_e = east_ref[i, pl.ds(k, 1), :]
+                row_e = jnp.zeros((1, ny), F32)
             east = jnp.where(sub == SUB - 1, jnp.broadcast_to(row_e, c.shape), pltpu.roll(c, SUB - 1, 0))
             west = jnp.where(sub == 0, jnp.broadcast_to(row_w, c.shape), pltpu.roll(c, 1, 0))
             centre.append(c)
@@ -131,136 +163,105 @@
         bottom = choose(offs, [rows_ref[1, o, pl.ds(k, 1), :] for o in range(count)])
         new = []
         for i in range(parts):
-            forcing_ref[slot, i, pl.ds(at, SUB), :] = out[i]
+            forcing_ref[g, i, pl.ds(at, SUB), :] = out[i]
             for h in range(2):
                 piece = out[i][:, h * half : (h + 1) * half]
                 at_0, at_1 = sums[2 * (i * 2 + h)], sums[2 * (i * 2 + h) + 1]
                 new += [at_0 + top * piece, at_1 + bottom * piece]
         return tuple(new)
 
-    sums = tuple(jnp.zeros((SUB, half), F32) for _ in range(4 * parts))
-    step = levels // len(stages)
-    for c, wait in enumerate(stages):
-        wait()
-        sums = lax.fori_loop(c * step, (c + 1) * step, one_level, sums, unroll=step)
-    for i in range(parts):
-        for h in range(2):
-            cut = slice(h * half, (h + 1) * half)
-            last = forcing_ref[slot, i, (levels - 1) * SUB :, cut]
-            sides_ref[0, i, slot, :, cut] = last + gate * sums[2 * (i * 2 + h) + 1]
-            sides_ref[1, i, slot, :, cut] = face * sums[2 * (i * 2 + h)]
-
-
-def nothing():
-    pass
+    def close(sums):
+        for i in range(parts):
+            for h in range(2):
+                cut = slice(h * half, (h + 1) * half)
+                last = forcing_ref[g, i, (levels - 1) * SUB :, cut]
+                at = i * lines + first
+                sides_ref[at : at + SUB, cut] = last + gate * sums[2 * (i * 2 + h) + 1]
+                at += parts * lines
+                sides_ref[at : at + SUB, cut] = face * sums[2 * (i * 2 + h)]
+
+    return one_level, tuple(jnp.zeros((SUB, half), F32) for _ in range(4 * parts)), close
+
+
+def run_groups(groups, levels):
+    for one_level, sums, close in groups:
+        close(lax.fori_loop(0, levels, one_level, sums, unroll=SUB))
 
 
 def inner_kernel(
-    fields_hbm,
-    diff_hbm,
+    fields_ref,
+    diff_ref,
     offs_ref,
     coupling_ref,
     inverse_ref,
-    fields_ref,
-    diff_ref,
     offsb_ref,
     spikes_ref,
     rows_ref,
     coefs_ref,
     forcing_ref,
     sides_ref,
-    sems,
 ):
-    parts, levels, lines, _ = fields_ref.shape
-    groups = lines // SUB
-    chunks = sems.shape[0] // (parts + 1)
-    step = levels // chunks
-    waits = []
-    for c in range(chunks):
-        at = pl.ds(c * step, step)
-        copies = [
-            pltpu.make_async_copy(fields_hbm.at[i, at], fields_ref.at[i, at], sems.at[c * (parts + 1) + i])
-            for i in range(parts)
-        ]
-        copies.append(pltpu.make_async_copy(diff_hbm.at[at], diff_ref.at[at], sems.at[c * (parts + 1) + parts]))
-        for copy in copies:
-            copy.start()
-        waits.append(lambda copies=copies: [copy.wait() for copy in copies])
+    levels, lines, _ = diff_ref.shape
     fill_tables(offs_ref, coupling_ref, inverse_ref, offsb_ref, spikes_ref, rows_ref, coefs_ref)
-    for slot, g in enumerate(range(1, groups - 1)):
-        force_group(
-            g,
-            slot,
-            waits if slot == 0 else [nothing] * chunks,
-            fields_ref,
-            diff_ref,
-            None,
-            None,
-            offsb_ref,
-            rows_ref,
-            coefs_ref,
-            forcing_ref,
-            sides_ref,
-        )
-
-
-def edge_kernel(
-    fields_ref,
-    diff_ref,
-    west_ref,
-    east_ref,
-    offsb_ref,
-    rows_ref,
-    coefs_ref,
-    inner_ref,
-    forcing_ref,
-    send_ref,
-    keep_ref,
-    sides_ref,
+    work = [
+        force_group(g, fields_ref, diff_ref, offsb_ref, rows_ref, coefs_ref, forcing_ref, sides_ref)
+        for g in range(lines // SUB)
+    ]
+    run_groups(work, levels)
+
+
+def correct_kernel(
+    side_ref, far_ref, sides_ref, diff_rows_ref, offsb_ref, rows_ref, coefs_ref, extra_ref, send_ref, keep_ref
 ):
-    parts, levels, lines, ny = fields_ref.shape
-    groups = lines // SUB
+    parts, levels, ny = side_ref.shape
+    lines = offsb_ref.shape[0]
     half = ny // 2
     count = rows_ref.shape[1]
     core = lax.axis_index("depth") % 2
-    for slot, g in enumerate((0, groups - 1)):
-        force_group(
-            g,
-            slot,
-            [nothing] * (levels // SUB),
-            fields_ref,
-            diff_ref,
-            west_ref,
-            east_ref,
-            offsb_ref,
-            rows_ref,
-            coefs_ref,
-            forcing_ref,
-            sides_ref,
-        )
-    for g in range(groups):
-        ref, slot = place(g, groups, inner_ref, sides_ref)
-        for i in range(parts):
-            for k in range(2):
-                at = (k * parts + i) * lines + g * SUB
-                left, right = ref[k, i, slot, :, :half], ref[k, i, slot, :, half:]
-                keep_ref[at : at + SUB, :] = jnp.where(core == 0, left, right)
-                send_ref[at : at + SUB, :] = jnp.where(core == 0, right, left)
-
+    even = lax.axis_index("horiz") % 2 == 0
+    sub = lax.broadcasted_iota(jnp.int32, (SUB, half), 0)
+    scale = 0.5 * wave_gain
     base = 2 * parts * lines
+    for at in range(0, base, SUB):
+        left, right = sides_ref[at : at + SUB, :half], sides_ref[at : at + SUB, half:]
+        keep_ref[at : at + SUB, :] = jnp.where(core == 0, left, right)
+        send_ref[at : at + SUB, :] = jnp.where(core == 0, right, left)
     send_ref[base : base + 4 * count, :] = coefs_ref[: 4 * count, :]
     keep_ref[base : base + 4 * count, :] = coefs_ref[: 4 * count, :]
 
-
-def place(g, groups, inner_ref, outer_ref):
-    if g == 0:
-        return outer_ref, 0
-    if g == groups - 1:
-        return outer_ref, 1
-    return inner_ref, g - 1
-
-
-def block_kernel(after_ref, inner_ref, outer_ref, offsb_ref, inverse_ref, solved_ref, token_ref, wide_ref, big_ref):
+    for e, (line, sign) in enumerate(((0, scale), (lines - 1, -scale))):
+        near, other = (far_ref, side_ref) if e == 0 else (side_ref, far_ref)
+        halo = [jnp.where(even, near[i], other[i]) for i in range(parts)]
+        d = diff_rows_ref[e]
+        extra = (d * halo[0] + sign * halo[2], d * halo[1], d * halo[2] + sign * halo[0])
+        offs = jnp.broadcast_to(offsb_ref[line : line + 1, :], (levels, half))
+        one = offs[:1]
+        gate = choose(one, [coefs_ref[4 * count + o : 4 * count + o + 1, :] for o in range(count)])
+        face = choose(one, [coefs_ref[5 * count + o : 5 * count + o + 1, :] for o in range(count)])
+        top = choose(offs, [rows_ref[0, o] for o in range(count)])
+        bottom = choose(offs, [rows_ref[1, o] for o in range(count)])
+        group, place = line // SUB * SUB, line % SUB
+        for i in range(parts):
+            extra_ref[e, i] = extra[i]
+            more = []
+            for h in range(2):
+                piece = extra[i][:, h * half : (h + 1) * half]
+                a_side = piece[levels - 1 :, :] + gate * jnp.sum(bottom * piece, axis=0, keepdims=True)
+                more.append((a_side, face * jnp.sum(top * piece, axis=0, keepdims=True)))
+            for k in range(2):
+                left, right = more[0][k], more[1][k]
+                at = (k * parts + i) * lines + group
+                zero = jnp.zeros((SUB, half), F32)
+                for ref, row in (
+                    (keep_ref, jnp.where(core == 0, left, right)),
+                    (send_ref, jnp.where(core == 0, right, left)),
+                ):
+                    ref[at : at + SUB, :] += jnp.where(sub == place, jnp.broadcast_to(row, zero.shape), zero)
+
+
+def block_kernel(
+    after_ref, forcing_ref, extra_ref, offsb_ref, inverse_ref, solved_ref, token_ref, wide_ref, big_ref, work_ref
+):
     count, levels, _ = inverse_ref.shape
     groups, parts, width, ny = solved_ref.shape
     token_ref[...] = after_ref[:SUB, :]
@@ -298,12 +299,22 @@
         return 0
 
     lax.fori_loop(0, levels // 2, one_pair, 0)
+    here = lax.broadcasted_iota(jnp.int32, (SUB, ny), 0)
+    nought = jnp.zeros((SUB, ny), F32)
     for g in range(groups):
-        ref, slot = place(g, groups, inner_ref, outer_ref)
         m_high = big_ref[g, 0]
         m_low = big_ref[g, 1]
         for i in range(parts):
-            x_high, x_low = split_bf16(ref[slot, i])
+            if 0 < g < groups - 1:
+                x = forcing_ref[g, i]
+            else:
+                e, line = (0, 0) if g == 0 else (1, SUB - 1)
+                for k in range(levels):
+                    at = slice(k * SUB, (k + 1) * SUB)
+                    row = jnp.broadcast_to(extra_ref[e, i, k : k + 1, :], (SUB, ny))
+                    work_ref[e, i, at, :] = forcing_ref[g, i, at, :] + jnp.where(here == line, row, nought)
+                x = work_ref[e, i]
+            x_high, x_low = split_bf16(x)
             solved_ref[g, i] = (
                 jnp.dot(m_high, x_high, preferred_element_type=F32)
                 + jnp.dot(m_low, x_high, preferred_element_type=F32)
@@ -412,68 +423,76 @@
             send_ref[rows:, :] = jnp.where(lower, above, middle)
 
 
-def finish_kernel(step, solved_ref, own_ref, other_ref, offsb_ref, spikes_ref, out_ref, stage_ref, sems):
+def finish_kernel(step, own, solved_ref, ends_ref, offsb_ref, spikes_ref, *refs):
+    out_ref, stage_ref, sems = refs[-3:]
     parts, levels, lines, ny = out_ref.shape
     groups = lines // SUB
     half = ny // 2
     count = spikes_ref.shape[1]
     rows = parts * lines
     core = lax.axis_index("depth") % 2
-
-    def ends(g):
-        values = []
-        for k in range(2):
-            for i in range(parts):
-                at = k * rows + i * lines + g * SUB
-                own = own_ref[at : at + SUB, :]
-                other = other_ref[at : at + SUB, :]
-                values.append((jnp.where(core == 0, own, other), jnp.where(core == 0, other, own)))
-        return values
+    cut = pl.ds(pl.multiple_of((core if own else 1 - core) * half, half), half)
 
     copies = []
     for c in range(levels // step):
         for g in range(groups):
             lane = slice(g * SUB, (g + 1) * SUB)
             offs = offsb_ref[lane, :]
-            side = ends(g)
-
-            def one_level(k, _):
-                at = pl.multiple_of(k * SUB, SUB)
-                low = choose(offs, [spikes_ref[0, o, pl.ds(k, 1), :] for o in range(count)])
-                high = choose(offs, [spikes_ref[1, o, pl.ds(k, 1), :] for o in range(count)])
+            side = [
+                [ends_ref[k * rows + i * lines + g * SUB : k * rows + i * lines + (g + 1) * SUB, :] for i in range(parts)]
+                for k in range(2)
+            ]
+            for k in range(c * step, (c + 1) * step):
+                if k == levels - 1:
+                    for i in range(parts):
+                        stage_ref[i, k, lane, :] = side[1][i]
+                    continue
+                low = choose(offs, [spikes_ref[0, o, k : k + 1, :] for o in range(count)])
+                high = choose(offs, [spikes_ref[1, o, k : k + 1, :] for o in range(count)])
                 for i in range(parts):
-                    for h in range(2):
-                        cut = slice(h * half, (h + 1) * half)
-                        stage_ref[i, k, lane, cut] = (
-                            solved_ref[g, i, pl.ds(at, SUB), cut] + low * side[i][h] + high * side[parts + i][h]
-                        )
-                return 0
-
-            stop = (c + 1) * step
-            last = stop == levels
-            lax.fori_loop(c * step, stop - 1 if last else stop, one_level, 0, unroll=True)
-            if last:
-                for i in range(parts):
-                    for h in range(2):
-                        cut = slice(h * half, (h + 1) * half)
-                        stage_ref[i, levels - 1, lane, cut] = side[parts + i][h]
+                    value = solved_ref[g, i, k * SUB : (k + 1) * SUB, cut]
+                    stage_ref[i, k, lane, :] = value + low * side[0][i] + high * side[1][i]
         for i in range(parts):
             at = pl.ds(c * step, step)
-            copy = pltpu.make_async_copy(stage_ref.at[i, at], out_ref.at[i, at], sems.at[c * parts + i])
+            copy = pltpu.make_async_copy(stage_ref.at[i, at], out_ref.at[i, at, :, cut], sems.at[c * parts + i])
             copy.start()
             copies.append(copy)
     for copy in copies:
         copy.wait()
 
 
-def call(kernel, outs, args, scratch=(), specs=None, keep=True):
+def call(kernel, outs, args, scratch=(), specs=None, **options):
     put = [pltpu.with_memory_space_constraint(x, VMEM) for x in args] if specs is None else args
     return pl.pallas_call(
         kernel,
-        out_shape=[VMEM(s, d) if keep else jax.ShapeDtypeStruct(s, d) for s, d in outs],
+        out_shape=[VMEM(s, d) for s, d in outs],
         in_specs=specs or [vmem_spec()] * len(args),
-        out_specs=[vmem_spec() if keep else pl.BlockSpec(memory_space=pl.ANY)] * len(outs),
+        out_specs=[vmem_spec()] * len(outs),
         scratch_shapes=list(scratch),
+        compiler_params=pltpu.CompilerParams(vmem_limit_bytes=16 * 2**20),
+    )(*put)
+
+
+def finish(own, out_shape, args, before=None):
+    step = SUB
+    parts, levels, lines, ny = out_shape
+    put = [pltpu.with_memory_space_constraint(x, VMEM) for x in args]
+    specs = [vmem_spec()] * len(args)
+    aliases = {}
+    if before is not None:
+        put.append(pltpu.with_memory_space_constraint(before, pltpu.HBM))
+        specs.append(pl.BlockSpec(memory_space=pltpu.HBM))
+        aliases = {len(args): 0}
+    return pl.pallas_call(
+        functools.partial(finish_kernel, step, own),
+        out_shape=pltpu.HBM(out_shape, F32),
+        in_specs=specs,
+        out_specs=pl.BlockSpec(memory_space=pltpu.HBM),
+        scratch_shapes=[
+            pltpu.VMEM((parts, levels, lines, ny // 2), F32),
+            pltpu.SemaphoreType.DMA((parts * (levels // step),)),
+        ],
+        input_output_aliases=aliases,
         compiler_params=pltpu.CompilerParams(vmem_limit_bytes=16 * 2**20),
     )(*put)
 
@@ -487,51 +506,49 @@
     around = lax.axis_size("horiz")
     ranks = lax.axis_size("depth")
     bits = ranks.bit_length() - 1
-    assert ranks == 1 << bits and bits >= 2 and half == LANE and groups >= 3
+    assert ranks == 1 << bits and bits >= 2 and around % 2 == 0 and half == LANE and groups >= 2
 
     def swap(x, bit):
         return lax.ppermute(x, "depth", [(i, i ^ (1 << bit)) for i in range(ranks)])
 
-    anywhere = pl.BlockSpec(memory_space=pltpu.HBM)
-    fields = pltpu.with_memory_space_constraint(fields, pltpu.HBM)
-    diffusivity = pltpu.with_memory_space_constraint(diffusivity, pltpu.HBM)
+    in_hbm = pl.BlockSpec(memory_space=pltpu.HBM)
     edge = ((parts, levels, ny), F32)
-    first, last = call(
+    offsets = offsets.reshape(1, lines)
+    to_side, to_far, diff_rows, offsets, coupling, inverse = call(
         outermost_kernel,
-        [edge, edge],
-        (fields,),
-        scratch=[pltpu.VMEM((2, parts, levels, SUB, ny), F32), pltpu.SemaphoreType.DMA((2,))],
-        specs=[anywhere],
+        [edge, edge, ((2, levels, ny), F32), (offsets.shape, jnp.int32), (coupling.shape, F32), (inverse.shape, F32)],
+        [pltpu.with_memory_space_constraint(x, pltpu.HBM) for x in (fields, diffusivity, offsets, coupling, inverse)],
+        scratch=[
+            pltpu.VMEM((2, parts, levels, 1, ny), F32),
+            pltpu.VMEM((2, levels, 1, ny), F32),
+            pltpu.SemaphoreType.DMA((7,)),
+        ],
+        specs=[in_hbm] * 5,
     )
-    west = lax.ppermute(last, "horiz", [(i, (i + 1) % around) for i in range(around)])
-    east = lax.ppermute(first, "horiz", [(i, (i - 1) % around) for i in range(around)])
+    far = lax.ppermute(to_far, "horiz", [(i, (i + 2 * (i % 2) - 1) % around) for i in range(around)])
+    side = lax.ppermute(to_side, "horiz", [(i, (i + 1 - 2 * (i % 2)) % around) for i in range(around)])
 
     rows = parts * lines
-    chunks = levels // SUB
     table = ((2, count, levels, LANE), F32)
-    fields_v, diff_v, offsb, spikes, k_rows, coefs, inner, sides = call(
+    offsb, spikes, k_rows, coefs, forcing, sides = call(
         inner_kernel,
         [
-            (fields.shape, F32),
-            (diffusivity.shape, F32),
             ((lines, LANE), jnp.int32),
             table,
             table,
             ((6 * count, LANE), F32),
-            ((groups - 2, parts, width, ny), F32),
-            ((2, parts, groups - 2, SUB, ny), F32),
+            ((groups, parts, width, ny), F32),
+            ((2 * rows, ny), F32),
         ],
         (fields, diffusivity, offsets, coupling, inverse),
-        scratch=[pltpu.SemaphoreType.DMA(((parts + 1) * chunks,))],
-        specs=[anywhere, anywhere, pl.BlockSpec(memory_space=pltpu.SMEM), vmem_spec(), vmem_spec()],
+        specs=[vmem_spec()] * 5,
     )
     element_shape = ((2 * rows + 4 * count, half), F32)
     saved_shape = ((rows + 2 * count, half), F32)
-    outer, send, mine = call(
-        edge_kernel,
-        [((2, parts, width, ny), F32), element_shape, element_shape],
-        (fields_v, diff_v, west, east, offsb, k_rows, coefs, sides),
-        scratch=[pltpu.VMEM((2, parts, 2, SUB, ny), F32)],
+    extra, send, mine = call(
+        correct_kernel,
+        [((2, parts, levels, ny), F32), element_shape, element_shape],
+        (side, far, sides, diff_rows, offsb, k_rows, coefs),
     )
     got = swap(send, 0)
     saved = []
@@ -547,10 +564,11 @@
             solved, token = call(
                 block_kernel,
                 [((groups, parts, width, ny), F32), ((SUB, LANE), F32)],
-                (mine, inner, outer, offsb, inverse),
+                (mine, forcing, extra, offsb, inverse),
                 scratch=[
                     pltpu.VMEM((count, levels, width), F32),
                     pltpu.VMEM((groups, 2, width, width), BF16),
+                    pltpu.VMEM((2, parts, width, ny), F32),
                 ],
             )
         if bit == bits - 2:
@@ -568,14 +586,8 @@
         (send, got, mine, offsb, *saved),
     )
     other = swap(theirs, 0)
-    (out,) = call(
-        functools.partial(finish_kernel, SUB),
-        [((parts, levels, lines, ny), F32)],
-        (solved, own, other, offsb, spikes),
-        scratch=[pltpu.VMEM((parts, levels, lines, ny), F32), pltpu.SemaphoreType.DMA((parts * chunks,))],
-        keep=False,
-    )
-    return out
+    half_out = finish(True, (parts, levels, lines, ny), (solved, own, offsb, spikes))
+    return finish(False, (parts, levels, lines, ny), (solved, other, offsb, spikes), half_out)
 
 
 def solution(mesh):

time: 27.1 us -> 25.4 us (0.937)
  waiting for transfers between devices: 7.75 us -> 6.23 us
  Pallas kernels: 10.6 us -> 9.94 us
  starting transfers between devices: 8.48 us -> 8.96 us
    ppermute x4, waiting for transfers between devices: 6.4 us -> 5.03 us  [swap(): return lax.ppermute(x, 'depth', [(i, i ^ 1 << bit) for i in range(ranks)])]
    pallas_call x8 -> x9, Pallas kernels: 10.6 us -> 9.94 us  [the longest x7 7.26 us: call(): pl.pallas_call(kernel, out_shape=[VMEM(s, d) for s, d in outs], in_specs=...]
    ppermute x2, starting transfers between devices: 4.05 us -> 4.52 us  [the longest x1 3.03 us: body(): lax.ppermute(to_side, 'horiz', [(i, (i + 1 - 2 * (i % 2)) % around) for i...]
  transfers between devices with their start and end apart: 6 -> 6, of which waited for: 5 -> 4; matrix products, arithmetic and copies ran while one was open for 0% -> 0% of each run, Pallas kernels for 22% -> 28%
where the time goes in v3:
time: 25.4 us; the launch traced here: 25.2 us
  Pallas kernels  9.94 us (39%)
  starting transfers between devices  8.96 us (35%)
  waiting for transfers between devices  6.23 us (25%)
    pallas_call x7, Pallas kernels, call(): pl.pallas_call(kernel, out_shape=[VMEM(s, d) for s, d in outs], in_specs=...  7.26 us
    ppermute x4, waiting for transfers between devices, swap(): return lax.ppermute(x, 'depth', [(i, i ^ 1 << bit) for i in range(ranks)])  5.03 us
    ppermute x4, starting transfers between devices, swap(): return lax.ppermute(x, 'depth', [(i, i ^ 1 << bit) for i in range(ranks)])  4.44 us
    ppermute x1, starting transfers between devices, body(): lax.ppermute(to_side, 'horiz', [(i, (i + 1 - 2 * (i % 2)) % around) for i...  3.03 us
    pallas_call x2, Pallas kernels, finish(): pl.pallas_call(functools.partial(finish_kernel, step, own), out_shape=plt...  2.68 us
    ppermute x1, starting transfers between devices, body(): lax.ppermute(to_far, 'horiz', [(i, (i + 2 * (i % 2) - 1) % around) for i...  1.49 us
    ppermute x1, waiting for transfers between devices, body(): lax.ppermute(to_far, 'horiz', [(i, (i + 2 * (i % 2) - 1) % around) for i...  1.2 us
  transfers between devices with their start and end apart: 6, of which 4 were waited for; matrix products, arithmetic and copies ran while one was open for 0% of the time, Pallas kernels for 28%

profile of v3, /device:TPU:0, one launch (start us, length us, event | category | flops | bytes accessed | tf_op | source)
XLA Modules:
  0.0 25.2 jit_solution(4738991699315703920)
XLA Ops:
  0.0 0.0 copy-start.1
  0.0 0.0 copy-start
  0.0 1.3 %shard_map.55 = (f32[3,32,256]{2,1,0:T(8,128)S(1)}, f32[3,32,256]{2,1,0:T(8,128)S(1)}, f32[2,32,256]{2,1,0:T(8,128)S(1)}, s32[1,32]{1,0:T(1,128)S(1)}, f32[4,32]{1,0:T(4,128)S(1)}, /*index=5*/f32[4,32,32]{2,1,0:T(8,128)S(1)}) custom-call(f32[3,32,32,256]{3,2,1,0:T(8,128)} %fields_ref.3, f32[32,32,256]{2,1,0:T(8,128)} %diff_ref.3, s32[1,32]{1,0:T(1,128)} %bitcast.1, ...), custom_call_target="tpu_custom_call" | custom-call | tf_op jit(solution)/shard_map/pallas_call | solution.py:466
  1.3 3.0 %collective-permute-start = (f32[3,32,256]{2,1,0:T(8,128)S(1)}, f32[3,32,256]{2,1,0:T(8,128)S(1)}, u32[]{:S(2)}, u32[]{:S(2)}) collective-permute-start(f32[3,32,256]{2,1,0:T(8,128)S(1)} %get-tuple-element.29), channel_id=1, source_target_pairs={{0,8},{8,0},{16,24},{24,16},{1,9},{9,1},{17,25},{25,17},{2,10},{10... | collective-permute-start | bytes 294920 | tf_op jit(solution)/shard_map/ppermute | solution.py:529
  4.4 1.5 %collective-permute-start.1 = (f32[3,32,256]{2,1,0:T(8,128)S(1)}, f32[3,32,256]{2,1,0:T(8,128)S(1)}, u32[]{:S(2)}, u32[]{:S(2)}) collective-permute-start(f32[3,32,256]{2,1,0:T(8,128)S(1)} %get-tuple-element.30), channel_id=1, source_target_pairs={{0,24},{8,16},{16,8},{24,0},{1,25},{9,17},{17,9},{25,1},{2,26},{10... | collective-permute-start | bytes 294920 | tf_op jit(solution)/shard_map/ppermute | solution.py:528
  5.9 0.0 copy-done.1
  5.9 0.0 copy-done
  5.9 3.5 %shard_map.56 = (s32[32,128]{1,0:T(8,128)S(1)}, f32[2,4,32,128]{3,2,1,0:T(8,128)S(1)}, f32[2,4,32,128]{3,2,1,0:T(8,128)S(1)}, f32[24,128]{1,0:T(8,128)S(1)}, f32...) custom-call(f32[3,32,32,256]{3,2,1,0:T(8,128)S(1)} %copy-done, f32[32,32,256]{2,1,0:T(8,128)S(1)} %copy-done.1, ...), custom_call_target="tpu_custom_call" | custom-call | tf_op jit(solution)/shard_map/pallas_call | solution.py:466
  9.4 0.0 collective-permute-done.side_ref
  9.4 1.2 %collective-permute-done.1.far_ref = f32[3,32,256]{2,1,0:T(8,128)S(1)} collective-permute-done((f32[3,32,256]{2,1,0:T(8,128)S(1)}, f32[3,32,256]{2,1,0:T(8,128)S(1)}, u32[]{:S(2)}, u32[]{:S(2)}) %collective-permute-start.1) | collective-permute-done | bytes 98336 | tf_op jit(solution)/shard_map/ppermute | solution.py:528
  10.6 0.1 shard_map.57
  10.7 0.1 collective-permute-start.2
  10.8 1.3 %collective-permute-done.2.got_ref = f32[208,128]{1,0:T(8,128)S(1)} collective-permute-done((f32[208,128]{1,0:T(8,128)S(1)}, f32[208,128]{1,0:T(8,128)S(1)}, u32[]{:S(2)}, u32[]{:S(2)}) %collective-permute-start.2) | collective-permute-done | bytes 106528 | tf_op jit(solution)/shard_map/ppermute | solution.py:512
  12.1 1.6 %collective-permute-start.3 = (f32[208,128]{1,0:T(8,128)S(1)}, f32[208,128]{1,0:T(8,128)S(1)}, u32[]{:S(2)}, u32[]{:S(2)}) collective-permute-start(f32[208,128]{1,0:T(8,128)S(1)} %get-tuple-element.41.after_ref.mine_ref), channel_id=1, source_target_pairs={{0,2},{1,3},{2,0},{3,1},{4,6},{5,7},{6,4},{7,5},{8,10},{9,11},{10,... | collective-permute-start | bytes 319496 | tf_op jit(solution)/shard_map/ppermute | solution.py:512
  13.8 2.2 %shard_map.59 = (f32[4,3,256,256]{3,2,1,0:T(8,128)S(1)}, f32[8,128]{1,0:T(8,128)S(1)}) custom-call(f32[208,128]{1,0:T(8,128)S(1)} %get-tuple-element.41.after_ref.mine_ref, f32[4,3,256,256]{3,2,1,0:T(8,128)S(1)} %get-tuple-element.42.forcing_ref, f32[2,3,32,256]{3,2,1,0:T(8,128)S(1)} %get-tuple-element.43.extra_ref, ...), custom_call_target="tpu_custom_call" | custom-call | tf_op jit(solution)/shard_map/pallas_call | solution.py:466
  15.9 1.3 %collective-permute-done.3.got_ref = f32[208,128]{1,0:T(8,128)S(1)} collective-permute-done((f32[208,128]{1,0:T(8,128)S(1)}, f32[208,128]{1,0:T(8,128)S(1)}, u32[]{:S(2)}, u32[]{:S(2)}) %collective-permute-start.3) | collective-permute-done | bytes 106528 | tf_op jit(solution)/shard_map/ppermute | solution.py:512
  17.2 0.1 shard_map.60
  17.3 2.7 %collective-permute-start.4 = (f32[100,128]{1,0:T(8,128)S(1)}, f32[100,128]{1,0:T(8,128)S(1)}, u32[]{:S(2)}, u32[]{:S(2)}) collective-permute-start(f32[100,128]{1,0:T(8,128)S(1)} %get-tuple-element.46.refs_0_), channel_id=1, source_target_pairs={{0,4},{1,5},{2,6},{3,7},{4,0},{5,1},{6,2},{7,3},{8,12},{9,13},{10,... | collective-permute-start | bytes 153608 | tf_op jit(solution)/shard_map/ppermute | solution.py:512
  19.9 2.4 %collective-permute-done.4.refs_1_ = f32[100,128]{1,0:T(8,128)S(1)} collective-permute-done((f32[100,128]{1,0:T(8,128)S(1)}, f32[100,128]{1,0:T(8,128)S(1)}, u32[]{:S(2)}, u32[]{:S(2)}) %collective-permute-start.4) | collective-permute-done | bytes 51232 | tf_op jit(solution)/shard_map/ppermute | solution.py:512
  22.4 0.1 shard_map.61
  22.5 0.1 collective-permute-start.5
  22.5 1.3 %shard_map.62.refs_0_ = f32[3,32,32,256]{3,2,1,0:T(8,128)} custom-call(f32[4,3,256,256]{3,2,1,0:T(8,128)S(1)} %get-tuple-element.44.solved_ref, f32[192,128]{1,0:T(8,128)S(1)} %get-tuple-element.52.ends_ref, s32[32,128]{1,0:T(8,128)S(1)} %get-tuple-element.36.offsb_ref.refs_3_, f32[2,4,32,128]{3,2,1,0:T(8,128)S(1)} %get-tuple-element.51.spikes_ref), custom_call_target="tpu_custom_call" | custom-call | tf_op jit(solution)/shard_map/pallas_call | solution.py:486
  23.9 0.0 collective-permute-done.5.ends_ref
  23.9 1.3 %shard_map.63 = f32[3,32,32,256]{3,2,1,0:T(8,128)} custom-call(f32[4,3,256,256]{3,2,1,0:T(8,128)S(1)} %get-tuple-element.44.solved_ref, f32[192,128]{1,0:T(8,128)S(1)} %collective-permute-done.5.ends_ref, s32[32,128]{1,0:T(8,128)S(1)} %get-tuple-element.36.offsb_ref.refs_3_, ...), custom_call_target="tpu_custom_call", output_to_operand_aliasing={{}: (4, {})} | custom-call | tf_op jit(solution)/shard_map/pallas_call | solution.py:486
  (1 shorter events, 0.0 us)
Async XLA Ops:
  0.0 5.9 %copy-start.1 = (f32[32,32,256]{2,1,0:T(8,128)S(1)}, f32[32,32,256]{2,1,0:T(8,128)}, u32[]{:S(2)}) copy-start(f32[32,32,256]{2,1,0:T(8,128)} %diff_ref.3) | copy-start | bytes 3145732
  0.0 5.9 %copy-start = (f32[3,32,32,256]{3,2,1,0:T(8,128)S(1)}, f32[3,32,32,256]{3,2,1,0:T(8,128)}, u32[]{:S(2)}) copy-start(f32[3,32,32,256]{3,2,1,0:T(8,128)} %fields_ref.3) | copy-start | bytes 9437188
  1.3 8.0 %collective-permute-start = (f32[3,32,256]{2,1,0:T(8,128)S(1)}, f32[3,32,256]{2,1,0:T(8,128)S(1)}, u32[]{:S(2)}, u32[]{:S(2)}) collective-permute-start(f32[3,32,256]{2,1,0:T(8,128)S(1)} %get-tuple-element.29), channel_id=1, source_target_pairs={{0,8},{8,0},{16,24},{24,16},{1,9},{9,1},{17,25},{25,17},{2,10},{10... | collective-permute-start | bytes 294920 | tf_op jit(solution)/shard_map/ppermute | solution.py:529
  4.4 6.2 %collective-permute-start.1 = (f32[3,32,256]{2,1,0:T(8,128)S(1)}, f32[3,32,256]{2,1,0:T(8,128)S(1)}, u32[]{:S(2)}, u32[]{:S(2)}) collective-permute-start(f32[3,32,256]{2,1,0:T(8,128)S(1)} %get-tuple-element.30), channel_id=1, source_target_pairs={{0,24},{8,16},{16,8},{24,0},{1,25},{9,17},{17,9},{25,1},{2,26},{10... | collective-permute-start | bytes 294920 | tf_op jit(solution)/shard_map/ppermute | solution.py:528
  10.7 1.4 %collective-permute-start.2 = (f32[208,128]{1,0:T(8,128)S(1)}, f32[208,128]{1,0:T(8,128)S(1)}, u32[]{:S(2)}, u32[]{:S(2)}) collective-permute-start(f32[208,128]{1,0:T(8,128)S(1)} %get-tuple-element.40), channel_id=1, source_target_pairs={{0,1},{1,0},{2,3},{3,2},{4,5},{5,4},{6,7},{7,6},{8,9},{9,8},{10,11... | collective-permute-start | bytes 319496 | tf_op jit(solution)/shard_map/ppermute | solution.py:512
  12.1 5.1 %collective-permute-start.3 = (f32[208,128]{1,0:T(8,128)S(1)}, f32[208,128]{1,0:T(8,128)S(1)}, u32[]{:S(2)}, u32[]{:S(2)}) collective-permute-start(f32[208,128]{1,0:T(8,128)S(1)} %get-tuple-element.41.after_ref.mine_ref), channel_id=1, source_target_pairs={{0,2},{1,3},{2,0},{3,1},{4,6},{5,7},{6,4},{7,5},{8,10},{9,11},{10,... | collective-permute-start | bytes 319496 | tf_op jit(solution)/shard_map/ppermute | solution.py:512
  17.3 5.1 %collective-permute-start.4 = (f32[100,128]{1,0:T(8,128)S(1)}, f32[100,128]{1,0:T(8,128)S(1)}, u32[]{:S(2)}, u32[]{:S(2)}) collective-permute-start(f32[100,128]{1,0:T(8,128)S(1)} %get-tuple-element.46.refs_0_), channel_id=1, source_target_pairs={{0,4},{1,5},{2,6},{3,7},{4,0},{5,1},{6,2},{7,3},{8,12},{9,13},{10,... | collective-permute-start | bytes 153608 | tf_op jit(solution)/shard_map/ppermute | solution.py:512
  22.5 1.4 %collective-permute-start.5 = (f32[192,128]{1,0:T(8,128)S(1)}, f32[192,128]{1,0:T(8,128)S(1)}, u32[]{:S(2)}, u32[]{:S(2)}) collective-permute-start(f32[192,128]{1,0:T(8,128)S(1)} %get-tuple-element.50), channel_id=1, source_target_pairs={{0,1},{1,0},{2,3},{3,2},{4,5},{5,4},{6,7},{7,6},{8,9},{9,8},{10,11... | collective-permute-start | bytes 294920 | tf_op jit(solution)/shard_map/ppermute | solution.py:512

commit v4 on v3

--- a/solution.py
+++ b/solution.py
@@ -40,12 +40,11 @@
     inverse_hbm,
     side_ref,
     far_ref,
-    diff_rows_ref,
+    diff_stage_ref,
     offs_ref,
     coupling_ref,
     inverse_ref,
     stage_ref,
-    diff_stage_ref,
     sems,
 ):
     parts, levels, lines, ny = fields_ref.shape
@@ -71,17 +70,12 @@
             first, last = [gather_rows(lambda k: stage_ref[e, i, k, 0:1, :], c, ny) for e in range(2)]
             side_ref[i, at, :] = jnp.where(even, last, first)
             far_ref[i, at, :] = jnp.where(even, first, last)
-    for e in range(2):
-        for c in range(levels // SUB):
-            diff_rows_ref[e, c * SUB : (c + 1) * SUB, :] = gather_rows(
-                lambda k: diff_stage_ref[e, k, 0:1, :], c, ny
-            )
 
 
 def gather_rows(row_at, c, ny):
     sub = lax.broadcasted_iota(jnp.int32, (SUB, ny), 0)
-    value = jnp.zeros((SUB, ny), F32)
-    for t in range(SUB):
+    value = jnp.broadcast_to(row_at(c * SUB), (SUB, ny))
+    for t in range(1, SUB):
         value = jnp.where(sub == t, jnp.broadcast_to(row_at(c * SUB + t), value.shape), value)
     return value
 
@@ -148,15 +142,16 @@
             east = jnp.where(sub == SUB - 1, jnp.broadcast_to(row_e, c.shape), pltpu.roll(c, SUB - 1, 0))
             west = jnp.where(sub == 0, jnp.broadcast_to(row_w, c.shape), pltpu.roll(c, 1, 0))
             centre.append(c)
-            both.append((east + west) + (north + south) - 4.0 * c)
+            both.append((east + west) + (north + south))
             along.append(east - west)
             across.append(north - south)
         d = diff_ref[k, first : first + SUB, :]
+        rest = 1.0 - 4.0 * d
         scale = 0.5 * wave_gain
         out = (
-            centre[0] + d * both[0] - scale * along[2],
-            centre[1] + d * both[1] - scale * across[2],
-            centre[2] + d * both[2] - scale * (along[0] + across[1]),
+            rest * centre[0] + d * both[0] - scale * along[2],
+            rest * centre[1] + d * both[1] - scale * across[2],
+            rest * centre[2] + d * both[2] - scale * (along[0] + across[1]),
         )
         at = pl.multiple_of(k * SUB, SUB)
         top = choose(offs, [rows_ref[0, o, pl.ds(k, 1), :] for o in range(count)])
@@ -183,14 +178,22 @@
     return one_level, tuple(jnp.zeros((SUB, half), F32) for _ in range(4 * parts)), close
 
 
-def run_groups(groups, levels):
-    for one_level, sums, close in groups:
-        close(lax.fori_loop(0, levels, one_level, sums, unroll=SUB))
+def run_groups(groups, levels, waits):
+    for n, (one_level, sums, close) in enumerate(groups):
+        if n == 0:
+            step = levels // len(waits)
+            for c, wait in enumerate(waits):
+                wait()
+                sums = lax.fori_loop(c * step, (c + 1) * step, one_level, sums, unroll=True)
+        else:
+            sums = lax.fori_loop(0, levels, one_level, sums, unroll=True)
+        close(sums)
 
 
 def inner_kernel(
-    fields_ref,
-    diff_ref,
+    fields_hbm,
+    diff_hbm,
+    diff_stage_ref,
     offs_ref,
     coupling_ref,
     inverse_ref,
@@ -200,14 +203,37 @@
     coefs_ref,
     forcing_ref,
     sides_ref,
+    diff_rows_ref,
+    fields_ref,
+    diff_ref,
+    sems,
 ):
-    levels, lines, _ = diff_ref.shape
+    parts, levels, lines, ny = fields_ref.shape
+    chunks = sems.shape[0] // (parts + 1)
+    step = levels // chunks
+    waits = []
+    for c in range(chunks):
+        at = pl.ds(c * step, step)
+        pairs = [(fields_hbm.at[i, at], fields_ref.at[i, at]) for i in range(parts)]
+        pairs.append((diff_hbm.at[at], diff_ref.at[at]))
+        copies = [
+            pltpu.make_async_copy(source, target, sems.at[c * (parts + 1) + n])
+            for n, (source, target) in enumerate(pairs)
+        ]
+        for copy in copies:
+            copy.start()
+        waits.append(lambda copies=copies: [copy.wait() for copy in copies])
     fill_tables(offs_ref, coupling_ref, inverse_ref, offsb_ref, spikes_ref, rows_ref, coefs_ref)
+    for e in range(2):
+        for c in range(levels // SUB):
+            diff_rows_ref[e, c * SUB : (c + 1) * SUB, :] = gather_rows(
+                lambda k: diff_stage_ref[e, k, 0:1, :], c, ny
+            )
     work = [
         force_group(g, fields_ref, diff_ref, offsb_ref, rows_ref, coefs_ref, forcing_ref, sides_ref)
         for g in range(lines // SUB)
     ]
-    run_groups(work, levels)
+    run_groups(work, levels, waits)
 
 
 def correct_kernel(
@@ -514,13 +540,12 @@
     in_hbm = pl.BlockSpec(memory_space=pltpu.HBM)
     edge = ((parts, levels, ny), F32)
     offsets = offsets.reshape(1, lines)
-    to_side, to_far, diff_rows, offsets, coupling, inverse = call(
+    to_side, to_far, diff_stage, offsets, coupling, inverse = call(
         outermost_kernel,
-        [edge, edge, ((2, levels, ny), F32), (offsets.shape, jnp.int32), (coupling.shape, F32), (inverse.shape, F32)],
+        [edge, edge, ((2, levels, 1, ny), F32), (offsets.shape, jnp.int32), (coupling.shape, F32), (inverse.shape, F32)],
         [pltpu.with_memory_space_constraint(x, pltpu.HBM) for x in (fields, diffusivity, offsets, coupling, inverse)],
         scratch=[
             pltpu.VMEM((2, parts, levels, 1, ny), F32),
-            pltpu.VMEM((2, levels, 1, ny), F32),
             pltpu.SemaphoreType.DMA((7,)),
         ],
         specs=[in_hbm] * 5,
@@ -530,7 +555,7 @@
 
     rows = parts * lines
     table = ((2, count, levels, LANE), F32)
-    offsb, spikes, k_rows, coefs, forcing, sides = call(
+    offsb, spikes, k_rows, coefs, forcing, sides, diff_rows = call(
         inner_kernel,
         [
             ((lines, LANE), jnp.int32),
@@ -539,9 +564,16 @@
             ((6 * count, LANE), F32),
             ((groups, parts, width, ny), F32),
             ((2 * rows, ny), F32),
+            ((2, levels, ny), F32),
         ],
-        (fields, diffusivity, offsets, coupling, inverse),
-        specs=[vmem_spec()] * 5,
+        [pltpu.with_memory_space_constraint(x, pltpu.HBM) for x in (fields, diffusivity)]
+        + [diff_stage, offsets, coupling, inverse],
+        scratch=[
+            pltpu.VMEM(fields.shape, F32),
+            pltpu.VMEM(diffusivity.shape, F32),
+            pltpu.SemaphoreType.DMA(((parts + 1) * (levels // SUB),)),
+        ],
+        specs=[in_hbm] * 2 + [vmem_spec()] * 4,
     )
     element_shape = ((2 * rows + 4 * count, half), F32)
     saved_shape = ((rows + 2 * count, half), F32)

time: 25.4 us -> 25.2 us (level)
  waiting for transfers between devices: 6.23 us -> 5.43 us
  Pallas kernels: 9.94 us -> 10.6 us
    ppermute x1, waiting for transfers between devices: 1.2 us -> 0.36 us  [body(): lax.ppermute(to_far, 'horiz', [(i, (i + 2 * (i % 2) - 1) % around) for i...]
    pallas_call x7, Pallas kernels: 7.26 us -> 7.89 us  [call(): pl.pallas_call(kernel, out_shape=[VMEM(s, d) for s, d in outs], in_specs=...]
  transfers between devices with their start and end apart: 6 -> 6, of which waited for: 4 -> 4; matrix products, arithmetic and copies ran while one was open for 0% -> 0% of each run, Pallas kernels for 28% -> 31%
where the time goes in v4:
time: 25.2 us; the launch traced here: 25 us
  Pallas kernels  10.6 us (42%)
  starting transfers between devices  8.96 us (36%)
  waiting for transfers between devices  5.43 us (22%)
    pallas_call x7, Pallas kernels, call(): pl.pallas_call(kernel, out_shape=[VMEM(s, d) for s, d in outs], in_specs=...  7.89 us
    ppermute x4, waiting for transfers between devices, swap(): return lax.ppermute(x, 'depth', [(i, i ^ 1 << bit) for i in range(ranks)])  5.07 us
    ppermute x4, starting transfers between devices, swap(): return lax.ppermute(x, 'depth', [(i, i ^ 1 << bit) for i in range(ranks)])  4.44 us
    ppermute x1, starting transfers between devices, body(): lax.ppermute(to_side, 'horiz', [(i, (i + 1 - 2 * (i % 2)) % around) for i...  3.03 us
    pallas_call x2, Pallas kernels, finish(): pl.pallas_call(functools.partial(finish_kernel, step, own), out_shape=plt...  2.68 us
    ppermute x1, starting transfers between devices, body(): lax.ppermute(to_far, 'horiz', [(i, (i + 2 * (i % 2) - 1) % around) for i...  1.49 us
  transfers between devices with their start and end apart: 6, of which 4 were waited for; matrix products, arithmetic and copies ran while one was open for 0% of the time, Pallas kernels for 31%

profile of v4, /device:TPU:0, one launch (start us, length us, event | category | flops | bytes accessed | tf_op | source)
XLA Modules:
  0.0 25.0 jit_solution(14386871685889045636)
XLA Ops:
  0.0 1.2 %shard_map.55 = (f32[3,32,256]{2,1,0:T(8,128)S(1)}, f32[3,32,256]{2,1,0:T(8,128)S(1)}, f32[2,32,1,256]{3,2,1,0:T(1,128)S(1)}, s32[1,32]{1,0:T(1,128)S(1)}, f32[4...) custom-call(f32[3,32,32,256]{3,2,1,0:T(8,128)} %fields_hbm.1, f32[32,32,256]{2,1,0:T(8,128)} %diff_hbm.1, s32[1,32]{1,0:T(1,128)} %bitcast.1, ...), custom_call_target="tpu_custom_call" | custom-call | tf_op jit(solution)/shard_map/pallas_call | solution.py:492
  1.2 3.0 %collective-permute-start = (f32[3,32,256]{2,1,0:T(8,128)S(1)}, f32[3,32,256]{2,1,0:T(8,128)S(1)}, u32[]{:S(2)}, u32[]{:S(2)}) collective-permute-start(f32[3,32,256]{2,1,0:T(8,128)S(1)} %get-tuple-element.30), channel_id=1, source_target_pairs={{0,8},{8,0},{16,24},{24,16},{1,9},{9,1},{17,25},{25,17},{2,10},{10... | collective-permute-start | bytes 294920 | tf_op jit(solution)/shard_map/ppermute | solution.py:554
  4.2 1.5 %collective-permute-start.1 = (f32[3,32,256]{2,1,0:T(8,128)S(1)}, f32[3,32,256]{2,1,0:T(8,128)S(1)}, u32[]{:S(2)}, u32[]{:S(2)}) collective-permute-start(f32[3,32,256]{2,1,0:T(8,128)S(1)} %get-tuple-element.31), channel_id=1, source_target_pairs={{0,24},{8,16},{16,8},{24,0},{1,25},{9,17},{17,9},{25,1},{2,26},{10... | collective-permute-start | bytes 294920 | tf_op jit(solution)/shard_map/ppermute | solution.py:553
  5.7 4.3 %shard_map.56 = (s32[32,128]{1,0:T(8,128)S(1)}, f32[2,4,32,128]{3,2,1,0:T(8,128)S(1)}, f32[2,4,32,128]{3,2,1,0:T(8,128)S(1)}, f32[24,128]{1,0:T(8,128)S(1)}, f32...) custom-call(f32[3,32,32,256]{3,2,1,0:T(8,128)} %fields_hbm.1, ...), custom_call_target="tpu_custom_call" | custom-call | tf_op jit(solution)/shard_map/pallas_call | solution.py:492
  10.0 0.0 collective-permute-done.side_ref
  10.0 0.4 %collective-permute-done.1.far_ref = f32[3,32,256]{2,1,0:T(8,128)S(1)} collective-permute-done((f32[3,32,256]{2,1,0:T(8,128)S(1)}, f32[3,32,256]{2,1,0:T(8,128)S(1)}, u32[]{:S(2)}, u32[]{:S(2)}) %collective-permute-start.1) | collective-permute-done | bytes 98336 | tf_op jit(solution)/shard_map/ppermute | solution.py:553
  10.4 0.1 shard_map.57
  10.5 0.1 collective-permute-start.2
  10.6 1.3 %collective-permute-done.2.got_ref = f32[208,128]{1,0:T(8,128)S(1)} collective-permute-done((f32[208,128]{1,0:T(8,128)S(1)}, f32[208,128]{1,0:T(8,128)S(1)}, u32[]{:S(2)}, u32[]{:S(2)}) %collective-permute-start.2) | collective-permute-done | bytes 106528 | tf_op jit(solution)/shard_map/ppermute | solution.py:538
  11.9 1.6 %collective-permute-start.3 = (f32[208,128]{1,0:T(8,128)S(1)}, f32[208,128]{1,0:T(8,128)S(1)}, u32[]{:S(2)}, u32[]{:S(2)}) collective-permute-start(f32[208,128]{1,0:T(8,128)S(1)} %get-tuple-element.43.after_ref.mine_ref), channel_id=1, source_target_pairs={{0,2},{1,3},{2,0},{3,1},{4,6},{5,7},{6,4},{7,5},{8,10},{9,11},{10,... | collective-permute-start | bytes 319496 | tf_op jit(solution)/shard_map/ppermute | solution.py:538
  13.6 2.1 %shard_map.59 = (f32[4,3,256,256]{3,2,1,0:T(8,128)S(1)}, f32[8,128]{1,0:T(8,128)S(1)}) custom-call(f32[208,128]{1,0:T(8,128)S(1)} %get-tuple-element.43.after_ref.mine_ref, f32[4,3,256,256]{3,2,1,0:T(8,128)S(1)} %get-tuple-element.44.forcing_ref, f32[2,3,32,256]{3,2,1,0:T(8,128)S(1)} %get-tuple-element.45.extra_ref, ...), custom_call_target="tpu_custom_call" | custom-call | tf_op jit(solution)/shard_map/pallas_call | solution.py:492
  15.7 1.3 %collective-permute-done.3.got_ref = f32[208,128]{1,0:T(8,128)S(1)} collective-permute-done((f32[208,128]{1,0:T(8,128)S(1)}, f32[208,128]{1,0:T(8,128)S(1)}, u32[]{:S(2)}, u32[]{:S(2)}) %collective-permute-start.3) | collective-permute-done | bytes 106528 | tf_op jit(solution)/shard_map/ppermute | solution.py:538
  17.0 0.1 shard_map.60
  17.1 2.7 %collective-permute-start.4 = (f32[100,128]{1,0:T(8,128)S(1)}, f32[100,128]{1,0:T(8,128)S(1)}, u32[]{:S(2)}, u32[]{:S(2)}) collective-permute-start(f32[100,128]{1,0:T(8,128)S(1)} %get-tuple-element.48.refs_0_), channel_id=1, source_target_pairs={{0,4},{1,5},{2,6},{3,7},{4,0},{5,1},{6,2},{7,3},{8,12},{9,13},{10,... | collective-permute-start | bytes 153608 | tf_op jit(solution)/shard_map/ppermute | solution.py:538
  19.8 2.4 %collective-permute-done.4.refs_1_ = f32[100,128]{1,0:T(8,128)S(1)} collective-permute-done((f32[100,128]{1,0:T(8,128)S(1)}, f32[100,128]{1,0:T(8,128)S(1)}, u32[]{:S(2)}, u32[]{:S(2)}) %collective-permute-start.4) | collective-permute-done | bytes 51232 | tf_op jit(solution)/shard_map/ppermute | solution.py:538
  22.2 0.1 shard_map.61
  22.3 0.1 collective-permute-start.5
  22.3 1.3 %shard_map.62.refs_0_ = f32[3,32,32,256]{3,2,1,0:T(8,128)} custom-call(f32[4,3,256,256]{3,2,1,0:T(8,128)S(1)} %get-tuple-element.46.solved_ref, f32[192,128]{1,0:T(8,128)S(1)} %get-tuple-element.54.ends_ref, s32[32,128]{1,0:T(8,128)S(1)} %get-tuple-element.38.offsb_ref.refs_3_, f32[2,4,32,128]{3,2,1,0:T(8,128)S(1)} %get-tuple-element.53.spikes_ref), custom_call_target="tpu_custom_call" | custom-call | tf_op jit(solution)/shard_map/pallas_call | solution.py:512
  23.7 0.0 collective-permute-done.5.ends_ref
  23.7 1.3 %shard_map.63 = f32[3,32,32,256]{3,2,1,0:T(8,128)} custom-call(f32[4,3,256,256]{3,2,1,0:T(8,128)S(1)} %get-tuple-element.46.solved_ref, f32[192,128]{1,0:T(8,128)S(1)} %collective-permute-done.5.ends_ref, s32[32,128]{1,0:T(8,128)S(1)} %get-tuple-element.38.offsb_ref.refs_3_, ...), custom_call_target="tpu_custom_call", output_to_operand_aliasing={{}: (4, {})} | custom-call | tf_op jit(solution)/shard_map/pallas_call | solution.py:512
  (1 shorter events, 0.0 us)
Async XLA Ops:
  1.2 8.9 %collective-permute-start = (f32[3,32,256]{2,1,0:T(8,128)S(1)}, f32[3,32,256]{2,1,0:T(8,128)S(1)}, u32[]{:S(2)}, u32[]{:S(2)}) collective-permute-start(f32[3,32,256]{2,1,0:T(8,128)S(1)} %get-tuple-element.30), channel_id=1, source_target_pairs={{0,8},{8,0},{16,24},{24,16},{1,9},{9,1},{17,25},{25,17},{2,10},{10... | collective-permute-start | bytes 294920 | tf_op jit(solution)/shard_map/ppermute | solution.py:554
  4.2 6.2 %collective-permute-start.1 = (f32[3,32,256]{2,1,0:T(8,128)S(1)}, f32[3,32,256]{2,1,0:T(8,128)S(1)}, u32[]{:S(2)}, u32[]{:S(2)}) collective-permute-start(f32[3,32,256]{2,1,0:T(8,128)S(1)} %get-tuple-element.31), channel_id=1, source_target_pairs={{0,24},{8,16},{16,8},{24,0},{1,25},{9,17},{17,9},{25,1},{2,26},{10... | collective-permute-start | bytes 294920 | tf_op jit(solution)/shard_map/ppermute | solution.py:553
  10.5 1.4 %collective-permute-start.2 = (f32[208,128]{1,0:T(8,128)S(1)}, f32[208,128]{1,0:T(8,128)S(1)}, u32[]{:S(2)}, u32[]{:S(2)}) collective-permute-start(f32[208,128]{1,0:T(8,128)S(1)} %get-tuple-element.42), channel_id=1, source_target_pairs={{0,1},{1,0},{2,3},{3,2},{4,5},{5,4},{6,7},{7,6},{8,9},{9,8},{10,11... | collective-permute-start | bytes 319496 | tf_op jit(solution)/shard_map/ppermute | solution.py:538
  11.9 5.1 %collective-permute-start.3 = (f32[208,128]{1,0:T(8,128)S(1)}, f32[208,128]{1,0:T(8,128)S(1)}, u32[]{:S(2)}, u32[]{:S(2)}) collective-permute-start(f32[208,128]{1,0:T(8,128)S(1)} %get-tuple-element.43.after_ref.mine_ref), channel_id=1, source_target_pairs={{0,2},{1,3},{2,0},{3,1},{4,6},{5,7},{6,4},{7,5},{8,10},{9,11},{10,... | collective-permute-start | bytes 319496 | tf_op jit(solution)/shard_map/ppermute | solution.py:538
  17.1 5.1 %collective-permute-start.4 = (f32[100,128]{1,0:T(8,128)S(1)}, f32[100,128]{1,0:T(8,128)S(1)}, u32[]{:S(2)}, u32[]{:S(2)}) collective-permute-start(f32[100,128]{1,0:T(8,128)S(1)} %get-tuple-element.48.refs_0_), channel_id=1, source_target_pairs={{0,4},{1,5},{2,6},{3,7},{4,0},{5,1},{6,2},{7,3},{8,12},{9,13},{10,... | collective-permute-start | bytes 153608 | tf_op jit(solution)/shard_map/ppermute | solution.py:538
  22.3 1.4 %collective-permute-start.5 = (f32[192,128]{1,0:T(8,128)S(1)}, f32[192,128]{1,0:T(8,128)S(1)}, u32[]{:S(2)}, u32[]{:S(2)}) collective-permute-start(f32[192,128]{1,0:T(8,128)S(1)} %get-tuple-element.52), channel_id=1, source_target_pairs={{0,1},{1,0},{2,3},{3,2},{4,5},{5,4},{6,7},{7,6},{8,9},{9,8},{10,11... | collective-permute-start | bytes 294920 | tf_op jit(solution)/shard_map/ppermute | solution.py:538

commit v5 on v4

--- a/solution.py
+++ b/solution.py
@@ -179,15 +179,17 @@
 
 
 def run_groups(groups, levels, waits):
-    for n, (one_level, sums, close) in enumerate(groups):
-        if n == 0:
-            step = levels // len(waits)
-            for c, wait in enumerate(waits):
-                wait()
-                sums = lax.fori_loop(c * step, (c + 1) * step, one_level, sums, unroll=True)
-        else:
-            sums = lax.fori_loop(0, levels, one_level, sums, unroll=True)
-        close(sums)
+    step = levels // len(waits)
+    early = groups[:2]
+    sums = [start for _, start, _ in early]
+    for c, wait in enumerate(waits):
+        wait()
+        for n, (one_level, _, _) in enumerate(early):
+            sums[n] = lax.fori_loop(c * step, (c + 1) * step, one_level, sums[n], unroll=True)
+    for total, (_, _, close) in zip(sums, early):
+        close(total)
+    for one_level, start, close in groups[2:]:
+        close(lax.fori_loop(0, levels, one_level, start, unroll=True))
 
 
 def inner_kernel(
@@ -211,7 +213,7 @@
     parts, levels, lines, ny = fields_ref.shape
     chunks = sems.shape[0] // (parts + 1)
     step = levels // chunks
-    waits = []
+    starts, waits = [], []
     for c in range(chunks):
         at = pl.ds(c * step, step)
         pairs = [(fields_hbm.at[i, at], fields_ref.at[i, at]) for i in range(parts)]
@@ -220,9 +222,10 @@
             pltpu.make_async_copy(source, target, sems.at[c * (parts + 1) + n])
             for n, (source, target) in enumerate(pairs)
         ]
-        for copy in copies:
-            copy.start()
+        starts.append(lambda copies=copies: [copy.start() for copy in copies])
         waits.append(lambda copies=copies: [copy.wait() for copy in copies])
+    for start in starts:
+        start()
     fill_tables(offs_ref, coupling_ref, inverse_ref, offsb_ref, spikes_ref, rows_ref, coefs_ref)
     for e in range(2):
         for c in range(levels // SUB):

time: 25.2 us -> 25.2 us (level)
  Pallas kernels: 10.6 us -> 10.2 us
  waiting for transfers between devices: 5.43 us -> 5.83 us
    pallas_call x7, Pallas kernels: 7.89 us -> 7.49 us  [call(): pl.pallas_call(kernel, out_shape=[VMEM(s, d) for s, d in outs], in_specs=...]
    ppermute x1, waiting for transfers between devices: 0.36 us -> 0.76 us  [body(): lax.ppermute(to_far, 'horiz', [(i, (i + 2 * (i % 2) - 1) % around) for i...]
  transfers between devices with their start and end apart: 6 -> 6, of which waited for: 4 -> 4; matrix products, arithmetic and copies ran while one was open for 0% -> 0% of each run, Pallas kernels for 31% -> 30%
where the time goes in v5:
time: 25.2 us; the launch traced here: 25 us
  Pallas kernels  10.2 us (40%)
  starting transfers between devices  8.96 us (36%)
  waiting for transfers between devices  5.83 us (23%)
    pallas_call x7, Pallas kernels, call(): pl.pallas_call(kernel, out_shape=[VMEM(s, d) for s, d in outs], in_specs=...  7.49 us
    ppermute x4, waiting for transfers between devices, swap(): return lax.ppermute(x, 'depth', [(i, i ^ 1 << bit) for i in range(ranks)])  5.07 us
    ppermute x4, starting transfers between devices, swap(): return lax.ppermute(x, 'depth', [(i, i ^ 1 << bit) for i in range(ranks)])  4.44 us
    ppermute x1, starting transfers between devices, body(): lax.ppermute(to_side, 'horiz', [(i, (i + 1 - 2 * (i % 2)) % around) for i...  3.03 us
    pallas_call x2, Pallas kernels, finish(): pl.pallas_call(functools.partial(finish_kernel, step, own), out_shape=plt...  2.68 us
    ppermute x1, starting transfers between devices, body(): lax.ppermute(to_far, 'horiz', [(i, (i + 2 * (i % 2) - 1) % around) for i...  1.49 us
    ppermute x1, waiting for transfers between devices, body(): lax.ppermute(to_far, 'horiz', [(i, (i + 2 * (i % 2) - 1) % around) for i...  0.76 us
  transfers between devices with their start and end apart: 6, of which 4 were waited for; matrix products, arithmetic and copies ran while one was open for 0% of the time, Pallas kernels for 30%

profile of v5, /device:TPU:0, one launch (start us, length us, event | category | flops | bytes accessed | tf_op | source)
XLA Modules:
  0.0 25.0 jit_solution(5033934672190725249)
XLA Ops:
  0.0 1.2 %shard_map.55 = (f32[3,32,256]{2,1,0:T(8,128)S(1)}, f32[3,32,256]{2,1,0:T(8,128)S(1)}, f32[2,32,1,256]{3,2,1,0:T(1,128)S(1)}, s32[1,32]{1,0:T(1,128)S(1)}, f32[4...) custom-call(f32[3,32,32,256]{3,2,1,0:T(8,128)} %fields_hbm.1, f32[32,32,256]{2,1,0:T(8,128)} %diff_hbm.1, s32[1,32]{1,0:T(1,128)} %bitcast.1, ...), custom_call_target="tpu_custom_call" | custom-call | tf_op jit(solution)/shard_map/pallas_call | solution.py:495
  1.2 3.0 %collective-permute-start = (f32[3,32,256]{2,1,0:T(8,128)S(1)}, f32[3,32,256]{2,1,0:T(8,128)S(1)}, u32[]{:S(2)}, u32[]{:S(2)}) collective-permute-start(f32[3,32,256]{2,1,0:T(8,128)S(1)} %get-tuple-element.30), channel_id=1, source_target_pairs={{0,8},{8,0},{16,24},{24,16},{1,9},{9,1},{17,25},{25,17},{2,10},{10... | collective-permute-start | bytes 294920 | tf_op jit(solution)/shard_map/ppermute | solution.py:557
  4.2 1.5 %collective-permute-start.1 = (f32[3,32,256]{2,1,0:T(8,128)S(1)}, f32[3,32,256]{2,1,0:T(8,128)S(1)}, u32[]{:S(2)}, u32[]{:S(2)}) collective-permute-start(f32[3,32,256]{2,1,0:T(8,128)S(1)} %get-tuple-element.31), channel_id=1, source_target_pairs={{0,24},{8,16},{16,8},{24,0},{1,25},{9,17},{17,9},{25,1},{2,26},{10... | collective-permute-start | bytes 294920 | tf_op jit(solution)/shard_map/ppermute | solution.py:556
  5.7 3.9 %shard_map.56 = (s32[32,128]{1,0:T(8,128)S(1)}, f32[2,4,32,128]{3,2,1,0:T(8,128)S(1)}, f32[2,4,32,128]{3,2,1,0:T(8,128)S(1)}, f32[24,128]{1,0:T(8,128)S(1)}, f32...) custom-call(f32[3,32,32,256]{3,2,1,0:T(8,128)} %fields_hbm.1, ...), custom_call_target="tpu_custom_call" | custom-call | tf_op jit(solution)/shard_map/pallas_call | solution.py:495
  9.6 0.0 collective-permute-done.side_ref
  9.6 0.8 %collective-permute-done.1.far_ref = f32[3,32,256]{2,1,0:T(8,128)S(1)} collective-permute-done((f32[3,32,256]{2,1,0:T(8,128)S(1)}, f32[3,32,256]{2,1,0:T(8,128)S(1)}, u32[]{:S(2)}, u32[]{:S(2)}) %collective-permute-start.1) | collective-permute-done | bytes 98336 | tf_op jit(solution)/shard_map/ppermute | solution.py:556
  10.4 0.1 shard_map.57
  10.5 0.1 collective-permute-start.2
  10.6 1.3 %collective-permute-done.2.got_ref = f32[208,128]{1,0:T(8,128)S(1)} collective-permute-done((f32[208,128]{1,0:T(8,128)S(1)}, f32[208,128]{1,0:T(8,128)S(1)}, u32[]{:S(2)}, u32[]{:S(2)}) %collective-permute-start.2) | collective-permute-done | bytes 106528 | tf_op jit(solution)/shard_map/ppermute | solution.py:541
  11.9 1.6 %collective-permute-start.3 = (f32[208,128]{1,0:T(8,128)S(1)}, f32[208,128]{1,0:T(8,128)S(1)}, u32[]{:S(2)}, u32[]{:S(2)}) collective-permute-start(f32[208,128]{1,0:T(8,128)S(1)} %get-tuple-element.43.after_ref.mine_ref), channel_id=1, source_target_pairs={{0,2},{1,3},{2,0},{3,1},{4,6},{5,7},{6,4},{7,5},{8,10},{9,11},{10,... | collective-permute-start | bytes 319496 | tf_op jit(solution)/shard_map/ppermute | solution.py:541
  13.6 2.1 %shard_map.59 = (f32[4,3,256,256]{3,2,1,0:T(8,128)S(1)}, f32[8,128]{1,0:T(8,128)S(1)}) custom-call(f32[208,128]{1,0:T(8,128)S(1)} %get-tuple-element.43.after_ref.mine_ref, f32[4,3,256,256]{3,2,1,0:T(8,128)S(1)} %get-tuple-element.44.forcing_ref, f32[2,3,32,256]{3,2,1,0:T(8,128)S(1)} %get-tuple-element.45.extra_ref, ...), custom_call_target="tpu_custom_call" | custom-call | tf_op jit(solution)/shard_map/pallas_call | solution.py:495
  15.7 1.3 %collective-permute-done.3.got_ref = f32[208,128]{1,0:T(8,128)S(1)} collective-permute-done((f32[208,128]{1,0:T(8,128)S(1)}, f32[208,128]{1,0:T(8,128)S(1)}, u32[]{:S(2)}, u32[]{:S(2)}) %collective-permute-start.3) | collective-permute-done | bytes 106528 | tf_op jit(solution)/shard_map/ppermute | solution.py:541
  17.0 0.1 shard_map.60
  17.1 2.7 %collective-permute-start.4 = (f32[100,128]{1,0:T(8,128)S(1)}, f32[100,128]{1,0:T(8,128)S(1)}, u32[]{:S(2)}, u32[]{:S(2)}) collective-permute-start(f32[100,128]{1,0:T(8,128)S(1)} %get-tuple-element.48.refs_0_), channel_id=1, source_target_pairs={{0,4},{1,5},{2,6},{3,7},{4,0},{5,1},{6,2},{7,3},{8,12},{9,13},{10,... | collective-permute-start | bytes 153608 | tf_op jit(solution)/shard_map/ppermute | solution.py:541
  19.8 2.4 %collective-permute-done.4.refs_1_ = f32[100,128]{1,0:T(8,128)S(1)} collective-permute-done((f32[100,128]{1,0:T(8,128)S(1)}, f32[100,128]{1,0:T(8,128)S(1)}, u32[]{:S(2)}, u32[]{:S(2)}) %collective-permute-start.4) | collective-permute-done | bytes 51232 | tf_op jit(solution)/shard_map/ppermute | solution.py:541
  22.2 0.1 shard_map.61
  22.3 0.1 collective-permute-start.5
  22.3 1.3 %shard_map.62.refs_0_ = f32[3,32,32,256]{3,2,1,0:T(8,128)} custom-call(f32[4,3,256,256]{3,2,1,0:T(8,128)S(1)} %get-tuple-element.46.solved_ref, f32[192,128]{1,0:T(8,128)S(1)} %get-tuple-element.54.ends_ref, s32[32,128]{1,0:T(8,128)S(1)} %get-tuple-element.38.offsb_ref.refs_3_, f32[2,4,32,128]{3,2,1,0:T(8,128)S(1)} %get-tuple-element.53.spikes_ref), custom_call_target="tpu_custom_call" | custom-call | tf_op jit(solution)/shard_map/pallas_call | solution.py:515
  23.7 0.0 collective-permute-done.5.ends_ref
  23.7 1.3 %shard_map.63 = f32[3,32,32,256]{3,2,1,0:T(8,128)} custom-call(f32[4,3,256,256]{3,2,1,0:T(8,128)S(1)} %get-tuple-element.46.solved_ref, f32[192,128]{1,0:T(8,128)S(1)} %collective-permute-done.5.ends_ref, s32[32,128]{1,0:T(8,128)S(1)} %get-tuple-element.38.offsb_ref.refs_3_, ...), custom_call_target="tpu_custom_call", output_to_operand_aliasing={{}: (4, {})} | custom-call | tf_op jit(solution)/shard_map/pallas_call | solution.py:515
  (1 shorter events, 0.0 us)
Async XLA Ops:
  1.2 8.5 %collective-permute-start = (f32[3,32,256]{2,1,0:T(8,128)S(1)}, f32[3,32,256]{2,1,0:T(8,128)S(1)}, u32[]{:S(2)}, u32[]{:S(2)}) collective-permute-start(f32[3,32,256]{2,1,0:T(8,128)S(1)} %get-tuple-element.30), channel_id=1, source_target_pairs={{0,8},{8,0},{16,24},{24,16},{1,9},{9,1},{17,25},{25,17},{2,10},{10... | collective-permute-start | bytes 294920 | tf_op jit(solution)/shard_map/ppermute | solution.py:557
  4.2 6.2 %collective-permute-start.1 = (f32[3,32,256]{2,1,0:T(8,128)S(1)}, f32[3,32,256]{2,1,0:T(8,128)S(1)}, u32[]{:S(2)}, u32[]{:S(2)}) collective-permute-start(f32[3,32,256]{2,1,0:T(8,128)S(1)} %get-tuple-element.31), channel_id=1, source_target_pairs={{0,24},{8,16},{16,8},{24,0},{1,25},{9,17},{17,9},{25,1},{2,26},{10... | collective-permute-start | bytes 294920 | tf_op jit(solution)/shard_map/ppermute | solution.py:556
  10.5 1.4 %collective-permute-start.2 = (f32[208,128]{1,0:T(8,128)S(1)}, f32[208,128]{1,0:T(8,128)S(1)}, u32[]{:S(2)}, u32[]{:S(2)}) collective-permute-start(f32[208,128]{1,0:T(8,128)S(1)} %get-tuple-element.42), channel_id=1, source_target_pairs={{0,1},{1,0},{2,3},{3,2},{4,5},{5,4},{6,7},{7,6},{8,9},{9,8},{10,11... | collective-permute-start | bytes 319496 | tf_op jit(solution)/shard_map/ppermute | solution.py:541
  11.9 5.1 %collective-permute-start.3 = (f32[208,128]{1,0:T(8,128)S(1)}, f32[208,128]{1,0:T(8,128)S(1)}, u32[]{:S(2)}, u32[]{:S(2)}) collective-permute-start(f32[208,128]{1,0:T(8,128)S(1)} %get-tuple-element.43.after_ref.mine_ref), channel_id=1, source_target_pairs={{0,2},{1,3},{2,0},{3,1},{4,6},{5,7},{6,4},{7,5},{8,10},{9,11},{10,... | collective-permute-start | bytes 319496 | tf_op jit(solution)/shard_map/ppermute | solution.py:541
  17.1 5.1 %collective-permute-start.4 = (f32[100,128]{1,0:T(8,128)S(1)}, f32[100,128]{1,0:T(8,128)S(1)}, u32[]{:S(2)}, u32[]{:S(2)}) collective-permute-start(f32[100,128]{1,0:T(8,128)S(1)} %get-tuple-element.48.refs_0_), channel_id=1, source_target_pairs={{0,4},{1,5},{2,6},{3,7},{4,0},{5,1},{6,2},{7,3},{8,12},{9,13},{10,... | collective-permute-start | bytes 153608 | tf_op jit(solution)/shard_map/ppermute | solution.py:541
  22.3 1.4 %collective-permute-start.5 = (f32[192,128]{1,0:T(8,128)S(1)}, f32[192,128]{1,0:T(8,128)S(1)}, u32[]{:S(2)}, u32[]{:S(2)}) collective-permute-start(f32[192,128]{1,0:T(8,128)S(1)} %get-tuple-element.52), channel_id=1, source_target_pairs={{0,1},{1,0},{2,3},{3,2},{4,5},{5,4},{6,7},{7,6},{8,9},{9,8},{10,11... | collective-permute-start | bytes 294920 | tf_op jit(solution)/shard_map/ppermute | solution.py:541

commit v6 on v5

--- a/solution.py
+++ b/solution.py
@@ -54,6 +54,7 @@
         copy = pltpu.make_async_copy(fields_ref.at[:, :, pl.ds(line, 1), :], stage_ref.at[e], sems.at[e])
         copy.start()
         copies.append(copy)
+    for e, line in enumerate((0, lines - 1)):
         copy = pltpu.make_async_copy(diff_ref.at[:, pl.ds(line, 1), :], diff_stage_ref.at[e], sems.at[5 + e])
         copy.start()
         copies.append(copy)
@@ -62,7 +63,7 @@
         copy = pltpu.make_async_copy(source, target, sems.at[2 + n])
         copy.start()
         copies.append(copy)
-    for copy in copies:
+    for copy in copies[:2]:
         copy.wait()
     for i in range(parts):
         for c in range(levels // SUB):
@@ -70,6 +71,8 @@
             first, last = [gather_rows(lambda k: stage_ref[e, i, k, 0:1, :], c, ny) for e in range(2)]
             side_ref[i, at, :] = jnp.where(even, last, first)
             far_ref[i, at, :] = jnp.where(even, first, last)
+    for copy in copies[2:]:
+        copy.wait()
 
 
 def gather_rows(row_at, c, ny):

time: 25.2 us -> 25.2 us (level)
  no operation moved by 1% of the time
where the time goes in v6:
time: 25.2 us; the launch traced here: 25 us
  Pallas kernels  10.1 us (40%)
  starting transfers between devices  8.96 us (36%)
  waiting for transfers between devices  5.82 us (23%)
    pallas_call x7, Pallas kernels, call(): pl.pallas_call(kernel, out_shape=[VMEM(s, d) for s, d in outs], in_specs=...  7.45 us
    ppermute x4, waiting for transfers between devices, swap(): return lax.ppermute(x, 'depth', [(i, i ^ 1 << bit) for i in range(ranks)])  5.06 us
    ppermute x4, starting transfers between devices, swap(): return lax.ppermute(x, 'depth', [(i, i ^ 1 << bit) for i in range(ranks)])  4.44 us
    ppermute x1, starting transfers between devices, body(): lax.ppermute(to_side, 'horiz', [(i, (i + 1 - 2 * (i % 2)) % around) for i...  3.03 us
    pallas_call x2, Pallas kernels, finish(): pl.pallas_call(functools.partial(finish_kernel, step, own), out_shape=plt...  2.68 us
    ppermute x1, starting transfers between devices, body(): lax.ppermute(to_far, 'horiz', [(i, (i + 2 * (i % 2) - 1) % around) for i...  1.49 us
    ppermute x1, waiting for transfers between devices, body(): lax.ppermute(to_far, 'horiz', [(i, (i + 2 * (i % 2) - 1) % around) for i...  0.76 us
  transfers between devices with their start and end apart: 6, of which 4 were waited for; matrix products, arithmetic and copies ran while one was open for 0% of the time, Pallas kernels for 30%

profile of v6, /device:TPU:0, one launch (start us, length us, event | category | flops | bytes accessed | tf_op | source)
XLA Modules:
  0.0 25.0 jit_solution(3621966110632697627)
XLA Ops:
  0.0 1.1 %shard_map.55 = (f32[3,32,256]{2,1,0:T(8,128)S(1)}, f32[3,32,256]{2,1,0:T(8,128)S(1)}, f32[2,32,1,256]{3,2,1,0:T(1,128)S(1)}, s32[1,32]{1,0:T(1,128)S(1)}, f32[4...) custom-call(f32[3,32,32,256]{3,2,1,0:T(8,128)} %fields_hbm.1, f32[32,32,256]{2,1,0:T(8,128)} %diff_hbm.1, s32[1,32]{1,0:T(1,128)} %bitcast.1, ...), custom_call_target="tpu_custom_call" | custom-call | tf_op jit(solution)/shard_map/pallas_call | solution.py:498
  1.1 3.0 %collective-permute-start = (f32[3,32,256]{2,1,0:T(8,128)S(1)}, f32[3,32,256]{2,1,0:T(8,128)S(1)}, u32[]{:S(2)}, u32[]{:S(2)}) collective-permute-start(f32[3,32,256]{2,1,0:T(8,128)S(1)} %get-tuple-element.30), channel_id=1, source_target_pairs={{0,8},{8,0},{16,24},{24,16},{1,9},{9,1},{17,25},{25,17},{2,10},{10... | collective-permute-start | bytes 294920 | tf_op jit(solution)/shard_map/ppermute | solution.py:560
  4.1 1.5 %collective-permute-start.1 = (f32[3,32,256]{2,1,0:T(8,128)S(1)}, f32[3,32,256]{2,1,0:T(8,128)S(1)}, u32[]{:S(2)}, u32[]{:S(2)}) collective-permute-start(f32[3,32,256]{2,1,0:T(8,128)S(1)} %get-tuple-element.31), channel_id=1, source_target_pairs={{0,24},{8,16},{16,8},{24,0},{1,25},{9,17},{17,9},{25,1},{2,26},{10... | collective-permute-start | bytes 294920 | tf_op jit(solution)/shard_map/ppermute | solution.py:559
  5.6 3.9 %shard_map.56 = (s32[32,128]{1,0:T(8,128)S(1)}, f32[2,4,32,128]{3,2,1,0:T(8,128)S(1)}, f32[2,4,32,128]{3,2,1,0:T(8,128)S(1)}, f32[24,128]{1,0:T(8,128)S(1)}, f32...) custom-call(f32[3,32,32,256]{3,2,1,0:T(8,128)} %fields_hbm.1, ...), custom_call_target="tpu_custom_call" | custom-call | tf_op jit(solution)/shard_map/pallas_call | solution.py:498
  9.6 0.0 collective-permute-done.side_ref
  9.6 0.8 %collective-permute-done.1.far_ref = f32[3,32,256]{2,1,0:T(8,128)S(1)} collective-permute-done((f32[3,32,256]{2,1,0:T(8,128)S(1)}, f32[3,32,256]{2,1,0:T(8,128)S(1)}, u32[]{:S(2)}, u32[]{:S(2)}) %collective-permute-start.1) | collective-permute-done | bytes 98336 | tf_op jit(solution)/shard_map/ppermute | solution.py:559
  10.3 0.1 shard_map.57
  10.5 0.1 collective-permute-start.2
  10.6 1.3 %collective-permute-done.2.got_ref = f32[208,128]{1,0:T(8,128)S(1)} collective-permute-done((f32[208,128]{1,0:T(8,128)S(1)}, f32[208,128]{1,0:T(8,128)S(1)}, u32[]{:S(2)}, u32[]{:S(2)}) %collective-permute-start.2) | collective-permute-done | bytes 106528 | tf_op jit(solution)/shard_map/ppermute | solution.py:544
  11.9 1.6 %collective-permute-start.3 = (f32[208,128]{1,0:T(8,128)S(1)}, f32[208,128]{1,0:T(8,128)S(1)}, u32[]{:S(2)}, u32[]{:S(2)}) collective-permute-start(f32[208,128]{1,0:T(8,128)S(1)} %get-tuple-element.43.after_ref.mine_ref), channel_id=1, source_target_pairs={{0,2},{1,3},{2,0},{3,1},{4,6},{5,7},{6,4},{7,5},{8,10},{9,11},{10,... | collective-permute-start | bytes 319496 | tf_op jit(solution)/shard_map/ppermute | solution.py:544
  13.5 2.1 %shard_map.59 = (f32[4,3,256,256]{3,2,1,0:T(8,128)S(1)}, f32[8,128]{1,0:T(8,128)S(1)}) custom-call(f32[208,128]{1,0:T(8,128)S(1)} %get-tuple-element.43.after_ref.mine_ref, f32[4,3,256,256]{3,2,1,0:T(8,128)S(1)} %get-tuple-element.44.forcing_ref, f32[2,3,32,256]{3,2,1,0:T(8,128)S(1)} %get-tuple-element.45.extra_ref, ...), custom_call_target="tpu_custom_call" | custom-call | tf_op jit(solution)/shard_map/pallas_call | solution.py:498
  15.7 1.3 %collective-permute-done.3.got_ref = f32[208,128]{1,0:T(8,128)S(1)} collective-permute-done((f32[208,128]{1,0:T(8,128)S(1)}, f32[208,128]{1,0:T(8,128)S(1)}, u32[]{:S(2)}, u32[]{:S(2)}) %collective-permute-start.3) | collective-permute-done | bytes 106528 | tf_op jit(solution)/shard_map/ppermute | solution.py:544
  17.0 0.1 shard_map.60
  17.1 2.7 %collective-permute-start.4 = (f32[100,128]{1,0:T(8,128)S(1)}, f32[100,128]{1,0:T(8,128)S(1)}, u32[]{:S(2)}, u32[]{:S(2)}) collective-permute-start(f32[100,128]{1,0:T(8,128)S(1)} %get-tuple-element.48.refs_0_), channel_id=1, source_target_pairs={{0,4},{1,5},{2,6},{3,7},{4,0},{5,1},{6,2},{7,3},{8,12},{9,13},{10,... | collective-permute-start | bytes 153608 | tf_op jit(solution)/shard_map/ppermute | solution.py:544
  19.7 2.4 %collective-permute-done.4.refs_1_ = f32[100,128]{1,0:T(8,128)S(1)} collective-permute-done((f32[100,128]{1,0:T(8,128)S(1)}, f32[100,128]{1,0:T(8,128)S(1)}, u32[]{:S(2)}, u32[]{:S(2)}) %collective-permute-start.4) | collective-permute-done | bytes 51232 | tf_op jit(solution)/shard_map/ppermute | solution.py:544
  22.2 0.1 shard_map.61
  22.2 0.1 collective-permute-start.5
  22.3 1.3 %shard_map.62.refs_0_ = f32[3,32,32,256]{3,2,1,0:T(8,128)} custom-call(f32[4,3,256,256]{3,2,1,0:T(8,128)S(1)} %get-tuple-element.46.solved_ref, f32[192,128]{1,0:T(8,128)S(1)} %get-tuple-element.54.ends_ref, s32[32,128]{1,0:T(8,128)S(1)} %get-tuple-element.38.offsb_ref.refs_3_, f32[2,4,32,128]{3,2,1,0:T(8,128)S(1)} %get-tuple-element.53.spikes_ref), custom_call_target="tpu_custom_call" | custom-call | tf_op jit(solution)/shard_map/pallas_call | solution.py:518
  23.6 0.0 collective-permute-done.5.ends_ref
  23.7 1.3 %shard_map.63 = f32[3,32,32,256]{3,2,1,0:T(8,128)} custom-call(f32[4,3,256,256]{3,2,1,0:T(8,128)S(1)} %get-tuple-element.46.solved_ref, f32[192,128]{1,0:T(8,128)S(1)} %collective-permute-done.5.ends_ref, s32[32,128]{1,0:T(8,128)S(1)} %get-tuple-element.38.offsb_ref.refs_3_, ...), custom_call_target="tpu_custom_call", output_to_operand_aliasing={{}: (4, {})} | custom-call | tf_op jit(solution)/shard_map/pallas_call | solution.py:518
  (1 shorter events, 0.0 us)
Async XLA Ops:
  1.1 8.5 %collective-permute-start = (f32[3,32,256]{2,1,0:T(8,128)S(1)}, f32[3,32,256]{2,1,0:T(8,128)S(1)}, u32[]{:S(2)}, u32[]{:S(2)}) collective-permute-start(f32[3,32,256]{2,1,0:T(8,128)S(1)} %get-tuple-element.30), channel_id=1, source_target_pairs={{0,8},{8,0},{16,24},{24,16},{1,9},{9,1},{17,25},{25,17},{2,10},{10... | collective-permute-start | bytes 294920 | tf_op jit(solution)/shard_map/ppermute | solution.py:560
  4.1 6.2 %collective-permute-start.1 = (f32[3,32,256]{2,1,0:T(8,128)S(1)}, f32[3,32,256]{2,1,0:T(8,128)S(1)}, u32[]{:S(2)}, u32[]{:S(2)}) collective-permute-start(f32[3,32,256]{2,1,0:T(8,128)S(1)} %get-tuple-element.31), channel_id=1, source_target_pairs={{0,24},{8,16},{16,8},{24,0},{1,25},{9,17},{17,9},{25,1},{2,26},{10... | collective-permute-start | bytes 294920 | tf_op jit(solution)/shard_map/ppermute | solution.py:559
  10.5 1.4 %collective-permute-start.2 = (f32[208,128]{1,0:T(8,128)S(1)}, f32[208,128]{1,0:T(8,128)S(1)}, u32[]{:S(2)}, u32[]{:S(2)}) collective-permute-start(f32[208,128]{1,0:T(8,128)S(1)} %get-tuple-element.42), channel_id=1, source_target_pairs={{0,1},{1,0},{2,3},{3,2},{4,5},{5,4},{6,7},{7,6},{8,9},{9,8},{10,11... | collective-permute-start | bytes 319496 | tf_op jit(solution)/shard_map/ppermute | solution.py:544
  11.9 5.1 %collective-permute-start.3 = (f32[208,128]{1,0:T(8,128)S(1)}, f32[208,128]{1,0:T(8,128)S(1)}, u32[]{:S(2)}, u32[]{:S(2)}) collective-permute-start(f32[208,128]{1,0:T(8,128)S(1)} %get-tuple-element.43.after_ref.mine_ref), channel_id=1, source_target_pairs={{0,2},{1,3},{2,0},{3,1},{4,6},{5,7},{6,4},{7,5},{8,10},{9,11},{10,... | collective-permute-start | bytes 319496 | tf_op jit(solution)/shard_map/ppermute | solution.py:544
  17.1 5.1 %collective-permute-start.4 = (f32[100,128]{1,0:T(8,128)S(1)}, f32[100,128]{1,0:T(8,128)S(1)}, u32[]{:S(2)}, u32[]{:S(2)}) collective-permute-start(f32[100,128]{1,0:T(8,128)S(1)} %get-tuple-element.48.refs_0_), channel_id=1, source_target_pairs={{0,4},{1,5},{2,6},{3,7},{4,0},{5,1},{6,2},{7,3},{8,12},{9,13},{10,... | collective-permute-start | bytes 153608 | tf_op jit(solution)/shard_map/ppermute | solution.py:544
  22.2 1.4 %collective-permute-start.5 = (f32[192,128]{1,0:T(8,128)S(1)}, f32[192,128]{1,0:T(8,128)S(1)}, u32[]{:S(2)}, u32[]{:S(2)}) collective-permute-start(f32[192,128]{1,0:T(8,128)S(1)} %get-tuple-element.52), channel_id=1, source_target_pairs={{0,1},{1,0},{2,3},{3,2},{4,5},{5,4},{6,7},{7,6},{8,9},{9,8},{10,11... | collective-permute-start | bytes 294920 | tf_op jit(solution)/shard_map/ppermute | solution.py:544
